TPU v7x, 32 devices: a whole 2x2x4 slice. The times are simulated.
32 devices in a mesh: tm: 4 (over y, x), tile: 8 (over z, core).
Axes of the slice: x: 2, y: 2, z: 4, core: 2. Of those that a mesh axis runs over, the one named last changes fastest.
Arguments:
- frames: bfloat16 [16, 32, 128, 256], P('tm', 'tile'), may hold values from -20 to 20
- first_gain: float32 [256], replicated, may hold values from 0.1 to 1.9
- first_bias: float32 [256], replicated, may hold values from -3 to 3
- first_weight: bfloat16 [3, 3, 3, 256, 256], replicated, may hold values from -0.078125 to 0.078125
- second_gain: float32 [256], replicated, may hold values from 0.1 to 1.9
- second_bias: float32 [256], replicated, may hold values from -3 to 3
- second_weight: bfloat16 [3, 3, 3, 256, 256], replicated, may hold values from -0.1875 to 0.1875
- latent_weight: bfloat16 [256, 16], replicated, may hold values from -0.375 to 0.375
Outputs:
- features: bfloat16 [16, 32, 128, 256], P('tm', 'tile')
- tokens: bfloat16 [16, 16, 4096], P('tm', None, 'tile')
All inputs are finite; a program needn't handle non-finite values.
Results may differ from a plain program's by a relative error of at most 0.012.
Values may be sent and summed in bfloat16 or wider, within the bound.
No kernel may reach another device: no remote copies, remote signals or barrier semaphores. Data moves between devices by JAX's collectives and lax.ppermute only.
A program may use at most 128 MiB of HBM per device.

v0:
```python
import functools

import jax
import jax.numpy as jnp
from jax import lax
from jax.experimental import pallas as pl
from jax.experimental.pallas import tpu as pltpu
from jax.sharding import PartitionSpec as P


GROUPS = 32
ALL = ("tm", "tile")
VMEM = pl.BlockSpec(memory_space=pltpu.VMEM)
HBM = pl.BlockSpec(memory_space=pltpu.HBM)
LANES = 128


def params(mib):
    return pltpu.CompilerParams(vmem_limit_bytes=mib << 20)


def row_totals(value):
    folded = value.reshape(-1, 8, value.shape[-1])
    return jnp.sum(folded, axis=0)


def put_stats(out_ref, sums, squares):
    pair = jnp.concatenate(
        [jnp.sum(sums, axis=0, keepdims=True), jnp.sum(squares, axis=0, keepdims=True)], axis=0
    )
    out_ref[...] = jnp.broadcast_to(pair[None], out_ref.shape)


def stats_kernel(frames_ref, out_ref, head_ref, last_ref):
    depth, height, _, channels = frames_ref.shape

    def step(t, carry):
        sums, squares = carry
        for h in range(height):
            value = frames_ref[t, h].astype(jnp.float32)
            sums = sums + row_totals(value)
            squares = squares + row_totals(value * value)
        return sums, squares

    zero = jnp.zeros((8, channels), jnp.float32)
    sums, squares = lax.fori_loop(0, depth, step, (zero, zero))
    put_stats(out_ref, sums, squares)
    head_ref[...] = frames_ref[: depth - 2]
    last_ref[...] = frames_ref[depth - 2 :]


def pick_kernel(past_ref, *refs):
    *own_refs, near_ref, far_ref = refs
    height = past_ref.shape[1]
    even = lax.axis_index("tile") % 2 == 0
    near = jnp.where(even, height - 1, 0)
    far = jnp.where(even, 0, height - 1)
    t = 0
    for ref in (past_ref, *own_refs):
        for frame in range(ref.shape[0]):
            near_ref[t] = ref[frame, near]
            far_ref[t] = ref[frame, far]
            t += 1


def group_sum(value, size):
    channels = value.shape[1]
    lane = lax.broadcasted_iota(jnp.int32, value.shape, 1)
    step = 1
    while step < size:
        ahead = pltpu.roll(value, channels - step, 1)
        behind = pltpu.roll(value, step, 1)
        value = value + jnp.where((lane // step) % 2 == 0, ahead, behind)
        step *= 2
    return value


def scale_of(stats_ref, gain_ref, bias_ref, members):
    channels = stats_ref.shape[2]
    totals = jnp.sum(stats_ref[...], axis=0)
    totals = jnp.concatenate([totals, jnp.zeros((6, channels), jnp.float32)], axis=0)
    totals = group_sum(totals, channels // GROUPS)
    average = totals[0:1] / members
    spread = totals[1:2] / members - average * average
    factor = lax.rsqrt(spread + 1e-06) * gain_ref[...]
    return factor, bias_ref[...] - average * factor


def silu(value):
    return value * (0.5 * jnp.tanh(0.5 * value) + 0.5)


def fill(active_ref, begin, past_ref, own_refs, near_ref, far_ref, scale):
    factor, offset = scale
    height = past_ref.shape[1]
    index, count = lax.axis_index("tile"), lax.axis_size("tile")
    even = index % 2 == 0
    first = (lax.axis_index("tm") > 0).astype(jnp.float32)
    near_row, far_row = jnp.where(even, height + 1, 0), jnp.where(even, 0, height + 1)
    above, below = index > 0, index < count - 1
    near_keep = jnp.where(even, below, above).astype(jnp.float32)
    far_keep = jnp.where(even, above, below).astype(jnp.float32)

    def put(t, h, value, keep):
        active = silu(value.astype(jnp.float32) * factor + offset)
        if keep is not None:
            active = active * keep
        active_ref[t, h] = active.astype(jnp.bfloat16)

    frame = 0
    for ref in (past_ref, *own_refs):
        skip = max(0, begin - frame)

        def one(t, carry, ref=ref, frame=frame):
            keep = first if ref is past_ref else None
            place = frame + t - begin
            for h in range(height):
                put(place, h + 1, ref[t, h], keep)
            put(place, near_row, near_ref[frame + t], near_keep if keep is None else near_keep * keep)
            put(place, far_row, far_ref[frame + t], far_keep if keep is None else far_keep * keep)
            return carry

        stop = min(ref.shape[0], active_ref.shape[0] + begin - frame)
        if stop > skip:
            lax.fori_loop(skip, stop, one, 0)
        frame += ref.shape[0]


def weight_copies(weight_hbm, weight_ref, sem):
    return [
        pltpu.make_async_copy(weight_hbm.at[:, :, c], weight_ref.at[c], sem.at[c]) for c in range(3)
    ]


def convolve(active_ref, weight_ref, t, height, copies):
    columns, channels = active_ref.shape[2:]
    rows = height * columns
    totals = []
    for c in range(3):
        pl.when(t == 0)(copies[c].wait)
        total = None
        for a in range(3):
            for b in range(3):
                piece = active_ref[t + a, b : b + height].reshape(rows, channels)
                part = jnp.dot(piece, weight_ref[c, a, b], preferred_element_type=jnp.float32)
                total = part if total is None else total + part
        totals.append(total)
    column = lax.broadcasted_iota(jnp.int32, totals[0].shape, 0) % columns
    left = jnp.where(column == 0, 0.0, pltpu.roll(totals[0], 1, 0))
    right = jnp.where(column == columns - 1, 0.0, pltpu.roll(totals[2], rows - 1, 0))
    return totals[1] + left + right


def first_kernel(members, begin, owns, more, past, *refs):
    own, refs = refs[:owns], refs[owns:]
    near, far, stats, gain, bias, weight = refs[:6]
    hidden_ref, totals_ref, active_ref, weight_ref, sem = refs[-5:]
    depth, height, columns, channels = hidden_ref.shape
    copies = weight_copies(weight, weight_ref, sem)
    for copy in copies:
        copy.start()
    fill(active_ref, begin, past, own, near, far, scale_of(stats, gain, bias, members))

    def step(t, carry):
        sums, squares = carry
        hidden = convolve(active_ref, weight_ref, t, height, copies).astype(jnp.bfloat16)
        hidden_ref[t] = hidden.reshape(height, columns, channels)
        wide = hidden.astype(jnp.float32)
        return sums + row_totals(wide), squares + row_totals(wide * wide)

    zero = jnp.zeros((8, channels), jnp.float32)
    start = (refs[6][0], refs[6][1]) if more else (zero, zero)
    sums, squares = lax.fori_loop(0, depth, step, start)
    if more:
        put_stats(totals_ref, sums, squares)
    else:
        totals_ref[0] = sums
        totals_ref[1] = squares


def second_kernel(members, owns, past, *refs):
    own, refs = refs[:owns], refs[owns:]
    near, far, stats, gain, bias, weight, frames, latent = refs[:8]
    features_hbm, patches_ref, active_ref, latents_ref, packed_ref = refs[8:13]
    weight_ref, cells_ref, sem, in_sem, out_sem = refs[13:]
    depth, height, columns, channels = frames.shape
    copies = weight_copies(weight, weight_ref, sem)
    for copy in copies:
        copy.start()
    loads = pltpu.make_async_copy(frames, cells_ref, in_sem)
    loads.start()
    width = LANES // 8
    fill(active_ref, 0, past, own, near, far, scale_of(stats, gain, bias, members))
    parts, rows = packed_ref.shape[:2]
    pairs = height // 2
    blocks = rows // (depth * pairs)
    lane = lax.broadcasted_iota(jnp.int32, (columns // 4, LANES), 1) // width
    spread = lax.broadcasted_iota(jnp.int32, (width, LANES), 0) == (
        lax.broadcasted_iota(jnp.int32, (width, LANES), 1) % width
    )
    wide_latent = lax.dot_general(
        latent[...], spread.astype(jnp.bfloat16), (((0,), (0,)), ((), ())),
        preferred_element_type=jnp.float32,
    ).astype(jnp.bfloat16)

    def step(t, carry):
        branch = convolve(active_ref, weight_ref, t, height, copies)
        pl.when(t == 0)(loads.wait)
        residual = cells_ref[t].reshape(height * columns, channels).astype(jnp.float32)
        features = (residual + branch).astype(jnp.bfloat16)
        cells_ref[t] = features.reshape(height, columns, channels)
        pltpu.make_async_copy(cells_ref.at[t], features_hbm.at[t], out_sem.at[t]).start()
        latents_ref[...] = (
            jnp.dot(features, wide_latent, preferred_element_type=jnp.float32)
            .astype(jnp.bfloat16)
            .astype(jnp.float32)
        )
        for i in range(pairs):
            mixed = None
            for cell in range(8):
                j, p, q = cell // 4, cell // 2 % 2, cell % 2
                start = (2 * i + p) * columns + 2 * j + q
                value = latents_ref[pl.ds(start, columns // 4, stride=4), :]
                mixed = value if mixed is None else jnp.where(lane == cell, value, mixed)
            for d in range(parts):
                packed_ref[d, pl.ds(t * blocks * pairs + i, blocks, stride=pairs), :] = mixed[
                    d * blocks : (d + 1) * blocks
                ]
        return carry

    lax.fori_loop(0, depth, step, 0)
    patches_ref[...] = packed_ref[...].astype(jnp.bfloat16)
    for t in range(depth):
        pltpu.make_async_copy(cells_ref.at[t], features_hbm.at[t], out_sem.at[t]).wait()


def unpack_kernel(blocks, pairs, received, tokens_ref, flat_ref, mixed_ref):
    parts, rows, lanes = received.shape
    flat_ref[...] = received[...].astype(jnp.float32).reshape(parts * rows, lanes)
    depth = rows // (blocks * pairs)
    for t in range(depth):
        for block in range(blocks):
            for i in range(pairs):
                start = (t * blocks + block) * pairs + i
                mixed_ref[t * blocks + block, pl.ds(i, parts, stride=pairs), :] = flat_ref[
                    pl.ds(start, parts, stride=rows), :
                ]
            tokens_ref[t, :, block * lanes : (block + 1) * lanes] = mixed_ref[
                t * blocks + block
            ].astype(jnp.bfloat16)


def ahead_pairs():
    return [(i, i + 1) for i in range(lax.axis_size("tm") - 1)]


def surround(last, own):
    past = lax.ppermute(last, "tm", ahead_pairs())
    _, columns, channels = last.shape[1:]
    count = lax.axis_size("tile")
    near_pairs = [(i, i ^ 1) for i in range(count) if i ^ 1 < count]
    far_pairs = [pair for i in range(1, count - 1, 2) for pair in ((i, i + 1), (i + 1, i))]
    rows = jax.ShapeDtypeStruct(
        (2 + sum(piece.shape[0] for piece in own), columns, channels), jnp.bfloat16
    )
    near, far = pl.pallas_call(
        pick_kernel, out_shape=(rows, rows), in_specs=[VMEM] * (1 + len(own)),
        out_specs=(VMEM, VMEM), compiler_params=params(8), name="pick",
    )(past, *own)
    near = lax.ppermute(near, "tile", near_pairs)
    far = lax.ppermute(far, "tile", far_pairs)
    return past, *own, near, far


def exchange(stats):
    return lax.all_to_all(stats, ALL, split_axis=0, concat_axis=0, tiled=True)


def body(frames, first_gain, first_bias, first_weight, second_gain, second_bias, second_weight,
         latent_weight):
    depth, height, columns, channels = frames.shape
    parts = lax.axis_size("tile")
    devices = lax.axis_size("tm") * parts
    members = float(devices * depth * height * columns * (channels // GROUPS))
    latent_width = latent_weight.shape[1]
    pairs = height // 2
    blocks = columns // 2 * 4 * latent_width // parts // LANES
    rows = depth * blocks * pairs
    stats_shape = jax.ShapeDtypeStruct((devices, 2, channels), jnp.float32)
    cells_shape = jax.ShapeDtypeStruct(frames.shape, jnp.bfloat16)
    last_shape = jax.ShapeDtypeStruct((2, *frames.shape[1:]), jnp.bfloat16)
    head_shape = jax.ShapeDtypeStruct((depth - 2, *frames.shape[1:]), jnp.bfloat16)

    weights = [pltpu.VMEM((3, 3, 3, channels, channels), jnp.bfloat16), pltpu.SemaphoreType.DMA((3,))]

    def active(count):
        return [pltpu.VMEM((count + 2, height + 2, columns, channels), jnp.bfloat16), *weights]

    def cost(count):
        flops = 2 * 27 * count * height * columns * channels * channels
        return pl.CostEstimate(flops=flops, bytes_accessed=8 << 20, transcendentals=0)

    first_weight = pltpu.with_memory_space_constraint(first_weight, pltpu.HBM)
    second_weight = pltpu.with_memory_space_constraint(second_weight, pltpu.HBM)
    cells = pltpu.with_memory_space_constraint(frames, pltpu.HBM)
    stats, head, last = pl.pallas_call(
        stats_kernel, out_shape=(stats_shape, head_shape, last_shape), in_specs=[VMEM],
        out_specs=(VMEM, VMEM, VMEM), compiler_params=params(8), cost_estimate=cost(1), name="stats",
    )(frames)
    around = surround(last, (head, last))
    stats = exchange(stats)
    operands = (*around, stats, first_gain[None], first_bias[None], first_weight)
    last, totals = pl.pallas_call(
        functools.partial(first_kernel, members, depth - 2, 2, False),
        out_shape=(last_shape, jax.ShapeDtypeStruct((2, 8, channels), jnp.float32)),
        in_specs=[VMEM] * 8 + [HBM], out_specs=(VMEM, VMEM), scratch_shapes=active(2),
        compiler_params=params(24), cost_estimate=cost(2), name="first_last",
    )(*operands)
    head, stats = pl.pallas_call(
        functools.partial(first_kernel, members, 0, 2, True),
        out_shape=(head_shape, stats_shape),
        in_specs=[VMEM] * 8 + [HBM, VMEM], out_specs=(VMEM, VMEM), scratch_shapes=active(depth - 2),
        compiler_params=params(24), cost_estimate=cost(depth - 2), name="first_head",
    )(*operands, totals)
    around = surround(last, (head, last))
    stats = exchange(stats)
    features, patches = pl.pallas_call(
        functools.partial(second_kernel, members, 2),
        out_shape=(cells_shape, jax.ShapeDtypeStruct((parts, rows, LANES), jnp.bfloat16)),
        in_specs=[VMEM] * 8 + [HBM, HBM, VMEM], out_specs=(HBM, VMEM),
        scratch_shapes=[active(depth)[0], pltpu.VMEM((height * columns, LANES), jnp.float32),
                        pltpu.VMEM((parts, rows, LANES), jnp.float32), weights[0],
                        pltpu.VMEM(frames.shape, jnp.bfloat16), weights[1],
                        pltpu.SemaphoreType.DMA(()), pltpu.SemaphoreType.DMA((depth,))],
        compiler_params=params(24), cost_estimate=cost(depth), name="second",
    )(*around, stats, second_gain[None], second_bias[None], second_weight, cells, latent_weight.T)
    received = lax.all_to_all(patches, "tile", split_axis=0, concat_axis=0, tiled=True)
    tokens = pl.pallas_call(
        functools.partial(unpack_kernel, blocks, pairs),
        out_shape=jax.ShapeDtypeStruct((depth, parts * pairs, blocks * LANES), jnp.bfloat16),
        in_specs=[VMEM], out_specs=VMEM,
        scratch_shapes=[pltpu.VMEM((parts * rows, LANES), jnp.float32),
                        pltpu.VMEM((depth * blocks, parts * pairs, LANES), jnp.float32)],
        compiler_params=params(16), name="unpack",
    )(received)
    return features, tokens


def solution(mesh):
    in_specs = (P("tm", "tile", None, None), P(), P(), P(), P(), P(), P(), P())
    out_specs = (P("tm", "tile", None, None), P("tm", None, "tile"))
    return jax.shard_map(body, mesh=mesh, in_specs=in_specs, out_specs=out_specs, check_vma=False)
```

profile of v0, /device:TPU:0, one launch (start us, length us, event | category | flops | bytes accessed | tf_op | source)
XLA Modules:
  0.0 98.9 jit_solution(12331142294169370992)
XLA Ops:
  0.6 0.0 copy-start
  0.6 1.2 %copy-done = bf16[4,4,128,256]{3,2,1,0:T(8,128)(2,1)S(1)} copy-done((bf16[4,4,128,256]{3,2,1,0:T(8,128)(2,1)S(1)}, bf16[4,4,128,256]{3,2,1,0:T(8,128)(2,1)}, u32[]{:S(2)}) %copy-start) | copy-done | bytes 1048600
  1.9 0.3 stats.1
  2.1 4.9 %collective-permute-start = (bf16[2,4,128,256]{3,2,1,0:T(8,128)(2,1)S(1)}, bf16[2,4,128,256]{3,2,1,0:T(8,128)(2,1)S(1)}, u32[]{:S(2)}, u32[]{:S(2)}) collective-permute-start(bf16[2,4,128,256]{3,2,1,0:T(8,128)(2,1)S(1)} %get-tuple-element.15.refs_1_), channel_id=1, source_target_pairs={{0,8},{8,16},{16,24},{1,9},{9,17},{17,25},{2,10},{10,18},{18,26},{... | collective-permute-start | bytes 1572872 | tf_op jit(solution)/shard_map/ppermute | solution.py:258
  7.1 11.1 %collective-permute-done.past_ref.past = bf16[2,4,128,256]{3,2,1,0:T(8,128)(2,1)S(1)} collective-permute-done((bf16[2,4,128,256]{3,2,1,0:T(8,128)(2,1)S(1)}, bf16[2,4,128,256]{3,2,1,0:T(8,128)(2,1)S(1)}, u32[]{:S(2)}, u32[]{:S(2)}) %collective-permute-start) | collective-permute-done | bytes 524320 | tf_op jit(solution)/shard_map/ppermute | solution.py:258
  18.2 0.1 pick.2
  18.2 0.1 collective-permute-start.1
  18.3 0.7 collective-permute-start.2
  19.0 15.8 %all_to_all.15.refs_4_ = f32[32,2,256]{2,1,0:T(2,128)S(1)} all-to-all(f32[32,2,256]{2,1,0:T(2,128)S(1)} %get-tuple-element.19), channel_id=1, replica_groups=mesh['tm'=4,'tile'=8] {'tm','tile'}, dimensions={0} | all-to-all | bytes 131072 | tf_op jit(solution)/shard_map/all_to_all | solution.py:276
  34.8 0.0 collective-permute-done.1.refs_2_
  34.8 0.0 collective-permute-done.2.refs_3_
  34.8 0.0 copy-done.2
  34.8 0.0 copy-done.3
  34.8 8.5 %first_last.1 = (bf16[2,4,128,256]{3,2,1,0:T(8,128)(2,1)S(1)}, f32[2,8,256]{2,1,0:T(8,128)S(1)}) custom-call(bf16[2,4,128,256]{3,2,1,0:T(8,128)(2,1)S(1)} %collective-permute-done.past_ref.past, bf16[2,4,128,256]{3,2,1,0:T(8,128)(2,1)S(1)} %get-tuple-element.16.refs_0_, bf16[2,4,128,256]{3,2,1,0:T(8,128)(2,1)S(1)} %get-tuple-element.15.refs_1_, ...), custom_call_target="tpu_custom_call" | custom-call | flops 3623878656 | bytes 8388608 | tf_op jit(solution)/shard_map/first_last/pallas_call | solution.py:313
  43.3 2.6 %collective-permute-start.3 = (bf16[2,4,128,256]{3,2,1,0:T(8,128)(2,1)S(1)}, bf16[2,4,128,256]{3,2,1,0:T(8,128)(2,1)S(1)}, u32[]{:S(2)}, u32[]{:S(2)}) collective-permute-start(bf16[2,4,128,256]{3,2,1,0:T(8,128)(2,1)S(1)} %get-tuple-element.20.refs_1_), channel_id=1, source_target_pairs={{0,8},{8,16},{16,24},{1,9},{9,17},{17,25},{2,10},{10,18},{18,26},{... | collective-permute-start | bytes 1572872 | tf_op jit(solution)/shard_map/ppermute | solution.py:258
  46.0 0.0 copy-start.1
  46.0 0.0 copy-start.4
  46.0 0.0 copy-start.5
  46.0 8.6 %first_head.1 = (bf16[2,4,128,256]{3,2,1,0:T(8,128)(2,1)S(1)}, f32[32,2,256]{2,1,0:T(2,128)S(1)}) custom-call(bf16[2,4,128,256]{3,2,1,0:T(8,128)(2,1)S(1)} %collective-permute-done.past_ref.past, bf16[2,4,128,256]{3,2,1,0:T(8,128)(2,1)S(1)} %get-tuple-element.16.refs_0_, bf16[2,4,128,256]{3,2,1,0:T(8,128)(2,1)S(1)} %get-tuple-element.15.refs_1_, ...), custom_call_target="tpu_custom_call" | custom-call | flops 3623878656 | bytes 8388608 | tf_op jit(solution)/shard_map/first_head/pallas_call | solution.py:319
  54.6 2.4 %collective-permute-done.3.past_ref.past = bf16[2,4,128,256]{3,2,1,0:T(8,128)(2,1)S(1)} collective-permute-done((bf16[2,4,128,256]{3,2,1,0:T(8,128)(2,1)S(1)}, bf16[2,4,128,256]{3,2,1,0:T(8,128)(2,1)S(1)}, u32[]{:S(2)}, u32[]{:S(2)}) %collective-permute-start.3) | collective-permute-done | bytes 524320 | tf_op jit(solution)/shard_map/ppermute | solution.py:258
  57.0 0.1 pick.3
  57.1 0.1 collective-permute-start.4
  57.2 0.7 collective-permute-start.5
  57.8 13.9 %all_to_all.16.refs_4_ = f32[32,2,256]{2,1,0:T(2,128)S(1)} all-to-all(f32[32,2,256]{2,1,0:T(2,128)S(1)} %get-tuple-element.25), channel_id=1, replica_groups=mesh['tm'=4,'tile'=8] {'tm','tile'}, dimensions={0} | all-to-all | bytes 131072 | tf_op jit(solution)/shard_map/all_to_all | solution.py:276
  71.8 0.0 collective-permute-done.4.refs_2_
  71.8 0.0 collective-permute-done.5.refs_3_
  71.8 0.0 copy-done.1
  71.8 0.0 copy-done.4
  71.8 0.0 copy-done.5
  71.8 18.0 %second.1 = (bf16[4,4,128,256]{3,2,1,0:T(8,128)(2,1)}, bf16[8,32,128]{2,1,0:T(8,128)(2,1)S(1)}) custom-call(bf16[2,4,128,256]{3,2,1,0:T(8,128)(2,1)S(1)} %collective-permute-done.3.past_ref.past, bf16[2,4,128,256]{3,2,1,0:T(8,128)(2,1)S(1)} %get-tuple-element.22.refs_0_, bf16[2,4,128,256]{3,2,1,0:T(8,128)(2,1)S(1)} %get-tuple-element.20.refs_1_, ...), custom_call_target="tpu_custom_call" | custom-call | flops 7247757312 | bytes 8388608 | tf_op jit(solution)/shard_map/second/pallas_call | solution.py:327
  89.9 8.3 %all_to_all.17.received = bf16[8,32,128]{2,1,0:T(8,128)(2,1)S(1)} all-to-all(bf16[8,32,128]{2,1,0:T(8,128)(2,1)S(1)} %get-tuple-element.27), channel_id=1, replica_groups=mesh['tm'=4,'tile'=8] {'tile'}, dimensions={0} | all-to-all | bytes 131072 | tf_op jit(solution)/shard_map/all_to_all | solution.py:337
  98.1 0.8 unpack.1
  (2 shorter events, 0.0 us)
Async XLA Ops:
  0.6 1.2 %copy-start = (bf16[4,4,128,256]{3,2,1,0:T(8,128)(2,1)S(1)}, bf16[4,4,128,256]{3,2,1,0:T(8,128)(2,1)}, u32[]{:S(2)}) copy-start(bf16[4,4,128,256]{3,2,1,0:T(8,128)(2,1)} %refs_8_.1) | copy-start | bytes 3145732
  1.9 33.0 %copy-start.2 = (f32[256]{0:T(256)S(1)}, f32[256]{0:T(256)}, u32[]{:S(2)}) copy-start(f32[256]{0:T(256)} %param.9) | copy-start | bytes 3076
  1.9 33.0 %copy-start.3 = (f32[256]{0:T(256)S(1)}, f32[256]{0:T(256)}, u32[]{:S(2)}) copy-start(f32[256]{0:T(256)} %param.10) | copy-start | bytes 3076
  2.1 16.0 %collective-permute-start = (bf16[2,4,128,256]{3,2,1,0:T(8,128)(2,1)S(1)}, bf16[2,4,128,256]{3,2,1,0:T(8,128)(2,1)S(1)}, u32[]{:S(2)}, u32[]{:S(2)}) collective-permute-start(bf16[2,4,128,256]{3,2,1,0:T(8,128)(2,1)S(1)} %get-tuple-element.15.refs_1_), channel_id=1, source_target_pairs={{0,8},{8,16},{16,24},{1,9},{9,17},{17,25},{2,10},{10,18},{18,26},{... | collective-permute-start | bytes 1572872 | tf_op jit(solution)/shard_map/ppermute | solution.py:258
  18.2 16.6 %collective-permute-start.1 = (bf16[6,128,256]{2,1,0:T(8,128)(2,1)S(1)}, bf16[6,128,256]{2,1,0:T(8,128)(2,1)S(1)}, u32[]{:S(2)}, u32[]{:S(2)}) collective-permute-start(bf16[6,128,256]{2,1,0:T(8,128)(2,1)S(1)} %get-tuple-element.17), channel_id=1, source_target_pairs={{0,1},{1,0},{2,3},{3,2},{4,5},{5,4},{6,7},{7,6},{8,9},{9,8},{10,11... | collective-permute-start | bytes 1179656 | tf_op jit(solution)/shard_map/ppermute | solution.py:270
  18.3 16.5 %collective-permute-start.2 = (bf16[6,128,256]{2,1,0:T(8,128)(2,1)S(1)}, bf16[6,128,256]{2,1,0:T(8,128)(2,1)S(1)}, u32[]{:S(2)}, u32[]{:S(2)}) collective-permute-start(bf16[6,128,256]{2,1,0:T(8,128)(2,1)S(1)} %get-tuple-element.18), channel_id=1, source_target_pairs={{1,2},{2,1},{3,4},{4,3},{5,6},{6,5},{9,10},{10,9},{11,12},{12,11},... | collective-permute-start | bytes 1179656 | tf_op jit(solution)/shard_map/ppermute | solution.py:271
  43.3 13.7 %collective-permute-start.3 = (bf16[2,4,128,256]{3,2,1,0:T(8,128)(2,1)S(1)}, bf16[2,4,128,256]{3,2,1,0:T(8,128)(2,1)S(1)}, u32[]{:S(2)}, u32[]{:S(2)}) collective-permute-start(bf16[2,4,128,256]{3,2,1,0:T(8,128)(2,1)S(1)} %get-tuple-element.20.refs_1_), channel_id=1, source_target_pairs={{0,8},{8,16},{16,24},{1,9},{9,17},{17,25},{2,10},{10,18},{18,26},{... | collective-permute-start | bytes 1572872 | tf_op jit(solution)/shard_map/ppermute | solution.py:258
  46.0 25.8 %copy-start.1 = (bf16[256,16]{0,1:T(8,128)(2,1)S(1)}, bf16[256,16]{0,1:T(8,128)(2,1)}, u32[]{:S(2)}) copy-start(bf16[256,16]{0,1:T(8,128)(2,1)} %param.15) | copy-start | bytes 24580
  46.0 25.8 %copy-start.4 = (f32[256]{0:T(256)S(1)}, f32[256]{0:T(256)}, u32[]{:S(2)}) copy-start(f32[256]{0:T(256)} %param.12) | copy-start | bytes 3076
  46.0 25.8 %copy-start.5 = (f32[256]{0:T(256)S(1)}, f32[256]{0:T(256)}, u32[]{:S(2)}) copy-start(f32[256]{0:T(256)} %param.13) | copy-start | bytes 3076
  57.1 14.7 %collective-permute-start.4 = (bf16[6,128,256]{2,1,0:T(8,128)(2,1)S(1)}, bf16[6,128,256]{2,1,0:T(8,128)(2,1)S(1)}, u32[]{:S(2)}, u32[]{:S(2)}) collective-permute-start(bf16[6,128,256]{2,1,0:T(8,128)(2,1)S(1)} %get-tuple-element.23), channel_id=1, source_target_pairs={{0,1},{1,0},{2,3},{3,2},{4,5},{5,4},{6,7},{7,6},{8,9},{9,8},{10,11... | collective-permute-start | bytes 1179656 | tf_op jit(solution)/shard_map/ppermute | solution.py:270
  57.2 14.6 %collective-permute-start.5 = (bf16[6,128,256]{2,1,0:T(8,128)(2,1)S(1)}, bf16[6,128,256]{2,1,0:T(8,128)(2,1)S(1)}, u32[]{:S(2)}, u32[]{:S(2)}) collective-permute-start(bf16[6,128,256]{2,1,0:T(8,128)(2,1)S(1)} %get-tuple-element.24), channel_id=1, source_target_pairs={{1,2},{2,1},{3,4},{4,3},{5,6},{6,5},{9,10},{10,9},{11,12},{12,11},... | collective-permute-start | bytes 1179656 | tf_op jit(solution)/shard_map/ppermute | solution.py:271
where the time goes:
time: 99.2 us; the launch traced here: 98.9 us
  blocking collectives  38 us (38%)
  Pallas kernels  36.3 us (37%)
  waiting for transfers between devices  13.6 us (14%)
  starting transfers between devices  9.03 us (9%)
  local copies, waits for them, and re-layouts  1.25 us (1%)
    all_to_all x2, blocking collectives, exchange(): return lax.all_to_all(stats, ALL, split_axis=0, concat_axis=0, tiled=True)  29.7 us
    pallas_call x1, Pallas kernels, body(): pl.pallas_call(functools.partial(second_kernel, members, 2), out_shape=(c...  18 us
    ppermute x2, waiting for transfers between devices, surround(): past = lax.ppermute(last, 'tm', ahead_pairs())  13.5 us
    pallas_call x1, Pallas kernels, body(): pl.pallas_call(functools.partial(first_kernel, members, 0, 2, True), out_...  8.6 us
    pallas_call x1, Pallas kernels, body(): pl.pallas_call(functools.partial(first_kernel, members, depth - 2, 2, Fal...  8.5 us
    all_to_all x1, blocking collectives, body(): lax.all_to_all(patches, 'tile', split_axis=0, concat_axis=0, tiled=True)  8.3 us
    ppermute x2, starting transfers between devices, surround(): past = lax.ppermute(last, 'tm', ahead_pairs())  7.52 us
  transfers between devices with their start and end apart: 6, of which 2 were waited for; matrix products, arithmetic and copies ran while one was open for 0% of the time, Pallas kernels for 9%

commit v1 on v0

--- a/solution.py
+++ b/solution.py
@@ -31,8 +31,14 @@
     out_ref[...] = jnp.broadcast_to(pair[None], out_ref.shape)
 
 
-def stats_kernel(frames_ref, out_ref, head_ref, last_ref):
+def sides(height):
+    even = lax.axis_index("tile") % 2 == 0
+    return jnp.where(even, height - 1, 0), jnp.where(even, 0, height - 1)
+
+
+def stats_kernel(frames_ref, out_ref, head_ref, last_ref, near_ref, far_ref):
     depth, height, _, channels = frames_ref.shape
+    near, far = sides(height)
 
     def step(t, carry):
         sums, squares = carry
@@ -40,6 +46,8 @@
             value = frames_ref[t, h].astype(jnp.float32)
             sums = sums + row_totals(value)
             squares = squares + row_totals(value * value)
+        near_ref[t] = frames_ref[t, near]
+        far_ref[t] = frames_ref[t, far]
         return sums, squares
 
     zero = jnp.zeros((8, channels), jnp.float32)
@@ -49,14 +57,11 @@
     last_ref[...] = frames_ref[depth - 2 :]
 
 
-def pick_kernel(past_ref, *refs):
-    *own_refs, near_ref, far_ref = refs
-    height = past_ref.shape[1]
-    even = lax.axis_index("tile") % 2 == 0
-    near = jnp.where(even, height - 1, 0)
-    far = jnp.where(even, 0, height - 1)
+def pick_kernel(count, *refs):
+    cell_refs, (near_ref, far_ref) = refs[:count], refs[-2:]
+    near, far = sides(cell_refs[0].shape[1])
     t = 0
-    for ref in (past_ref, *own_refs):
+    for ref in cell_refs:
         for frame in range(ref.shape[0]):
             near_ref[t] = ref[frame, near]
             far_ref[t] = ref[frame, far]
@@ -90,9 +95,9 @@
     return value * (0.5 * jnp.tanh(0.5 * value) + 0.5)
 
 
-def fill(active_ref, begin, past_ref, own_refs, near_ref, far_ref, scale):
+def fill(active_ref, begin, pieces, scale):
     factor, offset = scale
-    height = past_ref.shape[1]
+    height = active_ref.shape[1] - 2
     index, count = lax.axis_index("tile"), lax.axis_size("tile")
     even = index % 2 == 0
     first = (lax.axis_index("tm") > 0).astype(jnp.float32)
@@ -107,42 +112,32 @@
             active = active * keep
         active_ref[t, h] = active.astype(jnp.bfloat16)
 
-    frame = 0
-    for ref in (past_ref, *own_refs):
+    for frame, ref, near_ref, far_ref, shift, is_past in pieces:
         skip = max(0, begin - frame)
-
-        def one(t, carry, ref=ref, frame=frame):
-            keep = first if ref is past_ref else None
+        stop = min(ref.shape[0], active_ref.shape[0] + begin - frame)
+
+        def one(t, carry):
             place = frame + t - begin
             for h in range(height):
-                put(place, h + 1, ref[t, h], keep)
-            put(place, near_row, near_ref[frame + t], near_keep if keep is None else near_keep * keep)
-            put(place, far_row, far_ref[frame + t], far_keep if keep is None else far_keep * keep)
+                put(place, h + 1, ref[t, h], first if is_past else None)
+            put(place, near_row, near_ref[shift + t], near_keep * first if is_past else near_keep)
+            put(place, far_row, far_ref[shift + t], far_keep * first if is_past else far_keep)
             return carry
 
-        stop = min(ref.shape[0], active_ref.shape[0] + begin - frame)
         if stop > skip:
             lax.fori_loop(skip, stop, one, 0)
-        frame += ref.shape[0]
-
-
-def weight_copies(weight_hbm, weight_ref, sem):
-    return [
-        pltpu.make_async_copy(weight_hbm.at[:, :, c], weight_ref.at[c], sem.at[c]) for c in range(3)
-    ]
-
-
-def convolve(active_ref, weight_ref, t, height, copies):
+
+
+def convolve(active_ref, weight_ref, t, height):
     columns, channels = active_ref.shape[2:]
     rows = height * columns
     totals = []
     for c in range(3):
-        pl.when(t == 0)(copies[c].wait)
         total = None
         for a in range(3):
             for b in range(3):
                 piece = active_ref[t + a, b : b + height].reshape(rows, channels)
-                part = jnp.dot(piece, weight_ref[c, a, b], preferred_element_type=jnp.float32)
+                part = jnp.dot(piece, weight_ref[a, b, c], preferred_element_type=jnp.float32)
                 total = part if total is None else total + part
         totals.append(total)
     column = lax.broadcasted_iota(jnp.int32, totals[0].shape, 0) % columns
@@ -151,46 +146,53 @@
     return totals[1] + left + right
 
 
-def first_kernel(members, begin, owns, more, past, *refs):
-    own, refs = refs[:owns], refs[owns:]
-    near, far, stats, gain, bias, weight = refs[:6]
-    hidden_ref, totals_ref, active_ref, weight_ref, sem = refs[-5:]
+def first_kernel(members, begin, with_past, with_totals, *refs):
+    refs = list(refs)
+    pieces = []
+    if with_past:
+        past, near, far = refs[:3]
+        pieces.append((0, past, near, far, 0, True))
+        del refs[:3]
+    head, last, near, far, stats, gain, bias, weight = refs[:8]
+    before = head.shape[0]
+    pieces.append((2, head, near, far, 0, False))
+    pieces.append((2 + before, last, near, far, before, False))
+    hidden_ref, totals_ref, active_ref = refs[-3:]
     depth, height, columns, channels = hidden_ref.shape
-    copies = weight_copies(weight, weight_ref, sem)
-    for copy in copies:
-        copy.start()
-    fill(active_ref, begin, past, own, near, far, scale_of(stats, gain, bias, members))
+    fill(active_ref, begin, pieces, scale_of(stats, gain, bias, members))
 
     def step(t, carry):
         sums, squares = carry
-        hidden = convolve(active_ref, weight_ref, t, height, copies).astype(jnp.bfloat16)
+        hidden = convolve(active_ref, weight, t, height).astype(jnp.bfloat16)
         hidden_ref[t] = hidden.reshape(height, columns, channels)
         wide = hidden.astype(jnp.float32)
         return sums + row_totals(wide), squares + row_totals(wide * wide)
 
     zero = jnp.zeros((8, channels), jnp.float32)
-    start = (refs[6][0], refs[6][1]) if more else (zero, zero)
+    start = (refs[8][0], refs[8][1]) if with_totals else (zero, zero)
     sums, squares = lax.fori_loop(0, depth, step, start)
-    if more:
+    if with_totals:
         put_stats(totals_ref, sums, squares)
     else:
         totals_ref[0] = sums
         totals_ref[1] = squares
 
 
-def second_kernel(members, owns, past, *refs):
-    own, refs = refs[:owns], refs[owns:]
-    near, far, stats, gain, bias, weight, frames, latent = refs[:8]
-    features_hbm, patches_ref, active_ref, latents_ref, packed_ref = refs[8:13]
-    weight_ref, cells_ref, sem, in_sem, out_sem = refs[13:]
+def second_kernel(members, past, head, last, near, far, stats, gain, bias, weight, frames, latent,
+                  features_hbm, patches_ref, active_ref, latents_ref, packed_ref, cells_ref,
+                  in_sem, out_sem):
     depth, height, columns, channels = frames.shape
-    copies = weight_copies(weight, weight_ref, sem)
-    for copy in copies:
-        copy.start()
+    before = head.shape[0]
     loads = pltpu.make_async_copy(frames, cells_ref, in_sem)
     loads.start()
     width = LANES // 8
-    fill(active_ref, 0, past, own, near, far, scale_of(stats, gain, bias, members))
+    pieces = [
+        (0, past, near, far, 0, True),
+        (2, head, near, far, 2, False),
+        (2 + before, last, near, far, 2 + before, False),
+    ]
+    fill(active_ref, 0, pieces, scale_of(stats, gain, bias, members))
+    loads.wait()
     parts, rows = packed_ref.shape[:2]
     pairs = height // 2
     blocks = rows // (depth * pairs)
@@ -204,8 +206,7 @@
     ).astype(jnp.bfloat16)
 
     def step(t, carry):
-        branch = convolve(active_ref, weight_ref, t, height, copies)
-        pl.when(t == 0)(loads.wait)
+        branch = convolve(active_ref, weight, t, height)
         residual = cells_ref[t].reshape(height * columns, channels).astype(jnp.float32)
         features = (residual + branch).astype(jnp.bfloat16)
         cells_ref[t] = features.reshape(height, columns, channels)
@@ -250,26 +251,28 @@
             ].astype(jnp.bfloat16)
 
 
-def ahead_pairs():
-    return [(i, i + 1) for i in range(lax.axis_size("tm") - 1)]
-
-
-def surround(last, own):
-    past = lax.ppermute(last, "tm", ahead_pairs())
-    _, columns, channels = last.shape[1:]
+def sent_ahead(last):
+    pairs = [(i, i + 1) for i in range(lax.axis_size("tm") - 1)]
+    return lax.ppermute(last, "tm", pairs)
+
+
+def sent_sideways(near, far):
     count = lax.axis_size("tile")
     near_pairs = [(i, i ^ 1) for i in range(count) if i ^ 1 < count]
     far_pairs = [pair for i in range(1, count - 1, 2) for pair in ((i, i + 1), (i + 1, i))]
-    rows = jax.ShapeDtypeStruct(
-        (2 + sum(piece.shape[0] for piece in own), columns, channels), jnp.bfloat16
-    )
-    near, far = pl.pallas_call(
-        pick_kernel, out_shape=(rows, rows), in_specs=[VMEM] * (1 + len(own)),
-        out_specs=(VMEM, VMEM), compiler_params=params(8), name="pick",
-    )(past, *own)
     near = lax.ppermute(near, "tile", near_pairs)
     far = lax.ppermute(far, "tile", far_pairs)
-    return past, *own, near, far
+    return near, far
+
+
+def pick(cells, *after):
+    rows = sum(piece.shape[0] for piece in cells)
+    rows = jax.ShapeDtypeStruct((rows, *cells[0].shape[2:]), jnp.bfloat16)
+    return pl.pallas_call(
+        functools.partial(pick_kernel, len(cells)), out_shape=(rows, rows),
+        in_specs=[VMEM] * len(cells) + [pl.BlockSpec(memory_space=pl.ANY)] * len(after),
+        out_specs=(VMEM, VMEM), compiler_params=params(8), name="pick",
+    )(*cells, *after)
 
 
 def exchange(stats):
@@ -291,49 +294,55 @@
     last_shape = jax.ShapeDtypeStruct((2, *frames.shape[1:]), jnp.bfloat16)
     head_shape = jax.ShapeDtypeStruct((depth - 2, *frames.shape[1:]), jnp.bfloat16)
 
-    weights = [pltpu.VMEM((3, 3, 3, channels, channels), jnp.bfloat16), pltpu.SemaphoreType.DMA((3,))]
+    row_shape = jax.ShapeDtypeStruct((depth, columns, channels), jnp.bfloat16)
 
     def active(count):
-        return [pltpu.VMEM((count + 2, height + 2, columns, channels), jnp.bfloat16), *weights]
+        return pltpu.VMEM((count + 2, height + 2, columns, channels), jnp.bfloat16)
 
     def cost(count):
         flops = 2 * 27 * count * height * columns * channels * channels
         return pl.CostEstimate(flops=flops, bytes_accessed=8 << 20, transcendentals=0)
 
-    first_weight = pltpu.with_memory_space_constraint(first_weight, pltpu.HBM)
-    second_weight = pltpu.with_memory_space_constraint(second_weight, pltpu.HBM)
     cells = pltpu.with_memory_space_constraint(frames, pltpu.HBM)
-    stats, head, last = pl.pallas_call(
-        stats_kernel, out_shape=(stats_shape, head_shape, last_shape), in_specs=[VMEM],
-        out_specs=(VMEM, VMEM, VMEM), compiler_params=params(8), cost_estimate=cost(1), name="stats",
+    stats, head, last, near, far = pl.pallas_call(
+        stats_kernel, out_shape=(stats_shape, head_shape, last_shape, row_shape, row_shape),
+        in_specs=[VMEM], out_specs=(VMEM,) * 5, compiler_params=params(8), cost_estimate=cost(1),
+        name="stats",
     )(frames)
-    around = surround(last, (head, last))
+    near, far = sent_sideways(near, far)
+    past = sent_ahead(last)
     stats = exchange(stats)
-    operands = (*around, stats, first_gain[None], first_bias[None], first_weight)
+    corner = sent_sideways(*pick((past,), stats))
+    own = (head, last, near, far, stats, first_gain[None], first_bias[None], first_weight)
+    around = (past, *corner)
+    alone = depth >= 4
+    ahead = (() if alone else around) + own
     last, totals = pl.pallas_call(
-        functools.partial(first_kernel, members, depth - 2, 2, False),
+        functools.partial(first_kernel, members, depth - 2, not alone, False),
         out_shape=(last_shape, jax.ShapeDtypeStruct((2, 8, channels), jnp.float32)),
-        in_specs=[VMEM] * 8 + [HBM], out_specs=(VMEM, VMEM), scratch_shapes=active(2),
+        in_specs=[VMEM] * len(ahead), out_specs=(VMEM, VMEM), scratch_shapes=[active(2)],
         compiler_params=params(24), cost_estimate=cost(2), name="first_last",
-    )(*operands)
+    )(*ahead)
     head, stats = pl.pallas_call(
-        functools.partial(first_kernel, members, 0, 2, True),
+        functools.partial(first_kernel, members, 0, True, True),
         out_shape=(head_shape, stats_shape),
-        in_specs=[VMEM] * 8 + [HBM, VMEM], out_specs=(VMEM, VMEM), scratch_shapes=active(depth - 2),
+        in_specs=[VMEM] * 12, out_specs=(VMEM, VMEM), scratch_shapes=[active(depth - 2)],
         compiler_params=params(24), cost_estimate=cost(depth - 2), name="first_head",
-    )(*operands, totals)
-    around = surround(last, (head, last))
+    )(*around, *own, totals)
+    past = sent_ahead(last)
+    near, far = sent_sideways(*pick((past, head, last)))
     stats = exchange(stats)
     features, patches = pl.pallas_call(
-        functools.partial(second_kernel, members, 2),
+        functools.partial(second_kernel, members),
         out_shape=(cells_shape, jax.ShapeDtypeStruct((parts, rows, LANES), jnp.bfloat16)),
-        in_specs=[VMEM] * 8 + [HBM, HBM, VMEM], out_specs=(HBM, VMEM),
-        scratch_shapes=[active(depth)[0], pltpu.VMEM((height * columns, LANES), jnp.float32),
-                        pltpu.VMEM((parts, rows, LANES), jnp.float32), weights[0],
-                        pltpu.VMEM(frames.shape, jnp.bfloat16), weights[1],
+        in_specs=[VMEM] * 9 + [HBM, VMEM], out_specs=(HBM, VMEM),
+        scratch_shapes=[active(depth), pltpu.VMEM((height * columns, LANES), jnp.float32),
+                        pltpu.VMEM((parts, rows, LANES), jnp.float32),
+                        pltpu.VMEM(frames.shape, jnp.bfloat16),
                         pltpu.SemaphoreType.DMA(()), pltpu.SemaphoreType.DMA((depth,))],
         compiler_params=params(24), cost_estimate=cost(depth), name="second",
-    )(*around, stats, second_gain[None], second_bias[None], second_weight, cells, latent_weight.T)
+    )(past, head, last, near, far, stats, second_gain[None], second_bias[None], second_weight,
+      cells, latent_weight.T)
     received = lax.all_to_all(patches, "tile", split_axis=0, concat_axis=0, tiled=True)
     tokens = pl.pallas_call(
         functools.partial(unpack_kernel, blocks, pairs),

time: 99.2 us -> 82.3 us (0.83)
  Pallas kernels: 36.3 us -> 23.3 us
  waiting for transfers between devices: 13.6 us -> 4.88 us
  starting transfers between devices: 9.03 us -> 13 us
    pallas_call x5, Pallas kernels: 35.2 us -> 22.3 us  [the longest x1 11.5 us: body(): pl.pallas_call(functools.partial(second_kernel, members), out_shape=(cell...]
    ppermute x6 -> x8, waiting for transfers between devices: 13.6 us -> 4.88 us  [the longest x2 4.2 us: sent_ahead(): return lax.ppermute(last, 'tm', pairs)]
    ppermute x6 -> x8, starting transfers between devices: 9.03 us -> 13 us  [the longest x2 7.81 us: sent_ahead(): return lax.ppermute(last, 'tm', pairs)]
  transfers between devices with their start and end apart: 6 -> 8, of which waited for: 2 -> 2; matrix products, arithmetic and copies ran while one was open for 0% -> 0% of each run, Pallas kernels for 9% -> 13%
where the time goes in v1:
time: 82.3 us; the launch traced here: 82 us
  blocking collectives  38.6 us (47%)
  Pallas kernels  23.3 us (28%)
  starting transfers between devices  13 us (16%)
  waiting for transfers between devices  4.88 us (6%)
  local copies, waits for them, and re-layouts  1.4 us (2%)
    all_to_all x2, blocking collectives, exchange(): return lax.all_to_all(stats, ALL, split_axis=0, concat_axis=0, tiled=True)  30.3 us
    pallas_call x1, Pallas kernels, body(): pl.pallas_call(functools.partial(second_kernel, members), out_shape=(cell...  11.5 us
    all_to_all x1, blocking collectives, body(): lax.all_to_all(patches, 'tile', split_axis=0, concat_axis=0, tiled=True)  8.3 us
    ppermute x2, starting transfers between devices, sent_ahead(): return lax.ppermute(last, 'tm', pairs)  7.81 us
    pallas_call x1, Pallas kernels, body(): pl.pallas_call(functools.partial(first_kernel, members, 0, True, True), o...  5.38 us
    pallas_call x1, Pallas kernels, body(): pl.pallas_call(functools.partial(first_kernel, members, depth - 2, not al...  5.32 us
    ppermute x2, waiting for transfers between devices, sent_ahead(): return lax.ppermute(last, 'tm', pairs)  4.2 us
    ppermute x3, starting transfers between devices, sent_sideways(): near = lax.ppermute(near, 'tile', near_pairs)  3.18 us
  transfers between devices with their start and end apart: 8, of which 2 were waited for; matrix products, arithmetic and copies ran while one was open for 0% of the time, Pallas kernels for 13%

profile of v1, /device:TPU:0, one launch (start us, length us, event | category | flops | bytes accessed | tf_op | source)
XLA Modules:
  0.0 82.0 jit_solution(3981678361849840118)
XLA Ops:
  0.6 0.0 copy-start
  0.6 0.0 copy-start.2
  0.7 1.4 %copy-done.2 = bf16[4,4,128,256]{3,2,1,0:T(8,128)(2,1)S(1)} copy-done((bf16[4,4,128,256]{3,2,1,0:T(8,128)(2,1)S(1)}, bf16[4,4,128,256]{3,2,1,0:T(8,128)(2,1)}, u32[]{:S(2)}) %copy-start.2) | copy-done | bytes 1048600
  2.0 0.3 stats.1
  2.3 0.6 collective-permute-start
  2.9 0.7 collective-permute-start.1
  3.6 4.4 %collective-permute-start.3 = (bf16[2,4,128,256]{3,2,1,0:T(8,128)(2,1)S(1)}, bf16[2,4,128,256]{3,2,1,0:T(8,128)(2,1)S(1)}, u32[]{:S(2)}, u32[]{:S(2)}) collective-permute-start(bf16[2,4,128,256]{3,2,1,0:T(8,128)(2,1)S(1)} %get-tuple-element.18.refs_1_.refs_4_), channel_id=1, source_target_pairs={{0,8},{8,16},{16,24},{1,9},{9,17},{17,25},{2,10},{10,18},{18,26},{... | collective-permute-start | bytes 1572872 | tf_op jit(solution)/shard_map/ppermute | solution.py:256
  8.0 14.9 %all_to_all.15.refs_4_.refs_1_.refs_7_ = f32[32,2,256]{2,1,0:T(2,128)S(1)} all-to-all(f32[32,2,256]{2,1,0:T(2,128)S(1)} %get-tuple-element.21), channel_id=1, replica_groups=mesh['tm'=4,'tile'=8] {'tm','tile'}, dimensions={0} | all-to-all | bytes 131072 | tf_op jit(solution)/shard_map/all_to_all | solution.py:279
  22.9 0.0 collective-permute-done.refs_2_.refs_5_
  22.9 0.0 collective-permute-done.1.refs_3_.refs_6_
  22.9 0.0 copy-done
  22.9 0.0 copy-done.4
  23.0 5.3 %first_last.1 = (bf16[2,4,128,256]{3,2,1,0:T(8,128)(2,1)S(1)}, f32[2,8,256]{2,1,0:T(8,128)S(1)}) custom-call(bf16[2,4,128,256]{3,2,1,0:T(8,128)(2,1)S(1)} %get-tuple-element.17.refs_0_.refs_3_, bf16[2,4,128,256]{3,2,1,0:T(8,128)(2,1)S(1)} %get-tuple-element.18.refs_1_.refs_4_, bf16[4,128,256]{2,1,0:T(8,128)(2,1)S(1)} %collective-permute-done.refs_2_.refs_5_, ...), custom_call_target="tpu_custom_call" | custom-call | flops 3623878656 | bytes 8388608 | tf_op jit(solution)/shard_map/first_last/pallas_call | solution.py:320
  28.3 3.4 %collective-permute-start.2 = (bf16[2,4,128,256]{3,2,1,0:T(8,128)(2,1)S(1)}, bf16[2,4,128,256]{3,2,1,0:T(8,128)(2,1)S(1)}, u32[]{:S(2)}, u32[]{:S(2)}) collective-permute-start(bf16[2,4,128,256]{3,2,1,0:T(8,128)(2,1)S(1)} %get-tuple-element.22.refs_2_.last), channel_id=1, source_target_pairs={{0,8},{8,16},{16,24},{1,9},{9,17},{17,25},{2,10},{10,18},{18,26},{... | collective-permute-start | bytes 1572872 | tf_op jit(solution)/shard_map/ppermute | solution.py:256
  31.7 0.0 collective-permute-done.3.refs_0_
  31.7 0.1 collective-permute-start.4
  31.8 0.7 collective-permute-start.5
  32.5 0.7 collective-permute-done.4.refs_1_
  33.1 0.0 collective-permute-done.5.refs_2_
  33.2 0.0 copy-start.7
  33.2 5.4 %first_head.1 = (bf16[2,4,128,256]{3,2,1,0:T(8,128)(2,1)S(1)}, f32[32,2,256]{2,1,0:T(2,128)S(1)}) custom-call(bf16[2,4,128,256]{3,2,1,0:T(8,128)(2,1)S(1)} %collective-permute-done.3.refs_0_, bf16[2,128,256]{2,1,0:T(8,128)(2,1)S(1)} %collective-permute-done.4.refs_1_, bf16[2,128,256]{2,1,0:T(8,128)(2,1)S(1)} %collective-permute-done.5.refs_2_, ...), custom_call_target="tpu_custom_call" | custom-call | flops 3623878656 | bytes 8388608 | tf_op jit(solution)/shard_map/first_head/pallas_call | solution.py:326
  38.6 4.2 %collective-permute-done.2.refs_0_.past = bf16[2,4,128,256]{3,2,1,0:T(8,128)(2,1)S(1)} collective-permute-done((bf16[2,4,128,256]{3,2,1,0:T(8,128)(2,1)S(1)}, bf16[2,4,128,256]{3,2,1,0:T(8,128)(2,1)S(1)}, u32[]{:S(2)}, u32[]{:S(2)}) %collective-permute-start.2) | collective-permute-done | bytes 524320 | tf_op jit(solution)/shard_map/ppermute | solution.py:256
  42.8 0.1 pick.3
  42.8 2.6 %collective-permute-start.6 = (bf16[6,128,256]{2,1,0:T(8,128)(2,1)S(1)}, bf16[6,128,256]{2,1,0:T(8,128)(2,1)S(1)}, u32[]{:S(2)}, u32[]{:S(2)}) collective-permute-start(bf16[6,128,256]{2,1,0:T(8,128)(2,1)S(1)} %get-tuple-element.27), channel_id=1, source_target_pairs={{0,1},{1,0},{2,3},{3,2},{4,5},{5,4},{6,7},{7,6},{8,9},{9,8},{10,11... | collective-permute-start | bytes 1179656 | tf_op jit(solution)/shard_map/ppermute | solution.py:263
  45.4 0.7 collective-permute-start.7
  46.0 15.3 %all_to_all.16.stats = f32[32,2,256]{2,1,0:T(2,128)S(1)} all-to-all(f32[32,2,256]{2,1,0:T(2,128)S(1)} %get-tuple-element.29), channel_id=1, replica_groups=mesh['tm'=4,'tile'=8] {'tm','tile'}, dimensions={0} | all-to-all | bytes 131072 | tf_op jit(solution)/shard_map/all_to_all | solution.py:279
  61.4 0.0 collective-permute-done.6.near
  61.4 0.0 collective-permute-done.7.far
  61.4 0.0 copy-done.1
  61.4 11.5 %second.1 = (bf16[4,4,128,256]{3,2,1,0:T(8,128)(2,1)}, bf16[8,32,128]{2,1,0:T(8,128)(2,1)S(1)}) custom-call(bf16[2,4,128,256]{3,2,1,0:T(8,128)(2,1)S(1)} %collective-permute-done.2.refs_0_.past, bf16[2,4,128,256]{3,2,1,0:T(8,128)(2,1)S(1)} %get-tuple-element.26.refs_1_.head, bf16[2,4,128,256]{3,2,1,0:T(8,128)(2,1)S(1)} %get-tuple-element.22.refs_2_.last, ...), custom_call_target="tpu_custom_call" | custom-call | flops 7247757312 | bytes 8388608 | tf_op jit(solution)/shard_map/second/pallas_call | solution.py:335
  72.9 8.3 %all_to_all.17.received = bf16[8,32,128]{2,1,0:T(8,128)(2,1)S(1)} all-to-all(bf16[8,32,128]{2,1,0:T(8,128)(2,1)S(1)} %get-tuple-element.31), channel_id=1, replica_groups=mesh['tm'=4,'tile'=8] {'tile'}, dimensions={0} | all-to-all | bytes 131072 | tf_op jit(solution)/shard_map/all_to_all | solution.py:346
  81.2 0.8 unpack.1
  (10 shorter events, 0.0 us)
Async XLA Ops:
  0.6 22.3 %copy-start = (bf16[3,3,3,256,256]{4,3,2,1,0:T(8,128)(2,1)S(1)}, bf16[3,3,3,256,256]{4,3,2,1,0:T(8,128)(2,1)}, u32[]{:S(2)}) copy-start(bf16[3,3,3,256,256]{4,3,2,1,0:T(8,128)(2,1)} %refs_10_.1) | copy-start | bytes 10616836
  0.6 1.4 %copy-start.2 = (bf16[4,4,128,256]{3,2,1,0:T(8,128)(2,1)S(1)}, bf16[4,4,128,256]{3,2,1,0:T(8,128)(2,1)}, u32[]{:S(2)}) copy-start(bf16[4,4,128,256]{3,2,1,0:T(8,128)(2,1)} %frames.1) | copy-start | bytes 3145732
  2.0 20.9 %copy-start.4 = (f32[256]{0:T(256)S(1)}, f32[256]{0:T(256)}, u32[]{:S(2)}) copy-start(f32[256]{0:T(256)} %param.9) | copy-start | bytes 3076
  2.0 20.9 %copy-start.5 = (f32[256]{0:T(256)S(1)}, f32[256]{0:T(256)}, u32[]{:S(2)}) copy-start(f32[256]{0:T(256)} %param.10) | copy-start | bytes 3076
  2.3 20.6 %collective-permute-start = (bf16[4,128,256]{2,1,0:T(8,128)(2,1)S(1)}, bf16[4,128,256]{2,1,0:T(8,128)(2,1)S(1)}, u32[]{:S(2)}, u32[]{:S(2)}) collective-permute-start(bf16[4,128,256]{2,1,0:T(8,128)(2,1)S(1)} %get-tuple-element.19), channel_id=1, source_target_pairs={{0,1},{1,0},{2,3},{3,2},{4,5},{5,4},{6,7},{7,6},{8,9},{9,8},{10,11... | collective-permute-start | bytes 786440 | tf_op jit(solution)/shard_map/ppermute | solution.py:263
  2.9 20.1 %collective-permute-start.1 = (bf16[4,128,256]{2,1,0:T(8,128)(2,1)S(1)}, bf16[4,128,256]{2,1,0:T(8,128)(2,1)S(1)}, u32[]{:S(2)}, u32[]{:S(2)}) collective-permute-start(bf16[4,128,256]{2,1,0:T(8,128)(2,1)S(1)} %get-tuple-element.20), channel_id=1, source_target_pairs={{1,2},{2,1},{3,4},{4,3},{5,6},{6,5},{9,10},{10,9},{11,12},{12,11},... | collective-permute-start | bytes 786440 | tf_op jit(solution)/shard_map/ppermute | solution.py:264
  3.6 28.1 %collective-permute-start.3 = (bf16[2,4,128,256]{3,2,1,0:T(8,128)(2,1)S(1)}, bf16[2,4,128,256]{3,2,1,0:T(8,128)(2,1)S(1)}, u32[]{:S(2)}, u32[]{:S(2)}) collective-permute-start(bf16[2,4,128,256]{3,2,1,0:T(8,128)(2,1)S(1)} %get-tuple-element.18.refs_1_.refs_4_), channel_id=1, source_target_pairs={{0,8},{8,16},{16,24},{1,9},{9,17},{17,25},{2,10},{10,18},{18,26},{... | collective-permute-start | bytes 1572872 | tf_op jit(solution)/shard_map/ppermute | solution.py:256
  28.3 14.5 %collective-permute-start.2 = (bf16[2,4,128,256]{3,2,1,0:T(8,128)(2,1)S(1)}, bf16[2,4,128,256]{3,2,1,0:T(8,128)(2,1)S(1)}, u32[]{:S(2)}, u32[]{:S(2)}) collective-permute-start(bf16[2,4,128,256]{3,2,1,0:T(8,128)(2,1)S(1)} %get-tuple-element.22.refs_2_.last), channel_id=1, source_target_pairs={{0,8},{8,16},{16,24},{1,9},{9,17},{17,25},{2,10},{10,18},{18,26},{... | collective-permute-start | bytes 1572872 | tf_op jit(solution)/shard_map/ppermute | solution.py:256
  31.7 1.4 %collective-permute-start.4 = (bf16[2,128,256]{2,1,0:T(8,128)(2,1)S(1)}, bf16[2,128,256]{2,1,0:T(8,128)(2,1)S(1)}, u32[]{:S(2)}, u32[]{:S(2)}) collective-permute-start(bf16[2,128,256]{2,1,0:T(8,128)(2,1)S(1)} %get-tuple-element.23), channel_id=1, source_target_pairs={{0,1},{1,0},{2,3},{3,2},{4,5},{5,4},{6,7},{7,6},{8,9},{9,8},{10,11... | collective-permute-start | bytes 393224 | tf_op jit(solution)/shard_map/ppermute | solution.py:263
  31.8 1.3 %collective-permute-start.5 = (bf16[2,128,256]{2,1,0:T(8,128)(2,1)S(1)}, bf16[2,128,256]{2,1,0:T(8,128)(2,1)S(1)}, u32[]{:S(2)}, u32[]{:S(2)}) collective-permute-start(bf16[2,128,256]{2,1,0:T(8,128)(2,1)S(1)} %get-tuple-element.24), channel_id=1, source_target_pairs={{1,2},{2,1},{3,4},{4,3},{5,6},{6,5},{9,10},{10,9},{11,12},{12,11},... | collective-permute-start | bytes 393224 | tf_op jit(solution)/shard_map/ppermute | solution.py:264
  33.1 28.3 %copy-start.1 = (bf16[3,3,3,256,256]{4,3,2,1,0:T(8,128)(2,1)S(1)}, bf16[3,3,3,256,256]{4,3,2,1,0:T(8,128)(2,1)}, u32[]{:S(2)}) copy-start(bf16[3,3,3,256,256]{4,3,2,1,0:T(8,128)(2,1)} %weight.1) | copy-start | bytes 10616836
  33.1 28.3 %copy-start.3 = (bf16[256,16]{0,1:T(8,128)(2,1)S(1)}, bf16[256,16]{0,1:T(8,128)(2,1)}, u32[]{:S(2)}) copy-start(bf16[256,16]{0,1:T(8,128)(2,1)} %param.15) | copy-start | bytes 24580
  33.2 28.3 %copy-start.6 = (f32[256]{0:T(256)S(1)}, f32[256]{0:T(256)}, u32[]{:S(2)}) copy-start(f32[256]{0:T(256)} %param.12) | copy-start | bytes 3076
  33.2 28.3 %copy-start.7 = (f32[256]{0:T(256)S(1)}, f32[256]{0:T(256)}, u32[]{:S(2)}) copy-start(f32[256]{0:T(256)} %param.13) | copy-start | bytes 3076
  42.8 18.6 %collective-permute-start.6 = (bf16[6,128,256]{2,1,0:T(8,128)(2,1)S(1)}, bf16[6,128,256]{2,1,0:T(8,128)(2,1)S(1)}, u32[]{:S(2)}, u32[]{:S(2)}) collective-permute-start(bf16[6,128,256]{2,1,0:T(8,128)(2,1)S(1)} %get-tuple-element.27), channel_id=1, source_target_pairs={{0,1},{1,0},{2,3},{3,2},{4,5},{5,4},{6,7},{7,6},{8,9},{9,8},{10,11... | collective-permute-start | bytes 1179656 | tf_op jit(solution)/shard_map/ppermute | solution.py:263
  45.4 16.0 %collective-permute-start.7 = (bf16[6,128,256]{2,1,0:T(8,128)(2,1)S(1)}, bf16[6,128,256]{2,1,0:T(8,128)(2,1)S(1)}, u32[]{:S(2)}, u32[]{:S(2)}) collective-permute-start(bf16[6,128,256]{2,1,0:T(8,128)(2,1)S(1)} %get-tuple-element.28), channel_id=1, source_target_pairs={{1,2},{2,1},{3,4},{4,3},{5,6},{6,5},{9,10},{10,9},{11,12},{12,11},... | collective-permute-start | bytes 1179656 | tf_op jit(solution)/shard_map/ppermute | solution.py:264

commit v2 on v1

--- a/solution.py
+++ b/solution.py
@@ -95,16 +95,14 @@
     return value * (0.5 * jnp.tanh(0.5 * value) + 0.5)
 
 
-def fill(active_ref, begin, pieces, scale):
-    factor, offset = scale
+def edges(active_ref, scale):
+    index, count = lax.axis_index("tile"), lax.axis_size("tile")
     height = active_ref.shape[1] - 2
-    index, count = lax.axis_index("tile"), lax.axis_size("tile")
     even = index % 2 == 0
     first = (lax.axis_index("tm") > 0).astype(jnp.float32)
-    near_row, far_row = jnp.where(even, height + 1, 0), jnp.where(even, 0, height + 1)
-    above, below = index > 0, index < count - 1
-    near_keep = jnp.where(even, below, above).astype(jnp.float32)
-    far_keep = jnp.where(even, above, below).astype(jnp.float32)
+    above = (index > 0).astype(jnp.float32)
+    below = (index < count - 1).astype(jnp.float32)
+    factor, offset = scale
 
     def put(t, h, value, keep):
         active = silu(value.astype(jnp.float32) * factor + offset)
@@ -112,20 +110,26 @@
             active = active * keep
         active_ref[t, h] = active.astype(jnp.bfloat16)
 
-    for frame, ref, near_ref, far_ref, shift, is_past in pieces:
-        skip = max(0, begin - frame)
-        stop = min(ref.shape[0], active_ref.shape[0] + begin - frame)
-
-        def one(t, carry):
-            place = frame + t - begin
-            for h in range(height):
-                put(place, h + 1, ref[t, h], first if is_past else None)
-            put(place, near_row, near_ref[shift + t], near_keep * first if is_past else near_keep)
-            put(place, far_row, far_ref[shift + t], far_keep * first if is_past else far_keep)
-            return carry
-
-        if stop > skip:
-            lax.fori_loop(skip, stop, one, 0)
+    def fill(t, source):
+        cells, near, far, is_past = source
+        near, far = near[...], far[...]
+        put(t, 0, jnp.where(even, far, near), above * first if is_past else above)
+        for h in range(height):
+            put(t, h + 1, cells[h], first if is_past else None)
+        put(t, height + 1, jnp.where(even, near, far), below * first if is_past else below)
+
+    return fill
+
+
+def sources(pieces):
+    found = []
+    for cells, near, far, is_past in pieces:
+        row = 0
+        for ref in cells:
+            for t in range(ref.shape[0]):
+                found.append((ref.at[t], near.at[row], far.at[row], is_past))
+                row += 1
+    return found
 
 
 def convolve(active_ref, weight_ref, t, height):
@@ -146,56 +150,68 @@
     return totals[1] + left + right
 
 
-def first_kernel(members, begin, with_past, with_totals, *refs):
+def split(refs, with_past):
     refs = list(refs)
-    pieces = []
-    if with_past:
-        past, near, far = refs[:3]
-        pieces.append((0, past, near, far, 0, True))
-        del refs[:3]
-    head, last, near, far, stats, gain, bias, weight = refs[:8]
-    before = head.shape[0]
-    pieces.append((2, head, near, far, 0, False))
-    pieces.append((2 + before, last, near, far, before, False))
-    hidden_ref, totals_ref, active_ref = refs[-3:]
-    depth, height, columns, channels = hidden_ref.shape
-    fill(active_ref, begin, pieces, scale_of(stats, gain, bias, members))
-
-    def step(t, carry):
-        sums, squares = carry
+    pieces = [((refs.pop(0),), refs.pop(0), refs.pop(0), True)] if with_past else []
+    head, last, near, far = refs[:4]
+    pieces.append(((head, last), near, far, False))
+    return sources(pieces), refs[4:]
+
+
+def first_kernel(members, begin, count, with_past, *refs):
+    found, refs = split(refs, with_past)
+    found = found if with_past else [None, None, *found]
+    stats, gain, bias, weight = refs[:4]
+    active_ref = refs[-1]
+    height, columns, channels = active_ref.shape[1] - 2, *active_ref.shape[2:]
+    even = lax.axis_index("tile") % 2 == 0
+    fill = edges(active_ref, scale_of(stats, gain, bias, members))
+    if begin == 0:
+        totals, near_before, far_before, hidden_ref, totals_ref, near_ref, far_ref = refs[4:-1]
+        near_ref[count:] = near_before[...]
+        far_ref[count:] = far_before[...]
+        sums, squares = totals[0], totals[1]
+    else:
+        hidden_ref, totals_ref, near_ref, far_ref = refs[4:-1]
+        sums = squares = jnp.zeros((8, channels), jnp.float32)
+    for t in range(2):
+        fill(t, found[begin + t])
+    for t in range(count):
+        fill(t + 2, found[begin + t + 2])
         hidden = convolve(active_ref, weight, t, height).astype(jnp.bfloat16)
-        hidden_ref[t] = hidden.reshape(height, columns, channels)
         wide = hidden.astype(jnp.float32)
-        return sums + row_totals(wide), squares + row_totals(wide * wide)
-
-    zero = jnp.zeros((8, channels), jnp.float32)
-    start = (refs[8][0], refs[8][1]) if with_totals else (zero, zero)
-    sums, squares = lax.fori_loop(0, depth, step, start)
-    if with_totals:
+        sums = sums + row_totals(wide)
+        squares = squares + row_totals(wide * wide)
+        hidden = hidden.reshape(height, columns, channels)
+        hidden_ref[t] = hidden
+        near_ref[t] = jnp.where(even, hidden[height - 1], hidden[0])
+        far_ref[t] = jnp.where(even, hidden[0], hidden[height - 1])
+    if begin == 0:
         put_stats(totals_ref, sums, squares)
     else:
         totals_ref[0] = sums
         totals_ref[1] = squares
 
 
-def second_kernel(members, past, head, last, near, far, stats, gain, bias, weight, frames, latent,
-                  features_hbm, patches_ref, active_ref, latents_ref, packed_ref, cells_ref,
-                  in_sem, out_sem):
-    depth, height, columns, channels = frames.shape
-    before = head.shape[0]
-    loads = pltpu.make_async_copy(frames, cells_ref, in_sem)
+def second_kernel(members, begin, count, with_past, *refs):
+    found, refs = split(refs, with_past)
+    found = found if with_past else [None, None, *found]
+    stats, gain, bias, weight, frames, latent = refs[:6]
+    active_ref, latents_ref, packed_ref, cells_ref, in_sem, out_sem = refs[-6:]
+    height, columns, channels = active_ref.shape[1] - 2, *active_ref.shape[2:]
+    parts, rows = packed_ref.shape[:2]
+    if begin == 0:
+        before, _, features_hbm, patches_ref = refs[6:-6]
+        kept = rows - before.shape[1]
+        packed_ref[:, kept:, :] = before[...].astype(jnp.float32)
+    else:
+        features_hbm, patches_ref = refs[6:-6]
+        kept = rows
+    loads = pltpu.make_async_copy(frames.at[begin : begin + count], cells_ref, in_sem)
     loads.start()
     width = LANES // 8
-    pieces = [
-        (0, past, near, far, 0, True),
-        (2, head, near, far, 2, False),
-        (2 + before, last, near, far, 2 + before, False),
-    ]
-    fill(active_ref, 0, pieces, scale_of(stats, gain, bias, members))
-    loads.wait()
-    parts, rows = packed_ref.shape[:2]
     pairs = height // 2
-    blocks = rows // (depth * pairs)
+    blocks = kept // (count * pairs)
     lane = lax.broadcasted_iota(jnp.int32, (columns // 4, LANES), 1) // width
     spread = lax.broadcasted_iota(jnp.int32, (width, LANES), 0) == (
         lax.broadcasted_iota(jnp.int32, (width, LANES), 1) % width
@@ -204,13 +220,22 @@
         latent[...], spread.astype(jnp.bfloat16), (((0,), (0,)), ((), ())),
         preferred_element_type=jnp.float32,
     ).astype(jnp.bfloat16)
-
-    def step(t, carry):
+    fill = edges(active_ref, scale_of(stats, gain, bias, members))
+    for t in range(3):
+        fill(t, found[begin + t])
+    loads.wait()
+    stores = []
+    for t in range(count):
+        if t > 0:
+            fill(t + 2, found[begin + t + 2])
         branch = convolve(active_ref, weight, t, height)
         residual = cells_ref[t].reshape(height * columns, channels).astype(jnp.float32)
         features = (residual + branch).astype(jnp.bfloat16)
         cells_ref[t] = features.reshape(height, columns, channels)
-        pltpu.make_async_copy(cells_ref.at[t], features_hbm.at[t], out_sem.at[t]).start()
+        stores.append(
+            pltpu.make_async_copy(cells_ref.at[t], features_hbm.at[begin + t], out_sem.at[t])
+        )
+        stores[-1].start()
         latents_ref[...] = (
             jnp.dot(features, wide_latent, preferred_element_type=jnp.float32)
             .astype(jnp.bfloat16)
@@ -227,12 +252,9 @@
                 packed_ref[d, pl.ds(t * blocks * pairs + i, blocks, stride=pairs), :] = mixed[
                     d * blocks : (d + 1) * blocks
                 ]
-        return carry
-
-    lax.fori_loop(0, depth, step, 0)
     patches_ref[...] = packed_ref[...].astype(jnp.bfloat16)
-    for t in range(depth):
-        pltpu.make_async_copy(cells_ref.at[t], features_hbm.at[t], out_sem.at[t]).wait()
+    for store in stores:
+        store.wait()
 
 
 def unpack_kernel(blocks, pairs, received, tokens_ref, flat_ref, mixed_ref):
@@ -309,40 +331,62 @@
         in_specs=[VMEM], out_specs=(VMEM,) * 5, compiler_params=params(8), cost_estimate=cost(1),
         name="stats",
     )(frames)
-    near, far = sent_sideways(near, far)
-    past = sent_ahead(last)
-    stats = exchange(stats)
-    corner = sent_sideways(*pick((past,), stats))
+
+    def gather(near, far, last, stats):
+        past = sent_ahead(last)
+        near, far = sent_sideways(near, far)
+        stats = exchange(stats)
+        corner = sent_sideways(*pick((past,), stats))
+        return (past, *corner), near, far, stats
+
+    alone = depth >= 4
+    ahead_shape = jax.ShapeDtypeStruct((2, columns, channels), jnp.bfloat16)
+    around, near, far, stats = gather(near, far, last, stats)
     own = (head, last, near, far, stats, first_gain[None], first_bias[None], first_weight)
-    around = (past, *corner)
-    alone = depth >= 4
     ahead = (() if alone else around) + own
-    last, totals = pl.pallas_call(
-        functools.partial(first_kernel, members, depth - 2, not alone, False),
-        out_shape=(last_shape, jax.ShapeDtypeStruct((2, 8, channels), jnp.float32)),
-        in_specs=[VMEM] * len(ahead), out_specs=(VMEM, VMEM), scratch_shapes=[active(2)],
+    last, totals, near, far = pl.pallas_call(
+        functools.partial(first_kernel, members, depth - 2, 2, not alone),
+        out_shape=(last_shape, jax.ShapeDtypeStruct((2, 8, channels), jnp.float32),
+                   ahead_shape, ahead_shape),
+        in_specs=[VMEM] * len(ahead), out_specs=(VMEM,) * 4, scratch_shapes=[active(2)],
         compiler_params=params(24), cost_estimate=cost(2), name="first_last",
     )(*ahead)
-    head, stats = pl.pallas_call(
-        functools.partial(first_kernel, members, 0, True, True),
-        out_shape=(head_shape, stats_shape),
-        in_specs=[VMEM] * 12, out_specs=(VMEM, VMEM), scratch_shapes=[active(depth - 2)],
+    head, stats, near, far = pl.pallas_call(
+        functools.partial(first_kernel, members, 0, depth - 2, True),
+        out_shape=(head_shape, stats_shape, row_shape, row_shape),
+        in_specs=[VMEM] * 14, out_specs=(VMEM,) * 4, scratch_shapes=[active(depth - 2)],
         compiler_params=params(24), cost_estimate=cost(depth - 2), name="first_head",
-    )(*around, *own, totals)
-    past = sent_ahead(last)
-    near, far = sent_sideways(*pick((past, head, last)))
-    stats = exchange(stats)
+    )(*around, *own, totals, near, far)
+
+    tail_rows = 2 * blocks * pairs
+
+    def scratch(count, held):
+        return [
+            active(count), pltpu.VMEM((height * columns, LANES), jnp.float32),
+            pltpu.VMEM((parts, held, LANES), jnp.float32),
+            pltpu.VMEM((count, *frames.shape[1:]), jnp.bfloat16),
+            pltpu.SemaphoreType.DMA(()), pltpu.SemaphoreType.DMA((count,)),
+        ]
+
+    around, near, far, stats = gather(near, far, last, stats)
+    own = (head, last, near, far, stats, second_gain[None], second_bias[None], second_weight,
+           cells, latent_weight.T)
+    ahead = (() if alone else around) + own
     features, patches = pl.pallas_call(
-        functools.partial(second_kernel, members),
+        functools.partial(second_kernel, members, depth - 2, 2, not alone),
+        out_shape=(cells_shape,
+                   jax.ShapeDtypeStruct((parts, tail_rows, LANES), jnp.bfloat16)),
+        in_specs=[VMEM] * (len(ahead) - 2) + [HBM, VMEM], out_specs=(HBM, VMEM),
+        scratch_shapes=scratch(2, tail_rows),
+        compiler_params=params(24), cost_estimate=cost(2), name="second_last",
+    )(*ahead)
+    features, patches = pl.pallas_call(
+        functools.partial(second_kernel, members, 0, depth - 2, True),
         out_shape=(cells_shape, jax.ShapeDtypeStruct((parts, rows, LANES), jnp.bfloat16)),
-        in_specs=[VMEM] * 9 + [HBM, VMEM], out_specs=(HBM, VMEM),
-        scratch_shapes=[active(depth), pltpu.VMEM((height * columns, LANES), jnp.float32),
-                        pltpu.VMEM((parts, rows, LANES), jnp.float32),
-                        pltpu.VMEM(frames.shape, jnp.bfloat16),
-                        pltpu.SemaphoreType.DMA(()), pltpu.SemaphoreType.DMA((depth,))],
-        compiler_params=params(24), cost_estimate=cost(depth), name="second",
-    )(past, head, last, near, far, stats, second_gain[None], second_bias[None], second_weight,
-      cells, latent_weight.T)
+        in_specs=[VMEM] * 11 + [HBM, VMEM, VMEM, HBM], out_specs=(HBM, VMEM),
+        scratch_shapes=scratch(depth - 2, rows), input_output_aliases={14: 0},
+        compiler_params=params(24), cost_estimate=cost(depth - 2), name="second_head",
+    )(*around, *own, patches, features)
     received = lax.all_to_all(patches, "tile", split_axis=0, concat_axis=0, tiled=True)
     tokens = pl.pallas_call(
         functools.partial(unpack_kernel, blocks, pairs),

time: 82.3 us -> 77.2 us (0.938)
  waiting for transfers between devices: 4.88 us -> 0.03 us
  blocking collectives: 38.6 us -> 37.4 us
    ppermute x2, waiting for transfers between devices: 4.2 us -> 0.01 us  [sent_ahead(): return lax.ppermute(last, 'tm', pairs)]
    all_to_all x2, blocking collectives: 30.3 us -> 27.2 us  [exchange(): return lax.all_to_all(stats, ALL, split_axis=0, concat_axis=0, tiled=True)]
    all_to_all x1, blocking collectives: 8.3 us -> 10.3 us  [body(): lax.all_to_all(patches, 'tile', split_axis=0, concat_axis=0, tiled=True)]
    ppermute x3 -> x4, starting transfers between devices: 2.01 us -> 2.84 us  [sent_sideways(): far = lax.ppermute(far, 'tile', far_pairs)]
    pallas_call x3 -> x4, Pallas kernels: 22.2 us -> 22.5 us  [the longest x1 7.06 us: body(): pl.pallas_call(functools.partial(second_kernel, members, depth - 2, 2, no...]
    ppermute x3 -> x4, starting transfers between devices: 3.18 us -> 3.14 us  [sent_sideways(): near = lax.ppermute(near, 'tile', near_pairs)]
  transfers between devices with their start and end apart: 8 -> 10, of which waited for: 2 -> 0; matrix products, arithmetic and copies ran while one was open for 0% -> 0% of each run, Pallas kernels for 13% -> 20%
where the time goes in v2:
time: 77.2 us; the launch traced here: 76.8 us
  blocking collectives  37.4 us (48%)
  Pallas kernels  23.6 us (31%)
  starting transfers between devices  13.4 us (17%)
  local copies, waits for them, and re-layouts  1.41 us (2%)
  between operations  0.9 us (1%)
    all_to_all x2, blocking collectives, exchange(): return lax.all_to_all(stats, ALL, split_axis=0, concat_axis=0, tiled=True)  27.2 us
    all_to_all x1, blocking collectives, body(): lax.all_to_all(patches, 'tile', split_axis=0, concat_axis=0, tiled=True)  10.3 us
    ppermute x2, starting transfers between devices, sent_ahead(): return lax.ppermute(last, 'tm', pairs)  7.43 us
    pallas_call x1, Pallas kernels, body(): pl.pallas_call(functools.partial(second_kernel, members, depth - 2, 2, no...  7.06 us
    pallas_call x1, Pallas kernels, body(): pl.pallas_call(functools.partial(second_kernel, members, 0, depth - 2, Tr...  7.02 us
    pallas_call x1, Pallas kernels, body(): pl.pallas_call(functools.partial(first_kernel, members, 0, depth - 2, Tru...  4.27 us
    pallas_call x1, Pallas kernels, body(): pl.pallas_call(functools.partial(first_kernel, members, depth - 2, 2, not...  4.2 us
    ppermute x4, starting transfers between devices, sent_sideways(): near = lax.ppermute(near, 'tile', near_pairs)  3.14 us
  transfers between devices with their start and end apart: 10, of which 0 were waited for; matrix products, arithmetic and copies ran while one was open for 0% of the time, Pallas kernels for 20%

profile of v2, /device:TPU:0, one launch (start us, length us, event | category | flops | bytes accessed | tf_op | source)
XLA Modules:
  0.0 76.8 jit_solution(3157480271077444263)
XLA Ops:
  0.6 0.0 copy-start.2
  0.7 1.4 %copy-done.2 = bf16[4,4,128,256]{3,2,1,0:T(8,128)(2,1)S(1)} copy-done((bf16[4,4,128,256]{3,2,1,0:T(8,128)(2,1)S(1)}, bf16[4,4,128,256]{3,2,1,0:T(8,128)(2,1)}, u32[]{:S(2)}) %copy-start.2) | copy-done | bytes 1048600
  2.0 0.3 stats.1
  2.3 4.9 %collective-permute-start.3 = (bf16[2,4,128,256]{3,2,1,0:T(8,128)(2,1)S(1)}, bf16[2,4,128,256]{3,2,1,0:T(8,128)(2,1)S(1)}, u32[]{:S(2)}, u32[]{:S(2)}) collective-permute-start(bf16[2,4,128,256]{3,2,1,0:T(8,128)(2,1)S(1)} %get-tuple-element.24.refs_1_.refs_4_), channel_id=1, source_target_pairs={{0,8},{8,16},{16,24},{1,9},{9,17},{17,25},{2,10},{10,18},{18,26},{... | collective-permute-start | bytes 1572872 | tf_op jit(solution)/shard_map/ppermute | solution.py:278
  7.2 0.1 collective-permute-start
  7.3 0.7 collective-permute-start.1
  8.0 13.9 %all_to_all.15.refs_4_.refs_1_.refs_7_ = f32[32,2,256]{2,1,0:T(2,128)S(1)} all-to-all(f32[32,2,256]{2,1,0:T(2,128)S(1)} %get-tuple-element.27), channel_id=1, replica_groups=mesh['tm'=4,'tile'=8] {'tm','tile'}, dimensions={0} | all-to-all | bytes 131072 | tf_op jit(solution)/shard_map/all_to_all | solution.py:301
  21.9 0.0 collective-permute-done.3.refs_0_
  21.9 0.2 collective-permute-start.4
  22.1 0.7 collective-permute-start.5
  22.7 0.0 collective-permute-done.refs_2_.refs_5_
  22.7 0.0 collective-permute-done.1.refs_3_.refs_6_
  22.8 4.2 %first_last.1 = (bf16[2,4,128,256]{3,2,1,0:T(8,128)(2,1)S(1)}, f32[2,8,256]{2,1,0:T(8,128)S(1)}, bf16[2,128,256]{2,1,0:T(8,128)(2,1)S(1)}, bf16[2,128,256]{2,1,0:T(8,128)(2,1)S(1)}) custom-call(bf16[2,4,128,256]{3,2,1,0:T(8,128)(2,1)S(1)} %get-tuple-element.23.refs_0_.refs_3_, bf16[2,4,128,256]{3,2,1,0:T(8,128)(2,1)S(1)} %get-tuple-element.24.refs_1_.refs_4_, ...), custom_call_target="tpu_custom_call" | custom-call | flops 3623878656 | bytes 8388608 | tf_op jit(solution)/shard_map/first_last/pallas_call | solution.py:347
  27.0 2.5 %collective-permute-start.2 = (bf16[2,4,128,256]{3,2,1,0:T(8,128)(2,1)S(1)}, bf16[2,4,128,256]{3,2,1,0:T(8,128)(2,1)S(1)}, u32[]{:S(2)}, u32[]{:S(2)}) collective-permute-start(bf16[2,4,128,256]{3,2,1,0:T(8,128)(2,1)S(1)} %get-tuple-element.28.refs_1_.refs_4_), channel_id=1, source_target_pairs={{0,8},{8,16},{16,24},{1,9},{9,17},{17,25},{2,10},{10,18},{18,26},{... | collective-permute-start | bytes 1572872 | tf_op jit(solution)/shard_map/ppermute | solution.py:278
  29.5 0.0 collective-permute-done.4.refs_1_
  29.5 0.0 collective-permute-done.5.refs_2_
  29.5 0.0 copy-start.1
  29.6 0.0 copy-start.3
  29.6 0.0 copy-start.6
  29.6 0.0 copy-start.7
  29.6 4.3 %first_head.1 = (bf16[2,4,128,256]{3,2,1,0:T(8,128)(2,1)S(1)}, f32[32,2,256]{2,1,0:T(2,128)S(1)}, bf16[4,128,256]{2,1,0:T(8,128)(2,1)S(1)}, bf16[4,128,256]{2,1,0:T(8,128)(2,1)S(1)}) custom-call(bf16[2,4,128,256]{3,2,1,0:T(8,128)(2,1)S(1)} %collective-permute-done.3.refs_0_, bf16[2,128,256]{2,1,0:T(8,128)(2,1)S(1)} %collective-permute-done.4.refs_1_, ...), custom_call_target="tpu_custom_call" | custom-call | flops 3623878656 | bytes 8388608 | tf_op jit(solution)/shard_map/first_head/pallas_call | solution.py:354
  33.9 2.7 %collective-permute-start.8 = (bf16[4,128,256]{2,1,0:T(8,128)(2,1)S(1)}, bf16[4,128,256]{2,1,0:T(8,128)(2,1)S(1)}, u32[]{:S(2)}, u32[]{:S(2)}) collective-permute-start(bf16[4,128,256]{2,1,0:T(8,128)(2,1)S(1)} %get-tuple-element.38), channel_id=1, source_target_pairs={{0,1},{1,0},{2,3},{3,2},{4,5},{5,4},{6,7},{7,6},{8,9},{9,8},{10,11... | collective-permute-start | bytes 786440 | tf_op jit(solution)/shard_map/ppermute | solution.py:285
  36.6 0.7 collective-permute-start.9
  37.3 13.3 %all_to_all.16.refs_1_.refs_4_.refs_7_ = f32[32,2,256]{2,1,0:T(2,128)S(1)} all-to-all(f32[32,2,256]{2,1,0:T(2,128)S(1)} %get-tuple-element.34), channel_id=1, replica_groups=mesh['tm'=4,'tile'=8] {'tm','tile'}, dimensions={0} | all-to-all | bytes 131072 | tf_op jit(solution)/shard_map/all_to_all | solution.py:301
  50.6 0.2 collective-permute-start.6
  50.8 0.8 %collective-permute-start.7 = (bf16[2,128,256]{2,1,0:T(8,128)(2,1)S(1)}, bf16[2,128,256]{2,1,0:T(8,128)(2,1)S(1)}, u32[]{:S(2)}, u32[]{:S(2)}) collective-permute-start(bf16[2,128,256]{2,1,0:T(8,128)(2,1)S(1)} %get-tuple-element.36), channel_id=1, source_target_pairs={{1,2},{2,1},{3,4},{4,3},{5,6},{6,5},{9,10},{10,9},{11,12},{12,11},... | collective-permute-start | bytes 393224 | tf_op jit(solution)/shard_map/ppermute | solution.py:286
  51.6 0.0 collective-permute-done.9.refs_3_.refs_6_
  51.7 7.1 %second_last.1 = (bf16[4,4,128,256]{3,2,1,0:T(8,128)(2,1)}, bf16[8,16,128]{2,1,0:T(8,128)(2,1)S(1)}) custom-call(bf16[2,4,128,256]{3,2,1,0:T(8,128)(2,1)S(1)} %get-tuple-element.37.refs_0_.refs_3_, bf16[2,4,128,256]{3,2,1,0:T(8,128)(2,1)S(1)} %get-tuple-element.28.refs_1_.refs_4_, bf16[4,128,256]{2,1,0:T(8,128)(2,1)S(1)} %collective-permute-done.8.refs_2_.refs_5_, ...), custom_call_target="tpu_custom_call" | custom-call | flops 3623878656 | bytes 8388608 | tf_op jit(solution)/shard_map/second_last/pallas_call | solution.py:375
  58.8 0.0 collective-permute-done.6.refs_1_
  58.8 7.0 %second_head.1 = (bf16[4,4,128,256]{3,2,1,0:T(8,128)(2,1)}, bf16[8,32,128]{2,1,0:T(8,128)(2,1)S(1)}) custom-call(bf16[2,4,128,256]{3,2,1,0:T(8,128)(2,1)S(1)} %collective-permute-done.2.refs_0_, bf16[2,128,256]{2,1,0:T(8,128)(2,1)S(1)} %collective-permute-done.6.refs_1_, ...), custom_call_target="tpu_custom_call", output_to_operand_aliasing={{0}: (14, {})} | custom-call | flops 3623878656 | bytes 8388608 | tf_op jit(solution)/shard_map/second_head/pallas_call | solution.py:383
  65.8 10.3 %all_to_all.17.received = bf16[8,32,128]{2,1,0:T(8,128)(2,1)S(1)} all-to-all(bf16[8,32,128]{2,1,0:T(8,128)(2,1)S(1)} %get-tuple-element.43), channel_id=1, replica_groups=mesh['tm'=4,'tile'=8] {'tile'}, dimensions={0} | all-to-all | bytes 131072 | tf_op jit(solution)/shard_map/all_to_all | solution.py:390
  76.1 0.8 unpack.1
  (15 shorter events, 0.1 us)
Async XLA Ops:
  0.6 22.1 %copy-start = (bf16[3,3,3,256,256]{4,3,2,1,0:T(8,128)(2,1)S(1)}, bf16[3,3,3,256,256]{4,3,2,1,0:T(8,128)(2,1)}, u32[]{:S(2)}) copy-start(bf16[3,3,3,256,256]{4,3,2,1,0:T(8,128)(2,1)} %refs_10_.2) | copy-start | bytes 10616836
  0.6 1.4 %copy-start.2 = (bf16[4,4,128,256]{3,2,1,0:T(8,128)(2,1)S(1)}, bf16[4,4,128,256]{3,2,1,0:T(8,128)(2,1)}, u32[]{:S(2)}) copy-start(bf16[4,4,128,256]{3,2,1,0:T(8,128)(2,1)} %refs_11_.1) | copy-start | bytes 3145732
  2.0 20.7 %copy-start.4 = (f32[256]{0:T(256)S(1)}, f32[256]{0:T(256)}, u32[]{:S(2)}) copy-start(f32[256]{0:T(256)} %param.9) | copy-start | bytes 3076
  2.0 20.8 %copy-start.5 = (f32[256]{0:T(256)S(1)}, f32[256]{0:T(256)}, u32[]{:S(2)}) copy-start(f32[256]{0:T(256)} %param.10) | copy-start | bytes 3076
  2.3 19.5 %collective-permute-start.3 = (bf16[2,4,128,256]{3,2,1,0:T(8,128)(2,1)S(1)}, bf16[2,4,128,256]{3,2,1,0:T(8,128)(2,1)S(1)}, u32[]{:S(2)}, u32[]{:S(2)}) collective-permute-start(bf16[2,4,128,256]{3,2,1,0:T(8,128)(2,1)S(1)} %get-tuple-element.24.refs_1_.refs_4_), channel_id=1, source_target_pairs={{0,8},{8,16},{16,24},{1,9},{9,17},{17,25},{2,10},{10,18},{18,26},{... | collective-permute-start | bytes 1572872 | tf_op jit(solution)/shard_map/ppermute | solution.py:278
  7.2 15.5 %collective-permute-start = (bf16[4,128,256]{2,1,0:T(8,128)(2,1)S(1)}, bf16[4,128,256]{2,1,0:T(8,128)(2,1)S(1)}, u32[]{:S(2)}, u32[]{:S(2)}) collective-permute-start(bf16[4,128,256]{2,1,0:T(8,128)(2,1)S(1)} %get-tuple-element.25), channel_id=1, source_target_pairs={{0,1},{1,0},{2,3},{3,2},{4,5},{5,4},{6,7},{7,6},{8,9},{9,8},{10,11... | collective-permute-start | bytes 786440 | tf_op jit(solution)/shard_map/ppermute | solution.py:285
  7.3 15.4 %collective-permute-start.1 = (bf16[4,128,256]{2,1,0:T(8,128)(2,1)S(1)}, bf16[4,128,256]{2,1,0:T(8,128)(2,1)S(1)}, u32[]{:S(2)}, u32[]{:S(2)}) collective-permute-start(bf16[4,128,256]{2,1,0:T(8,128)(2,1)S(1)} %get-tuple-element.26), channel_id=1, source_target_pairs={{1,2},{2,1},{3,4},{4,3},{5,6},{6,5},{9,10},{10,9},{11,12},{12,11},... | collective-permute-start | bytes 786440 | tf_op jit(solution)/shard_map/ppermute | solution.py:286
  21.9 7.6 %collective-permute-start.4 = (bf16[2,128,256]{2,1,0:T(8,128)(2,1)S(1)}, bf16[2,128,256]{2,1,0:T(8,128)(2,1)S(1)}, u32[]{:S(2)}, u32[]{:S(2)}) collective-permute-start(bf16[2,128,256]{2,1,0:T(8,128)(2,1)S(1)} %get-tuple-element.29), channel_id=1, source_target_pairs={{0,1},{1,0},{2,3},{3,2},{4,5},{5,4},{6,7},{7,6},{8,9},{9,8},{10,11... | collective-permute-start | bytes 393224 | tf_op jit(solution)/shard_map/ppermute | solution.py:285
  22.1 7.5 %collective-permute-start.5 = (bf16[2,128,256]{2,1,0:T(8,128)(2,1)S(1)}, bf16[2,128,256]{2,1,0:T(8,128)(2,1)S(1)}, u32[]{:S(2)}, u32[]{:S(2)}) collective-permute-start(bf16[2,128,256]{2,1,0:T(8,128)(2,1)S(1)} %get-tuple-element.30), channel_id=1, source_target_pairs={{1,2},{2,1},{3,4},{4,3},{5,6},{6,5},{9,10},{10,9},{11,12},{12,11},... | collective-permute-start | bytes 393224 | tf_op jit(solution)/shard_map/ppermute | solution.py:286
  27.0 23.6 %collective-permute-start.2 = (bf16[2,4,128,256]{3,2,1,0:T(8,128)(2,1)S(1)}, bf16[2,4,128,256]{3,2,1,0:T(8,128)(2,1)S(1)}, u32[]{:S(2)}, u32[]{:S(2)}) collective-permute-start(bf16[2,4,128,256]{3,2,1,0:T(8,128)(2,1)S(1)} %get-tuple-element.28.refs_1_.refs_4_), channel_id=1, source_target_pairs={{0,8},{8,16},{16,24},{1,9},{9,17},{17,25},{2,10},{10,18},{18,26},{... | collective-permute-start | bytes 1572872 | tf_op jit(solution)/shard_map/ppermute | solution.py:278
  29.5 22.1 %copy-start.1 = (bf16[3,3,3,256,256]{4,3,2,1,0:T(8,128)(2,1)S(1)}, bf16[3,3,3,256,256]{4,3,2,1,0:T(8,128)(2,1)}, u32[]{:S(2)}) copy-start(bf16[3,3,3,256,256]{4,3,2,1,0:T(8,128)(2,1)} %refs_10_.3) | copy-start | bytes 10616836
  29.6 22.1 %copy-start.3 = (bf16[256,16]{0,1:T(8,128)(2,1)S(1)}, bf16[256,16]{0,1:T(8,128)(2,1)}, u32[]{:S(2)}) copy-start(bf16[256,16]{0,1:T(8,128)(2,1)} %param.15) | copy-start | bytes 24580
  29.6 22.1 %copy-start.6 = (f32[256]{0:T(256)S(1)}, f32[256]{0:T(256)}, u32[]{:S(2)}) copy-start(f32[256]{0:T(256)} %param.12) | copy-start | bytes 3076
  29.6 22.1 %copy-start.7 = (f32[256]{0:T(256)S(1)}, f32[256]{0:T(256)}, u32[]{:S(2)}) copy-start(f32[256]{0:T(256)} %param.13) | copy-start | bytes 3076
  33.9 17.8 %collective-permute-start.8 = (bf16[4,128,256]{2,1,0:T(8,128)(2,1)S(1)}, bf16[4,128,256]{2,1,0:T(8,128)(2,1)S(1)}, u32[]{:S(2)}, u32[]{:S(2)}) collective-permute-start(bf16[4,128,256]{2,1,0:T(8,128)(2,1)S(1)} %get-tuple-element.38), channel_id=1, source_target_pairs={{0,1},{1,0},{2,3},{3,2},{4,5},{5,4},{6,7},{7,6},{8,9},{9,8},{10,11... | collective-permute-start | bytes 786440 | tf_op jit(solution)/shard_map/ppermute | solution.py:285
  36.6 15.1 %collective-permute-start.9 = (bf16[4,128,256]{2,1,0:T(8,128)(2,1)S(1)}, bf16[4,128,256]{2,1,0:T(8,128)(2,1)S(1)}, u32[]{:S(2)}, u32[]{:S(2)}) collective-permute-start(bf16[4,128,256]{2,1,0:T(8,128)(2,1)S(1)} %get-tuple-element.39), channel_id=1, source_target_pairs={{1,2},{2,1},{3,4},{4,3},{5,6},{6,5},{9,10},{10,9},{11,12},{12,11},... | collective-permute-start | bytes 786440 | tf_op jit(solution)/shard_map/ppermute | solution.py:286
  50.6 8.2 %collective-permute-start.6 = (bf16[2,128,256]{2,1,0:T(8,128)(2,1)S(1)}, bf16[2,128,256]{2,1,0:T(8,128)(2,1)S(1)}, u32[]{:S(2)}, u32[]{:S(2)}) collective-permute-start(bf16[2,128,256]{2,1,0:T(8,128)(2,1)S(1)} %get-tuple-element.35), channel_id=1, source_target_pairs={{0,1},{1,0},{2,3},{3,2},{4,5},{5,4},{6,7},{7,6},{8,9},{9,8},{10,11... | collective-permute-start | bytes 393224 | tf_op jit(solution)/shard_map/ppermute | solution.py:285
  50.8 8.0 %collective-permute-start.7 = (bf16[2,128,256]{2,1,0:T(8,128)(2,1)S(1)}, bf16[2,128,256]{2,1,0:T(8,128)(2,1)S(1)}, u32[]{:S(2)}, u32[]{:S(2)}) collective-permute-start(bf16[2,128,256]{2,1,0:T(8,128)(2,1)S(1)} %get-tuple-element.36), channel_id=1, source_target_pairs={{1,2},{2,1},{3,4},{4,3},{5,6},{6,5},{9,10},{10,9},{11,12},{12,11},... | collective-permute-start | bytes 393224 | tf_op jit(solution)/shard_map/ppermute | solution.py:286

commit v3 on v1

v3 whole, which is shorter than its diff:
```python
import functools

import jax
import jax.numpy as jnp
from jax import lax
from jax.experimental import pallas as pl
from jax.experimental.pallas import tpu as pltpu
from jax.sharding import PartitionSpec as P


GROUPS = 32
ALL = ("tm", "tile")
VMEM = pl.BlockSpec(memory_space=pltpu.VMEM)
HBM = pl.BlockSpec(memory_space=pltpu.HBM)
LANES = 128


def params(mib):
    return pltpu.CompilerParams(vmem_limit_bytes=mib << 20)


def row_totals(value):
    folded = value.reshape(-1, 8, value.shape[-1])
    return jnp.sum(folded, axis=0)


def put_stats(out_ref, sums, squares):
    pair = jnp.concatenate(
        [jnp.sum(sums, axis=0, keepdims=True), jnp.sum(squares, axis=0, keepdims=True)], axis=0
    )
    out_ref[...] = jnp.broadcast_to(pair[None], out_ref.shape)


def sides(height):
    even = lax.axis_index("tile") % 2 == 0
    return jnp.where(even, height - 1, 0), jnp.where(even, 0, height - 1)


def stats_kernel(frames_ref, out_ref, head_ref, last_ref):
    depth, height, _, channels = frames_ref.shape

    def step(t, carry):
        sums, squares = carry
        for h in range(height):
            value = frames_ref[t, h].astype(jnp.float32)
            sums = sums + row_totals(value)
            squares = squares + row_totals(value * value)
        return sums, squares

    zero = jnp.zeros((8, channels), jnp.float32)
    sums, squares = lax.fori_loop(0, depth, step, (zero, zero))
    put_stats(out_ref, sums, squares)
    head_ref[...] = frames_ref[: depth - 2]
    last_ref[...] = frames_ref[depth - 2 :]


def pick_kernel(count, *refs):
    cell_refs, (near_ref, far_ref) = refs[:count], refs[-2:]
    near, far = sides(cell_refs[0].shape[1])
    t = 0
    for ref in cell_refs:
        for frame in range(ref.shape[0]):
            near_ref[t] = ref[frame, near]
            far_ref[t] = ref[frame, far]
            t += 1


def group_sum(value, size):
    channels = value.shape[1]
    lane = lax.broadcasted_iota(jnp.int32, value.shape, 1)
    step = 1
    while step < size:
        ahead = pltpu.roll(value, channels - step, 1)
        behind = pltpu.roll(value, step, 1)
        value = value + jnp.where((lane // step) % 2 == 0, ahead, behind)
        step *= 2
    return value


def scale_of(stats_ref, gain_ref, bias_ref, members):
    channels = stats_ref.shape[2]
    totals = jnp.sum(stats_ref[...], axis=0)
    totals = jnp.concatenate([totals, jnp.zeros((6, channels), jnp.float32)], axis=0)
    totals = group_sum(totals, channels // GROUPS)
    average = totals[0:1] / members
    spread = totals[1:2] / members - average * average
    factor = lax.rsqrt(spread + 1e-06) * gain_ref[...]
    return factor, bias_ref[...] - average * factor


def silu(value):
    return value * (0.5 * jnp.tanh(0.5 * value) + 0.5)


def activate(value, scale, keep):
    factor, offset = scale
    active = silu(value.astype(jnp.float32) * factor + offset)
    if keep is not None:
        active = active * keep
    return active.astype(jnp.bfloat16)


def has_past():
    return (lax.axis_index("tm") > 0).astype(jnp.float32)


def convolve(piece, weight_ref, columns):
    totals = []
    for c in range(3):
        total = None
        for a in range(3):
            for b in range(3):
                part = jnp.dot(piece(a, b), weight_ref[a, b, c], preferred_element_type=jnp.float32)
                total = part if total is None else total + part
        totals.append(total)
    rows = totals[0].shape[0]
    column = lax.broadcasted_iota(jnp.int32, totals[0].shape, 0) % columns
    left = jnp.where(column == 0, 0.0, pltpu.roll(totals[0], 1, 0))
    right = jnp.where(column == columns - 1, 0.0, pltpu.roll(totals[2], rows - 1, 0))
    return totals[1] + left + right


def steps(count):
    return [(t, min(2, count - t)) for t in range(0, count, 2)]


def inner(members, past, head, last, stats, gain, bias, weight, active_ref, finish):
    height, columns, channels = active_ref.shape[1:]
    scale = scale_of(stats, gain, bias, members)
    first = has_past()
    found = [(ref.at[t], ref is past) for ref in (past, head, last) for t in range(ref.shape[0])]
    done = 0
    for t, count in steps(len(found) - 2):
        while done < t + count + 2:
            cells, is_past = found[done]
            for h in range(height):
                active_ref[done, h] = activate(cells[h], scale, first if is_past else None)
            done += 1

        def piece(a, b, t=t, count=count):
            cells = active_ref[t + a : t + a + count, b : b + height - 2]
            return cells.reshape(count * (height - 2) * columns, channels)

        finish(t, count, convolve(piece, weight, columns))


def inner_first(members, past, head, last, stats, gain, bias, weight,
                active_ref, inner_ref, totals_ref):
    totals_ref[...] = jnp.zeros_like(totals_ref)

    def finish(t, count, total):
        hidden = total.astype(jnp.bfloat16)
        inner_ref[t : t + count] = hidden.reshape(count, *inner_ref.shape[1:])
        wide = hidden.astype(jnp.float32)
        totals_ref[0] += row_totals(wide)
        totals_ref[1] += row_totals(wide * wide)

    inner(members, past, head, last, stats, gain, bias, weight, active_ref, finish)


def inner_second(members, past, head, last, stats, gain, bias, weight, frames,
                 active_ref, inner_ref, cells_ref, sem):
    height = frames.shape[1]
    loads = pltpu.make_async_copy(frames.at[:, 1 : height - 1], cells_ref, sem)
    loads.start()
    loads.wait()

    def finish(t, count, total):
        cells = cells_ref[t : t + count].astype(jnp.float32).reshape(total.shape)
        inner_ref[t : t + count] = (cells + total).astype(jnp.bfloat16).reshape(
            count, *inner_ref.shape[1:]
        )

    inner(members, past, head, last, stats, gain, bias, weight, active_ref, finish)


def outer(members, begin, frames, near, far, active, stats, gain, bias, weight, halo_ref, finish):
    height, columns = active.shape[1:3]
    scale = scale_of(stats, gain, bias, members)
    index, count = lax.axis_index("tile"), lax.axis_size("tile")
    even = index % 2 == 0
    first = has_past()
    above = (index > 0).astype(jnp.float32)
    below = (index < count - 1).astype(jnp.float32)
    for t in range(frames + 2):
        e = begin + t
        rows = near[e], far[e]
        top, bottom = (above * first, below * first) if e < 2 else (above, below)
        halo_ref[t, 0] = activate(jnp.where(even, rows[1], rows[0]), scale, top)
        halo_ref[t, 1] = activate(jnp.where(even, rows[0], rows[1]), scale, bottom)

    def row(t, h):
        if h == 0:
            return halo_ref[t, 0]
        if h == height + 1:
            return halo_ref[t, 1]
        return active[begin + t, h - 1]

    for t, count in steps(frames):

        def piece(a, b, t=t, count=count):
            cells = [
                row(t + a + f, h + b) for f in range(count) for h in (0, height - 1)
            ]
            return jnp.concatenate(cells, axis=0)

        finish(t, count, convolve(piece, weight, columns))


def outer_first(members, begin, frames, near, far, active, stats, gain, bias, weight, inside,
                before, cells_ref, totals_ref, halo_ref):
    height, columns, channels = cells_ref.shape[1:]
    sums, squares = [before[0]], [before[1]]

    def finish(t, count, total):
        hidden = total.astype(jnp.bfloat16)
        rows = hidden.reshape(count, 2, columns, channels)
        for f in range(count):
            cells_ref[t + f, 0] = rows[f, 0]
            cells_ref[t + f, height - 1] = rows[f, 1]
        wide = hidden.astype(jnp.float32)
        sums.append(row_totals(wide))
        squares.append(row_totals(wide * wide))

    cells_ref[:, 1 : height - 1] = inside[begin : begin + frames]
    outer(members, begin, frames, near, far, active, stats, gain, bias, weight, halo_ref, finish)
    if begin == 0:
        put_stats(totals_ref, sum(sums), sum(squares))
    else:
        totals_ref[0] = sum(sums)
        totals_ref[1] = sum(squares)


def outer_second(members, near, far, active, stats, gain, bias, weight, inside, frames, latent,
                 features_hbm, patches_ref, halo_ref, cells_ref, latents_ref, packed_ref, sem):
    depth, height, columns, channels = cells_ref.shape
    loads = [
        pltpu.make_async_copy(frames.at[:, h : h + 1], cells_ref.at[:, h : h + 1], sem.at[n])
        for n, h in enumerate((0, height - 1))
    ]
    for load in loads:
        load.start()
    width = LANES // 8
    parts, rows = packed_ref.shape[:2]
    pairs = height // 2
    blocks = rows // (depth * pairs)
    lane = lax.broadcasted_iota(jnp.int32, (columns // 4, LANES), 1) // width
    spread = lax.broadcasted_iota(jnp.int32, (width, LANES), 0) == (
        lax.broadcasted_iota(jnp.int32, (width, LANES), 1) % width
    )
    wide_latent = lax.dot_general(
        latent[...], spread.astype(jnp.bfloat16), (((0,), (0,)), ((), ())),
        preferred_element_type=jnp.float32,
    ).astype(jnp.bfloat16)
    for load in loads:
        load.wait()
    cells_ref[:, 1 : height - 1] = inside[...]

    def finish(t, count, total):
        branch = total.reshape(count, 2, columns, channels)
        for f in range(count):
            for n, h in enumerate((0, height - 1)):
                cells = cells_ref[t + f, h].astype(jnp.float32)
                cells_ref[t + f, h] = (cells + branch[f, n]).astype(jnp.bfloat16)

    outer(members, 0, depth, near, far, active, stats, gain, bias, weight, halo_ref, finish)
    store = pltpu.make_async_copy(cells_ref, features_hbm, sem.at[2])
    store.start()

    def step(t, carry):
        latents_ref[...] = (
            jnp.dot(
                cells_ref[t].reshape(height * columns, channels), wide_latent,
                preferred_element_type=jnp.float32,
            )
            .astype(jnp.bfloat16)
            .astype(jnp.float32)
        )
        for i in range(pairs):
            mixed = None
            for cell in range(8):
                j, p, q = cell // 4, cell // 2 % 2, cell % 2
                start = (2 * i + p) * columns + 2 * j + q
                value = latents_ref[pl.ds(start, columns // 4, stride=4), :]
                mixed = value if mixed is None else jnp.where(lane == cell, value, mixed)
            for d in range(parts):
                packed_ref[d, pl.ds(t * blocks * pairs + i, blocks, stride=pairs), :] = mixed[
                    d * blocks : (d + 1) * blocks
                ]
        return carry

    lax.fori_loop(0, depth, step, 0)
    patches_ref[...] = packed_ref[...].astype(jnp.bfloat16)
    store.wait()


def unpack_kernel(blocks, pairs, received, tokens_ref, flat_ref, mixed_ref):
    parts, rows, lanes = received.shape
    flat_ref[...] = received[...].astype(jnp.float32).reshape(parts * rows, lanes)
    depth = rows // (blocks * pairs)
    for t in range(depth):
        for block in range(blocks):
            for i in range(pairs):
                start = (t * blocks + block) * pairs + i
                mixed_ref[t * blocks + block, pl.ds(i, parts, stride=pairs), :] = flat_ref[
                    pl.ds(start, parts, stride=rows), :
                ]
            tokens_ref[t, :, block * lanes : (block + 1) * lanes] = mixed_ref[
                t * blocks + block
            ].astype(jnp.bfloat16)


def sent_ahead(last):
    pairs = [(i, i + 1) for i in range(lax.axis_size("tm") - 1)]
    return lax.ppermute(last, "tm", pairs)


def sent_sideways(near, far):
    count = lax.axis_size("tile")
    near_pairs = [(i, i ^ 1) for i in range(count) if i ^ 1 < count]
    far_pairs = [pair for i in range(1, count - 1, 2) for pair in ((i, i + 1), (i + 1, i))]
    near = lax.ppermute(near, "tile", near_pairs)
    far = lax.ppermute(far, "tile", far_pairs)
    return near, far


def pick(cells, *after):
    rows = sum(piece.shape[0] for piece in cells)
    rows = jax.ShapeDtypeStruct((rows, *cells[0].shape[2:]), jnp.bfloat16)
    return pl.pallas_call(
        functools.partial(pick_kernel, len(cells)), out_shape=(rows, rows),
        in_specs=[VMEM] * len(cells) + [pl.BlockSpec(memory_space=pl.ANY)] * len(after),
        out_specs=(VMEM, VMEM), compiler_params=params(8), name="pick",
    )(*cells, *after)


def exchange(stats):
    return lax.all_to_all(stats, ALL, split_axis=0, concat_axis=0, tiled=True)


def body(frames, first_gain, first_bias, first_weight, second_gain, second_bias, second_weight,
         latent_weight):
    depth, height, columns, channels = frames.shape
    parts = lax.axis_size("tile")
    devices = lax.axis_size("tm") * parts
    members = float(devices * depth * height * columns * (channels // GROUPS))
    latent_width = latent_weight.shape[1]
    pairs = height // 2
    blocks = columns // 2 * 4 * latent_width // parts // LANES
    rows = depth * blocks * pairs
    stats_shape = jax.ShapeDtypeStruct((devices, 2, channels), jnp.float32)
    cells_shape = jax.ShapeDtypeStruct(frames.shape, jnp.bfloat16)
    last_shape = jax.ShapeDtypeStruct((2, *frames.shape[1:]), jnp.bfloat16)
    head_shape = jax.ShapeDtypeStruct((depth - 2, *frames.shape[1:]), jnp.bfloat16)

    active_shape = jax.ShapeDtypeStruct((depth + 2, height, columns, channels), jnp.bfloat16)
    inner_shape = jax.ShapeDtypeStruct((depth, height - 2, columns, channels), jnp.bfloat16)
    totals_shape = jax.ShapeDtypeStruct((2, 8, channels), jnp.float32)

    def halo(count):
        return pltpu.VMEM((count + 2, 2, columns, channels), jnp.bfloat16)

    def call(kernel, outs, inputs, count, scratch=(), hbm=(), out_specs=None):
        flops = 27 * count * height * columns * channels * channels
        return pl.pallas_call(
            kernel, out_shape=outs, in_specs=[HBM if i in hbm else VMEM for i in range(len(inputs))],
            out_specs=out_specs or (VMEM,) * len(outs), scratch_shapes=list(scratch),
            compiler_params=params(24),
            cost_estimate=pl.CostEstimate(flops=flops, bytes_accessed=8 << 20, transcendentals=0),
        )(*inputs)

    def gather(head, last, stats):
        past = sent_ahead(last)
        stats = exchange(stats)
        near, far = sent_sideways(*pick((past, head, last), stats))
        return past, near, far, stats

    cells = pltpu.with_memory_space_constraint(frames, pltpu.HBM)
    stats, head, last = call(stats_kernel, (stats_shape, head_shape, last_shape), (frames,), 2)
    past, near, far, stats = gather(head, last, stats)
    norm = (stats, first_gain[None], first_bias[None], first_weight)
    active, inside, totals = call(
        functools.partial(inner_first, members),
        (active_shape, inner_shape, totals_shape), (past, head, last, *norm), depth,
    )
    around = (near, far, active, *norm, inside)
    last, totals = call(
        functools.partial(outer_first, members, depth - 2, 2),
        (last_shape, totals_shape), (*around, totals), 2, (halo(2),),
    )
    head, stats = call(
        functools.partial(outer_first, members, 0, depth - 2),
        (head_shape, stats_shape), (*around, totals), depth - 2, (halo(depth - 2),),
    )
    past, near, far, stats = gather(head, last, stats)
    norm = (stats, second_gain[None], second_bias[None], second_weight)
    active, inside = call(
        functools.partial(inner_second, members),
        (active_shape, inner_shape), (past, head, last, *norm, cells), depth,
        (pltpu.VMEM(inner_shape.shape, jnp.bfloat16), pltpu.SemaphoreType.DMA(())), (7,),
    )
    features, patches = call(
        functools.partial(outer_second, members),
        (cells_shape, jax.ShapeDtypeStruct((parts, rows, LANES), jnp.bfloat16)),
        (near, far, active, *norm, inside, cells, latent_weight.T), depth,
        (halo(depth), pltpu.VMEM(frames.shape, jnp.bfloat16),
         pltpu.VMEM((height * columns, LANES), jnp.float32),
         pltpu.VMEM((parts, rows, LANES), jnp.float32), pltpu.SemaphoreType.DMA((3,))),
        (8,), (HBM, VMEM),
    )
    received = lax.all_to_all(patches, "tile", split_axis=0, concat_axis=0, tiled=True)
    tokens = pl.pallas_call(
        functools.partial(unpack_kernel, blocks, pairs),
        out_shape=jax.ShapeDtypeStruct((depth, parts * pairs, blocks * LANES), jnp.bfloat16),
        in_specs=[VMEM], out_specs=VMEM,
        scratch_shapes=[pltpu.VMEM((parts * rows, LANES), jnp.float32),
                        pltpu.VMEM((depth * blocks, parts * pairs, LANES), jnp.float32)],
        compiler_params=params(16), name="unpack",
    )(received)
    return features, tokens


def solution(mesh):
    in_specs = (P("tm", "tile", None, None), P(), P(), P(), P(), P(), P(), P())
    out_specs = (P("tm", "tile", None, None), P("tm", None, "tile"))
    return jax.shard_map(body, mesh=mesh, in_specs=in_specs, out_specs=out_specs, check_vma=False)
```

time: 82.3 us -> 76.4 us (0.928)
  waiting for transfers between devices: 4.88 us -> 0.02 us
  blocking collectives: 38.6 us -> 42.3 us
  starting transfers between devices: 13 us -> 10.2 us
  Pallas kernels: 23.3 us -> 21.3 us
    ppermute x2, waiting for transfers between devices: 4.2 us -> 0.01 us  [sent_ahead(): return lax.ppermute(last, 'tm', pairs)]
    all_to_all x1, blocking collectives: 8.3 us -> 12.4 us  [body(): lax.all_to_all(patches, 'tile', split_axis=0, concat_axis=0, tiled=True)]
    ppermute x3 -> x2, starting transfers between devices: 3.18 us -> 0.36 us  [sent_sideways(): near = lax.ppermute(near, 'tile', near_pairs)]
    pallas_call x4 -> x6, Pallas kernels: 22.5 us -> 20.5 us  [call(): pl.pallas_call(kernel, out_shape=outs, in_specs=[HBM if i in hbm else VME...]
    ppermute x3 -> x2, starting transfers between devices: 2.01 us -> 1.53 us  [sent_sideways(): far = lax.ppermute(far, 'tile', far_pairs)]
  transfers between devices with their start and end apart: 8 -> 6, of which waited for: 2 -> 0; matrix products, arithmetic and copies ran while one was open for 0% -> 0% of each run, Pallas kernels for 13% -> 15%
where the time goes in v3:
time: 76.4 us; the launch traced here: 76.1 us
  blocking collectives  42.3 us (55%)
  Pallas kernels  21.3 us (28%)
  starting transfers between devices  10.2 us (13%)
  local copies, waits for them, and re-layouts  1.41 us (2%)
  between operations  0.85 us (1%)
    all_to_all x2, blocking collectives, exchange(): return lax.all_to_all(stats, ALL, split_axis=0, concat_axis=0, tiled=True)  29.9 us
    pallas_call x6, Pallas kernels, call(): pl.pallas_call(kernel, out_shape=outs, in_specs=[HBM if i in hbm else VME...  20.5 us
    all_to_all x1, blocking collectives, body(): lax.all_to_all(patches, 'tile', split_axis=0, concat_axis=0, tiled=True)  12.4 us
    ppermute x2, starting transfers between devices, sent_ahead(): return lax.ppermute(last, 'tm', pairs)  8.29 us
  transfers between devices with their start and end apart: 6, of which 0 were waited for; matrix products, arithmetic and copies ran while one was open for 0% of the time, Pallas kernels for 15%

profile of v3, /device:TPU:0, one launch (start us, length us, event | category | flops | bytes accessed | tf_op | source)
XLA Modules:
  0.0 76.1 jit_solution(10308987486806606353)
XLA Ops:
  0.6 0.0 copy-start.2
  0.7 1.4 %copy-done.2 = bf16[4,4,128,256]{3,2,1,0:T(8,128)(2,1)S(1)} copy-done((bf16[4,4,128,256]{3,2,1,0:T(8,128)(2,1)S(1)}, bf16[4,4,128,256]{3,2,1,0:T(8,128)(2,1)}, u32[]{:S(2)}) %copy-start.2) | copy-done | bytes 1048600
  2.0 0.3 shard_map.95
  2.3 4.9 %collective-permute-start = (bf16[2,4,128,256]{3,2,1,0:T(8,128)(2,1)S(1)}, bf16[2,4,128,256]{3,2,1,0:T(8,128)(2,1)S(1)}, u32[]{:S(2)}, u32[]{:S(2)}) collective-permute-start(bf16[2,4,128,256]{3,2,1,0:T(8,128)(2,1)S(1)} %get-tuple-element.20.refs_2_.last), channel_id=1, source_target_pairs={{0,8},{8,16},{16,24},{1,9},{9,17},{17,25},{2,10},{10,18},{18,26},{... | collective-permute-start | bytes 1572872 | tf_op jit(solution)/shard_map/ppermute | solution.py:315
  7.2 13.8 %all_to_all.15.refs_3_.stats = f32[32,2,256]{2,1,0:T(2,128)S(1)} all-to-all(f32[32,2,256]{2,1,0:T(2,128)S(1)} %get-tuple-element.22), channel_id=1, replica_groups=mesh['tm'=4,'tile'=8] {'tm','tile'}, dimensions={0} | all-to-all | bytes 131072 | tf_op jit(solution)/shard_map/all_to_all | solution.py:338
  21.0 0.0 collective-permute-done.refs_0_.past
  21.0 0.1 pick.2
  21.0 0.2 collective-permute-start.1
  21.2 0.7 collective-permute-start.2
  21.9 4.2 %shard_map.96 = (bf16[6,4,128,256]{3,2,1,0:T(8,128)(2,1)S(1)}, bf16[4,2,128,256]{3,2,1,0:T(8,128)(2,1)S(1)}, f32[2,8,256]{2,1,0:T(8,128)S(1)}) custom-call(bf16[2,4,128,256]{3,2,1,0:T(8,128)(2,1)S(1)} %collective-permute-done.refs_0_.past, bf16[2,4,128,256]{3,2,1,0:T(8,128)(2,1)S(1)} %get-tuple-element.21.refs_1_.head, ...), custom_call_target="tpu_custom_call" | custom-call | flops 3623878656 | bytes 8388608 | tf_op jit(solution)/shard_map/pallas_call | solution.py:365
  26.1 0.0 collective-permute-done.1.near
  26.1 0.0 collective-permute-done.2.far
  26.2 2.3 %shard_map.97 = (bf16[2,4,128,256]{3,2,1,0:T(8,128)(2,1)S(1)}, f32[2,8,256]{2,1,0:T(8,128)S(1)}) custom-call(bf16[6,128,256]{2,1,0:T(8,128)(2,1)S(1)} %collective-permute-done.1.near, bf16[6,128,256]{2,1,0:T(8,128)(2,1)S(1)} %collective-permute-done.2.far, bf16[6,4,128,256]{3,2,1,0:T(8,128)(2,1)S(1)} %get-tuple-element.25.active, ...), custom_call_target="tpu_custom_call" | custom-call | flops 1811939328 | bytes 8388608 | tf_op jit(solution)/shard_map/pallas_call | solution.py:365
  28.5 3.4 %collective-permute-start.3 = (bf16[2,4,128,256]{3,2,1,0:T(8,128)(2,1)S(1)}, bf16[2,4,128,256]{3,2,1,0:T(8,128)(2,1)S(1)}, u32[]{:S(2)}, u32[]{:S(2)}) collective-permute-start(bf16[2,4,128,256]{3,2,1,0:T(8,128)(2,1)S(1)} %get-tuple-element.28.refs_2_.last), channel_id=1, source_target_pairs={{0,8},{8,16},{16,24},{1,9},{9,17},{17,25},{2,10},{10,18},{18,26},{... | collective-permute-start | bytes 1572872 | tf_op jit(solution)/shard_map/ppermute | solution.py:315
  31.9 0.0 copy-start.1
  31.9 0.0 copy-start.6
  31.9 0.0 copy-start.7
  31.9 2.4 %shard_map.98 = (bf16[2,4,128,256]{3,2,1,0:T(8,128)(2,1)S(1)}, f32[32,2,256]{2,1,0:T(2,128)S(1)}) custom-call(bf16[6,128,256]{2,1,0:T(8,128)(2,1)S(1)} %collective-permute-done.1.near, bf16[6,128,256]{2,1,0:T(8,128)(2,1)S(1)} %collective-permute-done.2.far, bf16[6,4,128,256]{3,2,1,0:T(8,128)(2,1)S(1)} %get-tuple-element.25.active, ...), custom_call_target="tpu_custom_call" | custom-call | flops 1811939328 | bytes 8388608 | tf_op jit(solution)/shard_map/pallas_call | solution.py:365
  34.3 16.2 %all_to_all.16.refs_3_.stats = f32[32,2,256]{2,1,0:T(2,128)S(1)} all-to-all(f32[32,2,256]{2,1,0:T(2,128)S(1)} %get-tuple-element.31), channel_id=1, replica_groups=mesh['tm'=4,'tile'=8] {'tm','tile'}, dimensions={0} | all-to-all | bytes 131072 | tf_op jit(solution)/shard_map/all_to_all | solution.py:338
  50.4 0.0 collective-permute-done.3.refs_0_.past
  50.5 0.1 pick.3
  50.5 0.2 collective-permute-start.4
  50.7 0.9 %collective-permute-start.5 = (bf16[6,128,256]{2,1,0:T(8,128)(2,1)S(1)}, bf16[6,128,256]{2,1,0:T(8,128)(2,1)S(1)}, u32[]{:S(2)}, u32[]{:S(2)}) collective-permute-start(bf16[6,128,256]{2,1,0:T(8,128)(2,1)S(1)} %get-tuple-element.33), channel_id=1, source_target_pairs={{1,2},{2,1},{3,4},{4,3},{5,6},{6,5},{9,10},{10,9},{11,12},{12,11},... | collective-permute-start | bytes 1179656 | tf_op jit(solution)/shard_map/ppermute | solution.py:323
  51.6 0.0 copy-done.1
  51.6 0.0 copy-done.6
  51.6 0.0 copy-start.3
  51.6 5.2 %shard_map.99 = (bf16[6,4,128,256]{3,2,1,0:T(8,128)(2,1)S(1)}, bf16[4,2,128,256]{3,2,1,0:T(8,128)(2,1)S(1)}) custom-call(bf16[2,4,128,256]{3,2,1,0:T(8,128)(2,1)S(1)} %collective-permute-done.3.refs_0_.past, bf16[2,4,128,256]{3,2,1,0:T(8,128)(2,1)S(1)} %get-tuple-element.30.refs_1_.head, bf16[2,4,128,256]{3,2,1,0:T(8,128)(2,1)S(1)} %get-tuple-element.28.refs_2_.last, ...), custom_call_target="tpu_custom_call" | custom-call | flops 3623878656 | bytes 8388608 | tf_op jit(solution)/shard_map/pallas_call | solution.py:365
  56.8 0.0 collective-permute-done.4.near
  56.8 0.0 collective-permute-done.5.far
  56.9 6.1 %shard_map.100 = (bf16[4,4,128,256]{3,2,1,0:T(8,128)(2,1)}, bf16[8,32,128]{2,1,0:T(8,128)(2,1)S(1)}) custom-call(bf16[6,128,256]{2,1,0:T(8,128)(2,1)S(1)} %collective-permute-done.4.near, bf16[6,128,256]{2,1,0:T(8,128)(2,1)S(1)} %collective-permute-done.5.far, bf16[6,4,128,256]{3,2,1,0:T(8,128)(2,1)S(1)} %get-tuple-element.34.active, ...), custom_call_target="tpu_custom_call" | custom-call | flops 3623878656 | bytes 8388608 | tf_op jit(solution)/shard_map/pallas_call | solution.py:365
  63.0 12.4 %all_to_all.17.received = bf16[8,32,128]{2,1,0:T(8,128)(2,1)S(1)} all-to-all(bf16[8,32,128]{2,1,0:T(8,128)(2,1)S(1)} %get-tuple-element.37), channel_id=1, replica_groups=mesh['tm'=4,'tile'=8] {'tile'}, dimensions={0} | all-to-all | bytes 131072 | tf_op jit(solution)/shard_map/all_to_all | solution.py:411
  75.4 0.8 unpack.1
  (8 shorter events, 0.0 us)
Async XLA Ops:
  0.6 21.3 %copy-start = (bf16[3,3,3,256,256]{4,3,2,1,0:T(8,128)(2,1)S(1)}, bf16[3,3,3,256,256]{4,3,2,1,0:T(8,128)(2,1)}, u32[]{:S(2)}) copy-start(bf16[3,3,3,256,256]{4,3,2,1,0:T(8,128)(2,1)} %weight.7) | copy-start | bytes 10616836
  0.6 1.4 %copy-start.2 = (bf16[4,4,128,256]{3,2,1,0:T(8,128)(2,1)S(1)}, bf16[4,4,128,256]{3,2,1,0:T(8,128)(2,1)}, u32[]{:S(2)}) copy-start(bf16[4,4,128,256]{3,2,1,0:T(8,128)(2,1)} %frames.3) | copy-start | bytes 3145732
  2.0 19.9 %copy-start.4 = (f32[256]{0:T(256)S(1)}, f32[256]{0:T(256)}, u32[]{:S(2)}) copy-start(f32[256]{0:T(256)} %param.9) | copy-start | bytes 3076
  2.0 19.9 %copy-start.5 = (f32[256]{0:T(256)S(1)}, f32[256]{0:T(256)}, u32[]{:S(2)}) copy-start(f32[256]{0:T(256)} %param.10) | copy-start | bytes 3076
  2.3 18.7 %collective-permute-start = (bf16[2,4,128,256]{3,2,1,0:T(8,128)(2,1)S(1)}, bf16[2,4,128,256]{3,2,1,0:T(8,128)(2,1)S(1)}, u32[]{:S(2)}, u32[]{:S(2)}) collective-permute-start(bf16[2,4,128,256]{3,2,1,0:T(8,128)(2,1)S(1)} %get-tuple-element.20.refs_2_.last), channel_id=1, source_target_pairs={{0,8},{8,16},{16,24},{1,9},{9,17},{17,25},{2,10},{10,18},{18,26},{... | collective-permute-start | bytes 1572872 | tf_op jit(solution)/shard_map/ppermute | solution.py:315
  21.0 5.1 %collective-permute-start.1 = (bf16[6,128,256]{2,1,0:T(8,128)(2,1)S(1)}, bf16[6,128,256]{2,1,0:T(8,128)(2,1)S(1)}, u32[]{:S(2)}, u32[]{:S(2)}) collective-permute-start(bf16[6,128,256]{2,1,0:T(8,128)(2,1)S(1)} %get-tuple-element.23), channel_id=1, source_target_pairs={{0,1},{1,0},{2,3},{3,2},{4,5},{5,4},{6,7},{7,6},{8,9},{9,8},{10,11... | collective-permute-start | bytes 1179656 | tf_op jit(solution)/shard_map/ppermute | solution.py:322
  21.2 4.9 %collective-permute-start.2 = (bf16[6,128,256]{2,1,0:T(8,128)(2,1)S(1)}, bf16[6,128,256]{2,1,0:T(8,128)(2,1)S(1)}, u32[]{:S(2)}, u32[]{:S(2)}) collective-permute-start(bf16[6,128,256]{2,1,0:T(8,128)(2,1)S(1)} %get-tuple-element.24), channel_id=1, source_target_pairs={{1,2},{2,1},{3,4},{4,3},{5,6},{6,5},{9,10},{10,9},{11,12},{12,11},... | collective-permute-start | bytes 1179656 | tf_op jit(solution)/shard_map/ppermute | solution.py:323
  28.5 22.0 %collective-permute-start.3 = (bf16[2,4,128,256]{3,2,1,0:T(8,128)(2,1)S(1)}, bf16[2,4,128,256]{3,2,1,0:T(8,128)(2,1)S(1)}, u32[]{:S(2)}, u32[]{:S(2)}) collective-permute-start(bf16[2,4,128,256]{3,2,1,0:T(8,128)(2,1)S(1)} %get-tuple-element.28.refs_2_.last), channel_id=1, source_target_pairs={{0,8},{8,16},{16,24},{1,9},{9,17},{17,25},{2,10},{10,18},{18,26},{... | collective-permute-start | bytes 1572872 | tf_op jit(solution)/shard_map/ppermute | solution.py:315
  31.9 19.7 %copy-start.1 = (bf16[3,3,3,256,256]{4,3,2,1,0:T(8,128)(2,1)S(1)}, bf16[3,3,3,256,256]{4,3,2,1,0:T(8,128)(2,1)}, u32[]{:S(2)}) copy-start(bf16[3,3,3,256,256]{4,3,2,1,0:T(8,128)(2,1)} %weight.9) | copy-start | bytes 10616836
  31.9 19.7 %copy-start.6 = (f32[256]{0:T(256)S(1)}, f32[256]{0:T(256)}, u32[]{:S(2)}) copy-start(f32[256]{0:T(256)} %param.12) | copy-start | bytes 3076
  31.9 19.7 %copy-start.7 = (f32[256]{0:T(256)S(1)}, f32[256]{0:T(256)}, u32[]{:S(2)}) copy-start(f32[256]{0:T(256)} %param.13) | copy-start | bytes 3076
  50.5 6.3 %collective-permute-start.4 = (bf16[6,128,256]{2,1,0:T(8,128)(2,1)S(1)}, bf16[6,128,256]{2,1,0:T(8,128)(2,1)S(1)}, u32[]{:S(2)}, u32[]{:S(2)}) collective-permute-start(bf16[6,128,256]{2,1,0:T(8,128)(2,1)S(1)} %get-tuple-element.32), channel_id=1, source_target_pairs={{0,1},{1,0},{2,3},{3,2},{4,5},{5,4},{6,7},{7,6},{8,9},{9,8},{10,11... | collective-permute-start | bytes 1179656 | tf_op jit(solution)/shard_map/ppermute | solution.py:322
  50.7 6.1 %collective-permute-start.5 = (bf16[6,128,256]{2,1,0:T(8,128)(2,1)S(1)}, bf16[6,128,256]{2,1,0:T(8,128)(2,1)S(1)}, u32[]{:S(2)}, u32[]{:S(2)}) collective-permute-start(bf16[6,128,256]{2,1,0:T(8,128)(2,1)S(1)} %get-tuple-element.33), channel_id=1, source_target_pairs={{1,2},{2,1},{3,4},{4,3},{5,6},{6,5},{9,10},{10,9},{11,12},{12,11},... | collective-permute-start | bytes 1179656 | tf_op jit(solution)/shard_map/ppermute | solution.py:323
  51.6 5.3 %copy-start.3 = (bf16[256,16]{0,1:T(8,128)(2,1)S(1)}, bf16[256,16]{0,1:T(8,128)(2,1)}, u32[]{:S(2)}) copy-start(bf16[256,16]{0,1:T(8,128)(2,1)} %param.15) | copy-start | bytes 24580

commit v4 on v3

--- a/solution.py
+++ b/solution.py
@@ -36,8 +36,9 @@
     return jnp.where(even, height - 1, 0), jnp.where(even, 0, height - 1)
 
 
-def stats_kernel(frames_ref, out_ref, head_ref, last_ref):
+def stats_kernel(frames_ref, out_ref, head_ref, last_ref, near_ref, far_ref):
     depth, height, _, channels = frames_ref.shape
+    near, far = sides(height)
 
     def step(t, carry):
         sums, squares = carry
@@ -45,6 +46,8 @@
             value = frames_ref[t, h].astype(jnp.float32)
             sums = sums + row_totals(value)
             squares = squares + row_totals(value * value)
+        near_ref[t] = frames_ref[t, near]
+        far_ref[t] = frames_ref[t, far]
         return sums, squares
 
     zero = jnp.zeros((8, channels), jnp.float32)
@@ -124,6 +127,84 @@
     return [(t, min(2, count - t)) for t in range(0, count, 2)]
 
 
+def edges(active_ref, scale):
+    index, count = lax.axis_index("tile"), lax.axis_size("tile")
+    height = active_ref.shape[1] - 2
+    even = index % 2 == 0
+    first = (lax.axis_index("tm") > 0).astype(jnp.float32)
+    above = (index > 0).astype(jnp.float32)
+    below = (index < count - 1).astype(jnp.float32)
+    factor, offset = scale
+
+    def put(t, h, value, keep):
+        active = silu(value.astype(jnp.float32) * factor + offset)
+        if keep is not None:
+            active = active * keep
+        active_ref[t, h] = active.astype(jnp.bfloat16)
+
+    def fill(t, source):
+        cells, near, far, is_past = source
+        near, far = near[...], far[...]
+        put(t, 0, jnp.where(even, far, near), above * first if is_past else above)
+        for h in range(height):
+            put(t, h + 1, cells[h], first if is_past else None)
+        put(t, height + 1, jnp.where(even, near, far), below * first if is_past else below)
+
+    return fill
+
+
+def sources(pieces):
+    found = []
+    for cells, near, far, is_past in pieces:
+        row = 0
+        for ref in cells:
+            for t in range(ref.shape[0]):
+                found.append((ref.at[t], near.at[row], far.at[row], is_past))
+                row += 1
+    return found
+
+
+def split(refs, with_past):
+    refs = list(refs)
+    pieces = [((refs.pop(0),), refs.pop(0), refs.pop(0), True)] if with_past else []
+    head, last, near, far = refs[:4]
+    pieces.append(((head, last), near, far, False))
+    return sources(pieces), refs[4:]
+
+
+def first_kernel(members, begin, count, with_past, *refs):
+    found, refs = split(refs, with_past)
+    found = found if with_past else [None, None, *found]
+    stats, gain, bias, weight = refs[:4]
+    active_ref = refs[-1]
+    height, columns, channels = active_ref.shape[1] - 2, *active_ref.shape[2:]
+    fill = edges(active_ref, scale_of(stats, gain, bias, members))
+    if begin == 0:
+        totals, hidden_ref, totals_ref = refs[4:-1]
+        sums, squares = totals[0], totals[1]
+    else:
+        hidden_ref, totals_ref = refs[4:-1]
+        sums = squares = jnp.zeros((8, channels), jnp.float32)
+    for t in range(2):
+        fill(t, found[begin + t])
+    for t in range(count):
+        fill(t + 2, found[begin + t + 2])
+
+        def piece(a, b, t=t):
+            return active_ref[t + a, b : b + height].reshape(height * columns, channels)
+
+        hidden = convolve(piece, weight, columns).astype(jnp.bfloat16)
+        wide = hidden.astype(jnp.float32)
+        sums = sums + row_totals(wide)
+        squares = squares + row_totals(wide * wide)
+        hidden_ref[t] = hidden.reshape(height, columns, channels)
+    if begin == 0:
+        put_stats(totals_ref, sums, squares)
+    else:
+        totals_ref[0] = sums
+        totals_ref[1] = squares
+
+
 def inner(members, past, head, last, stats, gain, bias, weight, active_ref, finish):
     height, columns, channels = active_ref.shape[1:]
     scale = scale_of(stats, gain, bias, members)
@@ -144,29 +225,12 @@
         finish(t, count, convolve(piece, weight, columns))
 
 
-def inner_first(members, past, head, last, stats, gain, bias, weight,
-                active_ref, inner_ref, totals_ref):
-    totals_ref[...] = jnp.zeros_like(totals_ref)
+def inner_second(members, past, head, last, stats, gain, bias, weight, frames,
+                 active_ref, inner_ref):
+    height = frames.shape[1]
 
     def finish(t, count, total):
-        hidden = total.astype(jnp.bfloat16)
-        inner_ref[t : t + count] = hidden.reshape(count, *inner_ref.shape[1:])
-        wide = hidden.astype(jnp.float32)
-        totals_ref[0] += row_totals(wide)
-        totals_ref[1] += row_totals(wide * wide)
-
-    inner(members, past, head, last, stats, gain, bias, weight, active_ref, finish)
-
-
-def inner_second(members, past, head, last, stats, gain, bias, weight, frames,
-                 active_ref, inner_ref, cells_ref, sem):
-    height = frames.shape[1]
-    loads = pltpu.make_async_copy(frames.at[:, 1 : height - 1], cells_ref, sem)
-    loads.start()
-    loads.wait()
-
-    def finish(t, count, total):
-        cells = cells_ref[t : t + count].astype(jnp.float32).reshape(total.shape)
+        cells = frames[t : t + count, 1 : height - 1].astype(jnp.float32).reshape(total.shape)
         inner_ref[t : t + count] = (cells + total).astype(jnp.bfloat16).reshape(
             count, *inner_ref.shape[1:]
         )
@@ -207,39 +271,11 @@
         finish(t, count, convolve(piece, weight, columns))
 
 
-def outer_first(members, begin, frames, near, far, active, stats, gain, bias, weight, inside,
-                before, cells_ref, totals_ref, halo_ref):
-    height, columns, channels = cells_ref.shape[1:]
-    sums, squares = [before[0]], [before[1]]
-
-    def finish(t, count, total):
-        hidden = total.astype(jnp.bfloat16)
-        rows = hidden.reshape(count, 2, columns, channels)
-        for f in range(count):
-            cells_ref[t + f, 0] = rows[f, 0]
-            cells_ref[t + f, height - 1] = rows[f, 1]
-        wide = hidden.astype(jnp.float32)
-        sums.append(row_totals(wide))
-        squares.append(row_totals(wide * wide))
-
-    cells_ref[:, 1 : height - 1] = inside[begin : begin + frames]
-    outer(members, begin, frames, near, far, active, stats, gain, bias, weight, halo_ref, finish)
-    if begin == 0:
-        put_stats(totals_ref, sum(sums), sum(squares))
-    else:
-        totals_ref[0] = sum(sums)
-        totals_ref[1] = sum(squares)
-
-
 def outer_second(members, near, far, active, stats, gain, bias, weight, inside, frames, latent,
                  features_hbm, patches_ref, halo_ref, cells_ref, latents_ref, packed_ref, sem):
     depth, height, columns, channels = cells_ref.shape
-    loads = [
-        pltpu.make_async_copy(frames.at[:, h : h + 1], cells_ref.at[:, h : h + 1], sem.at[n])
-        for n, h in enumerate((0, height - 1))
-    ]
-    for load in loads:
-        load.start()
+    stores = [pltpu.make_async_copy(inside, features_hbm.at[:, 1 : height - 1], sem.at[2])]
+    stores[0].start()
     width = LANES // 8
     parts, rows = packed_ref.shape[:2]
     pairs = height // 2
@@ -252,23 +288,25 @@
         latent[...], spread.astype(jnp.bfloat16), (((0,), (0,)), ((), ())),
         preferred_element_type=jnp.float32,
     ).astype(jnp.bfloat16)
-    for load in loads:
-        load.wait()
     cells_ref[:, 1 : height - 1] = inside[...]
 
     def finish(t, count, total):
         branch = total.reshape(count, 2, columns, channels)
         for f in range(count):
             for n, h in enumerate((0, height - 1)):
-                cells = cells_ref[t + f, h].astype(jnp.float32)
+                cells = frames[t + f, h].astype(jnp.float32)
                 cells_ref[t + f, h] = (cells + branch[f, n]).astype(jnp.bfloat16)
 
     outer(members, 0, depth, near, far, active, stats, gain, bias, weight, halo_ref, finish)
-    store = pltpu.make_async_copy(cells_ref, features_hbm, sem.at[2])
-    store.start()
-
-    def step(t, carry):
-        latents_ref[...] = (
+    for n, h in enumerate((0, height - 1)):
+        stores.append(
+            pltpu.make_async_copy(
+                cells_ref.at[:, h : h + 1], features_hbm.at[:, h : h + 1], sem.at[n]
+            )
+        )
+        stores[-1].start()
+    for t in range(depth):
+        latents_ref[t] = (
             jnp.dot(
                 cells_ref[t].reshape(height * columns, channels), wide_latent,
                 preferred_element_type=jnp.float32,
@@ -276,22 +314,21 @@
             .astype(jnp.bfloat16)
             .astype(jnp.float32)
         )
+    for t in range(depth):
         for i in range(pairs):
             mixed = None
             for cell in range(8):
                 j, p, q = cell // 4, cell // 2 % 2, cell % 2
                 start = (2 * i + p) * columns + 2 * j + q
-                value = latents_ref[pl.ds(start, columns // 4, stride=4), :]
+                value = latents_ref[t, pl.ds(start, columns // 4, stride=4), :]
                 mixed = value if mixed is None else jnp.where(lane == cell, value, mixed)
             for d in range(parts):
                 packed_ref[d, pl.ds(t * blocks * pairs + i, blocks, stride=pairs), :] = mixed[
                     d * blocks : (d + 1) * blocks
                 ]
-        return carry
-
-    lax.fori_loop(0, depth, step, 0)
     patches_ref[...] = packed_ref[...].astype(jnp.bfloat16)
-    store.wait()
+    for store in stores:
+        store.wait()
 
 
 def unpack_kernel(blocks, pairs, received, tokens_ref, flat_ref, mixed_ref):
@@ -369,44 +406,47 @@
             cost_estimate=pl.CostEstimate(flops=flops, bytes_accessed=8 << 20, transcendentals=0),
         )(*inputs)
 
-    def gather(head, last, stats):
-        past = sent_ahead(last)
-        stats = exchange(stats)
-        near, far = sent_sideways(*pick((past, head, last), stats))
-        return past, near, far, stats
-
-    cells = pltpu.with_memory_space_constraint(frames, pltpu.HBM)
-    stats, head, last = call(stats_kernel, (stats_shape, head_shape, last_shape), (frames,), 2)
-    past, near, far, stats = gather(head, last, stats)
-    norm = (stats, first_gain[None], first_bias[None], first_weight)
-    active, inside, totals = call(
-        functools.partial(inner_first, members),
-        (active_shape, inner_shape, totals_shape), (past, head, last, *norm), depth,
-    )
-    around = (near, far, active, *norm, inside)
+    row_shape = jax.ShapeDtypeStruct((depth, columns, channels), jnp.bfloat16)
+
+    def padded(count):
+        return pltpu.VMEM((count + 2, height + 2, columns, channels), jnp.bfloat16)
+
+    stats, head, last, near, far = call(
+        stats_kernel, (stats_shape, head_shape, last_shape, row_shape, row_shape),
+        (frames,), 2,
+    )
+    past = sent_ahead(last)
+    near, far = sent_sideways(near, far)
+    stats = exchange(stats)
+    corner = sent_sideways(*pick((past,), stats))
+    around = (past, *corner)
+    own = (head, last, near, far, stats, first_gain[None], first_bias[None], first_weight)
+    alone = depth >= 4
+    ahead = (() if alone else around) + own
     last, totals = call(
-        functools.partial(outer_first, members, depth - 2, 2),
-        (last_shape, totals_shape), (*around, totals), 2, (halo(2),),
+        functools.partial(first_kernel, members, depth - 2, 2, not alone),
+        (last_shape, totals_shape), ahead, 2, (padded(2),),
     )
     head, stats = call(
-        functools.partial(outer_first, members, 0, depth - 2),
-        (head_shape, stats_shape), (*around, totals), depth - 2, (halo(depth - 2),),
-    )
-    past, near, far, stats = gather(head, last, stats)
+        functools.partial(first_kernel, members, 0, depth - 2, True),
+        (head_shape, stats_shape), (*around, *own, totals), depth - 2, (padded(depth - 2),),
+    )
+    past = sent_ahead(last)
+    stats = exchange(stats)
+    near, far = sent_sideways(*pick((past, head, last), stats))
     norm = (stats, second_gain[None], second_bias[None], second_weight)
     active, inside = call(
         functools.partial(inner_second, members),
-        (active_shape, inner_shape), (past, head, last, *norm, cells), depth,
-        (pltpu.VMEM(inner_shape.shape, jnp.bfloat16), pltpu.SemaphoreType.DMA(())), (7,),
+        (active_shape, inner_shape), (past, head, last, *norm, frames), depth,
     )
     features, patches = call(
         functools.partial(outer_second, members),
         (cells_shape, jax.ShapeDtypeStruct((parts, rows, LANES), jnp.bfloat16)),
-        (near, far, active, *norm, inside, cells, latent_weight.T), depth,
+        (near, far, active, *norm, inside, frames, latent_weight.T), depth,
         (halo(depth), pltpu.VMEM(frames.shape, jnp.bfloat16),
-         pltpu.VMEM((height * columns, LANES), jnp.float32),
+         pltpu.VMEM((depth, height * columns, LANES), jnp.float32),
          pltpu.VMEM((parts, rows, LANES), jnp.float32), pltpu.SemaphoreType.DMA((3,))),
-        (8,), (HBM, VMEM),
+        (), (HBM, VMEM),
     )
     received = lax.all_to_all(patches, "tile", split_axis=0, concat_axis=0, tiled=True)
     tokens = pl.pallas_call(

time: 76.4 us -> 77.5 us (1.014)
  Pallas kernels: 21.3 us -> 18.7 us
  blocking collectives: 42.3 us -> 44.7 us
    all_to_all x2, blocking collectives: 29.9 us -> 33 us  [exchange(): return lax.all_to_all(stats, ALL, split_axis=0, concat_axis=0, tiled=True)]
    pallas_call x6 -> x5, Pallas kernels: 20.5 us -> 17.9 us  [call(): pl.pallas_call(kernel, out_shape=outs, in_specs=[HBM if i in hbm else VME...]
    ppermute x2 -> x3, starting transfers between devices: 1.53 us -> 2.19 us  [sent_sideways(): far = lax.ppermute(far, 'tile', far_pairs)]
  transfers between devices with their start and end apart: 6 -> 8, of which waited for: 0 -> 1; matrix products, arithmetic and copies ran while one was open for 0% -> 0% of each run, Pallas kernels for 15% -> 16%
where the time goes in v4:
time: 77.5 us; the launch traced here: 77.2 us
  blocking collectives  44.7 us (58%)
  Pallas kernels  18.7 us (24%)
  starting transfers between devices  10.8 us (14%)
  local copies, waits for them, and re-layouts  1.41 us (2%)
  between operations  0.85 us (1%)
    all_to_all x2, blocking collectives, exchange(): return lax.all_to_all(stats, ALL, split_axis=0, concat_axis=0, tiled=True)  33 us
    pallas_call x5, Pallas kernels, call(): pl.pallas_call(kernel, out_shape=outs, in_specs=[HBM if i in hbm else VME...  17.9 us
    all_to_all x1, blocking collectives, body(): lax.all_to_all(patches, 'tile', split_axis=0, concat_axis=0, tiled=True)  11.7 us
    ppermute x2, starting transfers between devices, sent_ahead(): return lax.ppermute(last, 'tm', pairs)  7.82 us
    ppermute x3, starting transfers between devices, sent_sideways(): far = lax.ppermute(far, 'tile', far_pairs)  2.19 us
  transfers between devices with their start and end apart: 8, of which 1 were waited for; matrix products, arithmetic and copies ran while one was open for 0% of the time, Pallas kernels for 16%

profile of v4, /device:TPU:0, one launch (start us, length us, event | category | flops | bytes accessed | tf_op | source)
XLA Modules:
  0.0 77.2 jit_solution(7360897224934170083)
XLA Ops:
  0.6 0.0 copy-start
  0.6 0.0 copy-start.2
  0.7 1.4 %copy-done.2 = bf16[4,4,128,256]{3,2,1,0:T(8,128)(2,1)S(1)} copy-done((bf16[4,4,128,256]{3,2,1,0:T(8,128)(2,1)S(1)}, bf16[4,4,128,256]{3,2,1,0:T(8,128)(2,1)}, u32[]{:S(2)}) %copy-start.2) | copy-done | bytes 1048600
  2.0 0.3 shard_map.95
  2.3 0.6 collective-permute-start
  2.9 0.7 collective-permute-start.1
  3.6 4.4 %collective-permute-start.3 = (bf16[2,4,128,256]{3,2,1,0:T(8,128)(2,1)S(1)}, bf16[2,4,128,256]{3,2,1,0:T(8,128)(2,1)S(1)}, u32[]{:S(2)}, u32[]{:S(2)}) collective-permute-start(bf16[2,4,128,256]{3,2,1,0:T(8,128)(2,1)S(1)} %get-tuple-element.20.refs_1_.refs_4_), channel_id=1, source_target_pairs={{0,8},{8,16},{16,24},{1,9},{9,17},{17,25},{2,10},{10,18},{18,26},{... | collective-permute-start | bytes 1572872 | tf_op jit(solution)/shard_map/ppermute | solution.py:352
  8.0 14.9 %all_to_all.15.refs_4_.refs_1_.refs_7_ = f32[32,2,256]{2,1,0:T(2,128)S(1)} all-to-all(f32[32,2,256]{2,1,0:T(2,128)S(1)} %get-tuple-element.23), channel_id=1, replica_groups=mesh['tm'=4,'tile'=8] {'tm','tile'}, dimensions={0} | all-to-all | bytes 131072 | tf_op jit(solution)/shard_map/all_to_all | solution.py:375
  22.9 0.0 collective-permute-done.refs_2_.refs_5_
  22.9 0.0 collective-permute-done.1.refs_3_.refs_6_
  22.9 0.0 copy-done
  23.0 4.2 %shard_map.96 = (bf16[2,4,128,256]{3,2,1,0:T(8,128)(2,1)S(1)}, f32[2,8,256]{2,1,0:T(8,128)S(1)}) custom-call(bf16[2,4,128,256]{3,2,1,0:T(8,128)(2,1)S(1)} %get-tuple-element.19.refs_0_.refs_3_, bf16[2,4,128,256]{3,2,1,0:T(8,128)(2,1)S(1)} %get-tuple-element.20.refs_1_.refs_4_, bf16[4,128,256]{2,1,0:T(8,128)(2,1)S(1)} %collective-permute-done.refs_2_.refs_5_, ...), custom_call_target="tpu_custom_call" | custom-call | flops 1811939328 | bytes 8388608 | tf_op jit(solution)/shard_map/pallas_call | solution.py:402
  27.2 3.4 %collective-permute-start.2 = (bf16[2,4,128,256]{3,2,1,0:T(8,128)(2,1)S(1)}, bf16[2,4,128,256]{3,2,1,0:T(8,128)(2,1)S(1)}, u32[]{:S(2)}, u32[]{:S(2)}) collective-permute-start(bf16[2,4,128,256]{3,2,1,0:T(8,128)(2,1)S(1)} %get-tuple-element.24.refs_2_.last), channel_id=1, source_target_pairs={{0,8},{8,16},{16,24},{1,9},{9,17},{17,25},{2,10},{10,18},{18,26},{... | collective-permute-start | bytes 1572872 | tf_op jit(solution)/shard_map/ppermute | solution.py:352
  30.6 0.0 collective-permute-done.3.refs_0_
  30.6 0.1 collective-permute-start.4
  30.7 0.7 collective-permute-start.5
  31.4 0.7 collective-permute-done.4.refs_1_
  32.0 0.0 collective-permute-done.5.refs_2_
  32.1 0.0 copy-start.8
  32.1 4.2 %shard_map.97 = (bf16[2,4,128,256]{3,2,1,0:T(8,128)(2,1)S(1)}, f32[32,2,256]{2,1,0:T(2,128)S(1)}) custom-call(bf16[2,4,128,256]{3,2,1,0:T(8,128)(2,1)S(1)} %collective-permute-done.3.refs_0_, bf16[2,128,256]{2,1,0:T(8,128)(2,1)S(1)} %collective-permute-done.4.refs_1_, bf16[2,128,256]{2,1,0:T(8,128)(2,1)S(1)} %collective-permute-done.5.refs_2_, ...), custom_call_target="tpu_custom_call" | custom-call | flops 1811939328 | bytes 8388608 | tf_op jit(solution)/shard_map/pallas_call | solution.py:402
  36.3 18.1 %all_to_all.16.refs_3_.stats = f32[32,2,256]{2,1,0:T(2,128)S(1)} all-to-all(f32[32,2,256]{2,1,0:T(2,128)S(1)} %get-tuple-element.29), channel_id=1, replica_groups=mesh['tm'=4,'tile'=8] {'tm','tile'}, dimensions={0} | all-to-all | bytes 131072 | tf_op jit(solution)/shard_map/all_to_all | solution.py:375
  54.4 0.0 collective-permute-done.2.refs_0_.past
  54.4 0.1 pick.3
  54.5 0.2 collective-permute-start.6
  54.6 0.9 %collective-permute-start.7 = (bf16[6,128,256]{2,1,0:T(8,128)(2,1)S(1)}, bf16[6,128,256]{2,1,0:T(8,128)(2,1)S(1)}, u32[]{:S(2)}, u32[]{:S(2)}) collective-permute-start(bf16[6,128,256]{2,1,0:T(8,128)(2,1)S(1)} %get-tuple-element.31), channel_id=1, source_target_pairs={{1,2},{2,1},{3,4},{4,3},{5,6},{6,5},{9,10},{10,9},{11,12},{12,11},... | collective-permute-start | bytes 1179656 | tf_op jit(solution)/shard_map/ppermute | solution.py:360
  55.5 0.0 copy-start.4
  55.6 4.2 %shard_map.98 = (bf16[6,4,128,256]{3,2,1,0:T(8,128)(2,1)S(1)}, bf16[4,2,128,256]{3,2,1,0:T(8,128)(2,1)S(1)}) custom-call(bf16[2,4,128,256]{3,2,1,0:T(8,128)(2,1)S(1)} %collective-permute-done.2.refs_0_.past, bf16[2,4,128,256]{3,2,1,0:T(8,128)(2,1)S(1)} %get-tuple-element.28.refs_1_.head, bf16[2,4,128,256]{3,2,1,0:T(8,128)(2,1)S(1)} %get-tuple-element.24.refs_2_.last, ...), custom_call_target="tpu_custom_call" | custom-call | flops 3623878656 | bytes 8388608 | tf_op jit(solution)/shard_map/pallas_call | solution.py:402
  59.8 0.0 collective-permute-done.6.near
  59.8 0.0 collective-permute-done.7.far
  59.8 5.0 %shard_map.99 = (bf16[4,4,128,256]{3,2,1,0:T(8,128)(2,1)}, bf16[8,32,128]{2,1,0:T(8,128)(2,1)S(1)}) custom-call(bf16[6,128,256]{2,1,0:T(8,128)(2,1)S(1)} %collective-permute-done.6.near, bf16[6,128,256]{2,1,0:T(8,128)(2,1)S(1)} %collective-permute-done.7.far, bf16[6,4,128,256]{3,2,1,0:T(8,128)(2,1)S(1)} %get-tuple-element.32.active, ...), custom_call_target="tpu_custom_call" | custom-call | flops 3623878656 | bytes 8388608 | tf_op jit(solution)/shard_map/pallas_call | solution.py:402
  64.8 11.7 %all_to_all.17.received = bf16[8,32,128]{2,1,0:T(8,128)(2,1)S(1)} all-to-all(bf16[8,32,128]{2,1,0:T(8,128)(2,1)S(1)} %get-tuple-element.35), channel_id=1, replica_groups=mesh['tm'=4,'tile'=8] {'tile'}, dimensions={0} | all-to-all | bytes 131072 | tf_op jit(solution)/shard_map/all_to_all | solution.py:451
  76.5 0.8 unpack.1
  (13 shorter events, 0.1 us)
Async XLA Ops:
  0.6 22.3 %copy-start = (bf16[3,3,3,256,256]{4,3,2,1,0:T(8,128)(2,1)S(1)}, bf16[3,3,3,256,256]{4,3,2,1,0:T(8,128)(2,1)}, u32[]{:S(2)}) copy-start(bf16[3,3,3,256,256]{4,3,2,1,0:T(8,128)(2,1)} %refs_10_.1) | copy-start | bytes 10616836
  0.6 1.4 %copy-start.2 = (bf16[4,4,128,256]{3,2,1,0:T(8,128)(2,1)S(1)}, bf16[4,4,128,256]{3,2,1,0:T(8,128)(2,1)}, u32[]{:S(2)}) copy-start(bf16[4,4,128,256]{3,2,1,0:T(8,128)(2,1)} %frames.3) | copy-start | bytes 3145732
  2.0 20.9 %copy-start.5 = (f32[256]{0:T(256)S(1)}, f32[256]{0:T(256)}, u32[]{:S(2)}) copy-start(f32[256]{0:T(256)} %param.9) | copy-start | bytes 3076
  2.0 20.9 %copy-start.6 = (f32[256]{0:T(256)S(1)}, f32[256]{0:T(256)}, u32[]{:S(2)}) copy-start(f32[256]{0:T(256)} %param.10) | copy-start | bytes 3076
  2.3 20.6 %collective-permute-start = (bf16[4,128,256]{2,1,0:T(8,128)(2,1)S(1)}, bf16[4,128,256]{2,1,0:T(8,128)(2,1)S(1)}, u32[]{:S(2)}, u32[]{:S(2)}) collective-permute-start(bf16[4,128,256]{2,1,0:T(8,128)(2,1)S(1)} %get-tuple-element.21), channel_id=1, source_target_pairs={{0,1},{1,0},{2,3},{3,2},{4,5},{5,4},{6,7},{7,6},{8,9},{9,8},{10,11... | collective-permute-start | bytes 786440 | tf_op jit(solution)/shard_map/ppermute | solution.py:359
  2.9 20.1 %collective-permute-start.1 = (bf16[4,128,256]{2,1,0:T(8,128)(2,1)S(1)}, bf16[4,128,256]{2,1,0:T(8,128)(2,1)S(1)}, u32[]{:S(2)}, u32[]{:S(2)}) collective-permute-start(bf16[4,128,256]{2,1,0:T(8,128)(2,1)S(1)} %get-tuple-element.22), channel_id=1, source_target_pairs={{1,2},{2,1},{3,4},{4,3},{5,6},{6,5},{9,10},{10,9},{11,12},{12,11},... | collective-permute-start | bytes 786440 | tf_op jit(solution)/shard_map/ppermute | solution.py:360
  3.6 27.0 %collective-permute-start.3 = (bf16[2,4,128,256]{3,2,1,0:T(8,128)(2,1)S(1)}, bf16[2,4,128,256]{3,2,1,0:T(8,128)(2,1)S(1)}, u32[]{:S(2)}, u32[]{:S(2)}) collective-permute-start(bf16[2,4,128,256]{3,2,1,0:T(8,128)(2,1)S(1)} %get-tuple-element.20.refs_1_.refs_4_), channel_id=1, source_target_pairs={{0,8},{8,16},{16,24},{1,9},{9,17},{17,25},{2,10},{10,18},{18,26},{... | collective-permute-start | bytes 1572872 | tf_op jit(solution)/shard_map/ppermute | solution.py:352
  27.2 27.2 %collective-permute-start.2 = (bf16[2,4,128,256]{3,2,1,0:T(8,128)(2,1)S(1)}, bf16[2,4,128,256]{3,2,1,0:T(8,128)(2,1)S(1)}, u32[]{:S(2)}, u32[]{:S(2)}) collective-permute-start(bf16[2,4,128,256]{3,2,1,0:T(8,128)(2,1)S(1)} %get-tuple-element.24.refs_2_.last), channel_id=1, source_target_pairs={{0,8},{8,16},{16,24},{1,9},{9,17},{17,25},{2,10},{10,18},{18,26},{... | collective-permute-start | bytes 1572872 | tf_op jit(solution)/shard_map/ppermute | solution.py:352
  30.6 1.4 %collective-permute-start.4 = (bf16[2,128,256]{2,1,0:T(8,128)(2,1)S(1)}, bf16[2,128,256]{2,1,0:T(8,128)(2,1)S(1)}, u32[]{:S(2)}, u32[]{:S(2)}) collective-permute-start(bf16[2,128,256]{2,1,0:T(8,128)(2,1)S(1)} %get-tuple-element.25), channel_id=1, source_target_pairs={{0,1},{1,0},{2,3},{3,2},{4,5},{5,4},{6,7},{7,6},{8,9},{9,8},{10,11... | collective-permute-start | bytes 393224 | tf_op jit(solution)/shard_map/ppermute | solution.py:359
  30.7 1.3 %collective-permute-start.5 = (bf16[2,128,256]{2,1,0:T(8,128)(2,1)S(1)}, bf16[2,128,256]{2,1,0:T(8,128)(2,1)S(1)}, u32[]{:S(2)}, u32[]{:S(2)}) collective-permute-start(bf16[2,128,256]{2,1,0:T(8,128)(2,1)S(1)} %get-tuple-element.26), channel_id=1, source_target_pairs={{1,2},{2,1},{3,4},{4,3},{5,6},{6,5},{9,10},{10,9},{11,12},{12,11},... | collective-permute-start | bytes 393224 | tf_op jit(solution)/shard_map/ppermute | solution.py:360
  32.0 23.5 %copy-start.1 = (bf16[3,3,3,256,256]{4,3,2,1,0:T(8,128)(2,1)S(1)}, bf16[3,3,3,256,256]{4,3,2,1,0:T(8,128)(2,1)}, u32[]{:S(2)}) copy-start(bf16[3,3,3,256,256]{4,3,2,1,0:T(8,128)(2,1)} %weight.3) | copy-start | bytes 10616836
  32.0 23.5 %copy-start.3 = (bf16[4,4,128,256]{3,2,1,0:T(8,128)(2,1)S(1)}, bf16[4,4,128,256]{3,2,1,0:T(8,128)(2,1)}, u32[]{:S(2)}) copy-start(bf16[4,4,128,256]{3,2,1,0:T(8,128)(2,1)} %frames.3) | copy-start | bytes 3145732
  32.0 23.5 %copy-start.7 = (f32[256]{0:T(256)S(1)}, f32[256]{0:T(256)}, u32[]{:S(2)}) copy-start(f32[256]{0:T(256)} %param.12) | copy-start | bytes 3076
  32.1 23.5 %copy-start.8 = (f32[256]{0:T(256)S(1)}, f32[256]{0:T(256)}, u32[]{:S(2)}) copy-start(f32[256]{0:T(256)} %param.13) | copy-start | bytes 3076
  54.5 5.3 %collective-permute-start.6 = (bf16[6,128,256]{2,1,0:T(8,128)(2,1)S(1)}, bf16[6,128,256]{2,1,0:T(8,128)(2,1)S(1)}, u32[]{:S(2)}, u32[]{:S(2)}) collective-permute-start(bf16[6,128,256]{2,1,0:T(8,128)(2,1)S(1)} %get-tuple-element.30), channel_id=1, source_target_pairs={{0,1},{1,0},{2,3},{3,2},{4,5},{5,4},{6,7},{7,6},{8,9},{9,8},{10,11... | collective-permute-start | bytes 1179656 | tf_op jit(solution)/shard_map/ppermute | solution.py:359
  54.6 5.1 %collective-permute-start.7 = (bf16[6,128,256]{2,1,0:T(8,128)(2,1)S(1)}, bf16[6,128,256]{2,1,0:T(8,128)(2,1)S(1)}, u32[]{:S(2)}, u32[]{:S(2)}) collective-permute-start(bf16[6,128,256]{2,1,0:T(8,128)(2,1)S(1)} %get-tuple-element.31), channel_id=1, source_target_pairs={{1,2},{2,1},{3,4},{4,3},{5,6},{6,5},{9,10},{10,9},{11,12},{12,11},... | collective-permute-start | bytes 1179656 | tf_op jit(solution)/shard_map/ppermute | solution.py:360
  55.5 4.2 %copy-start.4 = (bf16[256,16]{0,1:T(8,128)(2,1)S(1)}, bf16[256,16]{0,1:T(8,128)(2,1)}, u32[]{:S(2)}) copy-start(bf16[256,16]{0,1:T(8,128)(2,1)} %param.15) | copy-start | bytes 24580

commit v5 on v4

--- a/solution.py
+++ b/solution.py
@@ -36,25 +36,37 @@
     return jnp.where(even, height - 1, 0), jnp.where(even, 0, height - 1)
 
 
-def stats_kernel(frames_ref, out_ref, head_ref, last_ref, near_ref, far_ref):
-    depth, height, _, channels = frames_ref.shape
+def take_kernel(frames_hbm, last_ref, sem):
+    depth = frames_hbm.shape[0]
+    copy = pltpu.make_async_copy(frames_hbm.at[depth - 2 :], last_ref, sem)
+    copy.start()
+    copy.wait()
+
+
+def stats_kernel(frames_hbm, last_ref, out_ref, head_ref, near_ref, far_ref, sem):
+    before, height, _, channels = head_ref.shape
     near, far = sides(height)
-
-    def step(t, carry):
-        sums, squares = carry
-        for h in range(height):
-            value = frames_ref[t, h].astype(jnp.float32)
-            sums = sums + row_totals(value)
-            squares = squares + row_totals(value * value)
-        near_ref[t] = frames_ref[t, near]
-        far_ref[t] = frames_ref[t, far]
-        return sums, squares
+    load = pltpu.make_async_copy(frames_hbm.at[:before], head_ref, sem)
+    load.start()
+
+    def totals(ref, shift, carry):
+        def step(t, carry):
+            sums, squares = carry
+            for h in range(height):
+                value = ref[t, h].astype(jnp.float32)
+                sums = sums + row_totals(value)
+                squares = squares + row_totals(value * value)
+            near_ref[shift + t] = ref[t, near]
+            far_ref[shift + t] = ref[t, far]
+            return sums, squares
+
+        return lax.fori_loop(0, ref.shape[0], step, carry)
 
     zero = jnp.zeros((8, channels), jnp.float32)
-    sums, squares = lax.fori_loop(0, depth, step, (zero, zero))
+    carry = totals(last_ref, before, (zero, zero))
+    load.wait()
+    sums, squares = totals(head_ref, 0, carry)
     put_stats(out_ref, sums, squares)
-    head_ref[...] = frames_ref[: depth - 2]
-    last_ref[...] = frames_ref[depth - 2 :]
 
 
 def pick_kernel(count, *refs):
@@ -107,14 +119,14 @@
     return (lax.axis_index("tm") > 0).astype(jnp.float32)
 
 
-def convolve(piece, weight_ref, columns):
+def convolve(piece, weight_ref, columns, taps=None):
+    taps = taps or [(a, b) for a in range(3) for b in range(3)]
     totals = []
     for c in range(3):
         total = None
-        for a in range(3):
-            for b in range(3):
-                part = jnp.dot(piece(a, b), weight_ref[a, b, c], preferred_element_type=jnp.float32)
-                total = part if total is None else total + part
+        for a, b in taps:
+            part = jnp.dot(piece(a, b), weight_ref[a, b, c], preferred_element_type=jnp.float32)
+            total = part if total is None else total + part
         totals.append(total)
     rows = totals[0].shape[0]
     column = lax.broadcasted_iota(jnp.int32, totals[0].shape, 0) % columns
@@ -205,7 +217,7 @@
         totals_ref[1] = squares
 
 
-def inner(members, past, head, last, stats, gain, bias, weight, active_ref, finish):
+def inner(members, past, head, last, stats, gain, bias, weight, active_ref, partial_ref, finish):
     height, columns, channels = active_ref.shape[1:]
     scale = scale_of(stats, gain, bias, members)
     first = has_past()
@@ -224,9 +236,18 @@
 
         finish(t, count, convolve(piece, weight, columns))
 
+    depth = len(found) - 2
+    for edge, shift in enumerate((-1, height - 2)):
+
+        def own(a, b, shift=shift):
+            return active_ref[a : a + depth, shift + b].reshape(depth * columns, channels)
+
+        taps = [(a, b) for a in range(3) for b in range(3) if 0 <= shift + b < height]
+        partial_ref[edge] = convolve(own, weight, columns, taps)
+
 
 def inner_second(members, past, head, last, stats, gain, bias, weight, frames,
-                 active_ref, inner_ref):
+                 inner_ref, partial_ref, active_ref):
     height = frames.shape[1]
 
     def finish(t, count, total):
@@ -235,43 +256,35 @@
             count, *inner_ref.shape[1:]
         )
 
-    inner(members, past, head, last, stats, gain, bias, weight, active_ref, finish)
-
-
-def outer(members, begin, frames, near, far, active, stats, gain, bias, weight, halo_ref, finish):
-    height, columns = active.shape[1:3]
+    inner(members, past, head, last, stats, gain, bias, weight, active_ref, partial_ref, finish)
+
+
+def outer(members, near, far, stats, gain, bias, weight, partial, halo_ref):
+    columns, channels = halo_ref.shape[2:]
+    depth = halo_ref.shape[0] - 2
     scale = scale_of(stats, gain, bias, members)
     index, count = lax.axis_index("tile"), lax.axis_size("tile")
     even = index % 2 == 0
     first = has_past()
     above = (index > 0).astype(jnp.float32)
     below = (index < count - 1).astype(jnp.float32)
-    for t in range(frames + 2):
-        e = begin + t
-        rows = near[e], far[e]
-        top, bottom = (above * first, below * first) if e < 2 else (above, below)
+    for t in range(depth + 2):
+        rows = near[t], far[t]
+        top, bottom = (above * first, below * first) if t < 2 else (above, below)
         halo_ref[t, 0] = activate(jnp.where(even, rows[1], rows[0]), scale, top)
         halo_ref[t, 1] = activate(jnp.where(even, rows[0], rows[1]), scale, bottom)
-
-    def row(t, h):
-        if h == 0:
-            return halo_ref[t, 0]
-        if h == height + 1:
-            return halo_ref[t, 1]
-        return active[begin + t, h - 1]
-
-    for t, count in steps(frames):
-
-        def piece(a, b, t=t, count=count):
-            cells = [
-                row(t + a + f, h + b) for f in range(count) for h in (0, height - 1)
-            ]
-            return jnp.concatenate(cells, axis=0)
-
-        finish(t, count, convolve(piece, weight, columns))
-
-
-def outer_second(members, near, far, active, stats, gain, bias, weight, inside, frames, latent,
+    totals = []
+    for edge in range(2):
+
+        def piece(a, b, edge=edge):
+            return halo_ref[a : a + depth, edge].reshape(depth * columns, channels)
+
+        taps = [(a, 2 * edge) for a in range(3)]
+        totals.append(partial[edge] + convolve(piece, weight, columns, taps))
+    return totals
+
+
+def outer_second(members, near, far, stats, gain, bias, weight, inside, partial, frames, latent,
                  features_hbm, patches_ref, halo_ref, cells_ref, latents_ref, packed_ref, sem):
     depth, height, columns, channels = cells_ref.shape
     stores = [pltpu.make_async_copy(inside, features_hbm.at[:, 1 : height - 1], sem.at[2])]
@@ -290,14 +303,11 @@
     ).astype(jnp.bfloat16)
     cells_ref[:, 1 : height - 1] = inside[...]
 
-    def finish(t, count, total):
-        branch = total.reshape(count, 2, columns, channels)
-        for f in range(count):
-            for n, h in enumerate((0, height - 1)):
-                cells = frames[t + f, h].astype(jnp.float32)
-                cells_ref[t + f, h] = (cells + branch[f, n]).astype(jnp.bfloat16)
-
-    outer(members, 0, depth, near, far, active, stats, gain, bias, weight, halo_ref, finish)
+    totals = outer(members, near, far, stats, gain, bias, weight, partial, halo_ref)
+    for total, h in zip(totals, (0, height - 1)):
+        branch = total.reshape(depth, columns, channels)
+        for t in range(depth):
+            cells_ref[t, h] = (frames[t, h].astype(jnp.float32) + branch[t]).astype(jnp.bfloat16)
     for n, h in enumerate((0, height - 1)):
         stores.append(
             pltpu.make_async_copy(
@@ -392,6 +402,7 @@
 
     active_shape = jax.ShapeDtypeStruct((depth + 2, height, columns, channels), jnp.bfloat16)
     inner_shape = jax.ShapeDtypeStruct((depth, height - 2, columns, channels), jnp.bfloat16)
+    partial_shape = jax.ShapeDtypeStruct((2, depth * columns, channels), jnp.float32)
     totals_shape = jax.ShapeDtypeStruct((2, 8, channels), jnp.float32)
 
     def halo(count):
@@ -411,11 +422,13 @@
     def padded(count):
         return pltpu.VMEM((count + 2, height + 2, columns, channels), jnp.bfloat16)
 
-    stats, head, last, near, far = call(
-        stats_kernel, (stats_shape, head_shape, last_shape, row_shape, row_shape),
-        (frames,), 2,
-    )
+    cells = pltpu.with_memory_space_constraint(frames, pltpu.HBM)
+    (last,) = call(take_kernel, (last_shape,), (cells,), 1, (pltpu.SemaphoreType.DMA(()),), (0,))
     past = sent_ahead(last)
+    stats, head, near, far = call(
+        stats_kernel, (stats_shape, head_shape, row_shape, row_shape),
+        (cells, last), 2, (pltpu.SemaphoreType.DMA(()),), (0,),
+    )
     near, far = sent_sideways(near, far)
     stats = exchange(stats)
     corner = sent_sideways(*pick((past,), stats))
@@ -435,14 +448,15 @@
     stats = exchange(stats)
     near, far = sent_sideways(*pick((past, head, last), stats))
     norm = (stats, second_gain[None], second_bias[None], second_weight)
-    active, inside = call(
+    inside, partial = call(
         functools.partial(inner_second, members),
-        (active_shape, inner_shape), (past, head, last, *norm, frames), depth,
+        (inner_shape, partial_shape), (past, head, last, *norm, frames), depth,
+        (pltpu.VMEM(active_shape.shape, jnp.bfloat16),),
     )
     features, patches = call(
         functools.partial(outer_second, members),
         (cells_shape, jax.ShapeDtypeStruct((parts, rows, LANES), jnp.bfloat16)),
-        (near, far, active, *norm, inside, frames, latent_weight.T), depth,
+        (near, far, *norm, inside, partial, frames, latent_weight.T), depth,
         (halo(depth), pltpu.VMEM(frames.shape, jnp.bfloat16),
          pltpu.VMEM((depth, height * columns, LANES), jnp.float32),
          pltpu.VMEM((parts, rows, LANES), jnp.float32), pltpu.SemaphoreType.DMA((3,))),

time: 77.5 us -> 77.2 us (level)
  Pallas kernels: 18.7 us -> 21.2 us
  blocking collectives: 44.7 us -> 43.3 us
  local copies, waits for them, and re-layouts: 1.41 us -> 0.04 us
    pallas_call x5 -> x6, Pallas kernels: 17.9 us -> 20.3 us  [call(): pl.pallas_call(kernel, out_shape=outs, in_specs=[HBM if i in hbm else VME...]
    all_to_all x1, blocking collectives: 11.7 us -> 10.2 us  [body(): lax.all_to_all(patches, 'tile', split_axis=0, concat_axis=0, tiled=True)]
    unnamed x18 -> x16, local copies, waits for them, and re-layouts: 1.41 us -> 0.04 us
  transfers between devices with their start and end apart: 8 -> 8, of which waited for: 1 -> 1; matrix products, arithmetic and copies ran while one was open for 0% -> 0% of each run, Pallas kernels for 16% -> 20%
where the time goes in v5:
time: 77.2 us; the launch traced here: 76.8 us
  blocking collectives  43.3 us (56%)
  Pallas kernels  21.2 us (27%)
  starting transfers between devices  10.8 us (14%)
  between operations  0.87 us (1%)
    all_to_all x2, blocking collectives, exchange(): return lax.all_to_all(stats, ALL, split_axis=0, concat_axis=0, tiled=True)  33 us
    pallas_call x6, Pallas kernels, call(): pl.pallas_call(kernel, out_shape=outs, in_specs=[HBM if i in hbm else VME...  20.3 us
    all_to_all x1, blocking collectives, body(): lax.all_to_all(patches, 'tile', split_axis=0, concat_axis=0, tiled=True)  10.2 us
    ppermute x2, starting transfers between devices, sent_ahead(): return lax.ppermute(last, 'tm', pairs)  7.82 us
    ppermute x3, starting transfers between devices, sent_sideways(): far = lax.ppermute(far, 'tile', far_pairs)  2.19 us
  transfers between devices with their start and end apart: 8, of which 1 were waited for; matrix products, arithmetic and copies ran while one was open for 0% of the time, Pallas kernels for 20%

profile of v5, /device:TPU:0, one launch (start us, length us, event | category | flops | bytes accessed | tf_op | source)
XLA Modules:
  0.0 76.8 jit_solution(13468415976486828880)
XLA Ops:
  0.6 1.1 %shard_map.95.last_ref.refs_1_.refs_4_ = bf16[2,4,128,256]{3,2,1,0:T(8,128)(2,1)S(1)} custom-call(bf16[4,4,128,256]{3,2,1,0:T(8,128)(2,1)} %frames.3), custom_call_target="tpu_custom_call" | custom-call | flops 905969664 | bytes 8388608 | tf_op jit(solution)/shard_map/pallas_call | solution.py:413
  1.7 0.0 copy-start
  1.7 0.0 copy-start.4
  1.7 0.0 copy-start.5
  1.7 1.3 %shard_map.96 = (f32[32,2,256]{2,1,0:T(2,128)S(1)}, bf16[2,4,128,256]{3,2,1,0:T(8,128)(2,1)S(1)}, bf16[4,128,256]{2,1,0:T(8,128)(2,1)S(1)}, bf16[4,128,256]{2,1,0:T(8,128)(2,1)S(1)}) custom-call(bf16[4,4,128,256]{3,2,1,0:T(8,128)(2,1)} %frames.3, bf16[2,4,128,256]{3,2,1,0:T(8,128)(2,1)S(1)} %shard_map.95.last_ref.refs_1_.refs_4_), custom_call_target="tpu_custom_call" | custom-call | flops 1811939328 | bytes 8388608 | tf_op jit(solution)/shard_map/pallas_call | solution.py:413
  3.1 0.6 collective-permute-start
  3.6 0.7 collective-permute-start.1
  4.3 4.4 %collective-permute-start.3 = (bf16[2,4,128,256]{3,2,1,0:T(8,128)(2,1)S(1)}, bf16[2,4,128,256]{3,2,1,0:T(8,128)(2,1)S(1)}, u32[]{:S(2)}, u32[]{:S(2)}) collective-permute-start(bf16[2,4,128,256]{3,2,1,0:T(8,128)(2,1)S(1)} %shard_map.95.last_ref.refs_1_.refs_4_), channel_id=1, source_target_pairs={{0,8},{8,16},{16,24},{1,9},{9,17},{17,25},{2,10},{10,18},{18,26},{... | collective-permute-start | bytes 1572872 | tf_op jit(solution)/shard_map/ppermute | solution.py:362
  8.7 14.9 %all_to_all.15.refs_4_.refs_1_.refs_7_ = f32[32,2,256]{2,1,0:T(2,128)S(1)} all-to-all(f32[32,2,256]{2,1,0:T(2,128)S(1)} %get-tuple-element.21), channel_id=1, replica_groups=mesh['tm'=4,'tile'=8] {'tm','tile'}, dimensions={0} | all-to-all | bytes 131072 | tf_op jit(solution)/shard_map/all_to_all | solution.py:385
  23.7 0.0 collective-permute-done.refs_2_.refs_5_
  23.7 0.0 collective-permute-done.1.refs_3_.refs_6_
  23.7 4.2 %shard_map.97 = (bf16[2,4,128,256]{3,2,1,0:T(8,128)(2,1)S(1)}, f32[2,8,256]{2,1,0:T(8,128)S(1)}) custom-call(bf16[2,4,128,256]{3,2,1,0:T(8,128)(2,1)S(1)} %get-tuple-element.18.refs_0_.refs_3_, bf16[2,4,128,256]{3,2,1,0:T(8,128)(2,1)S(1)} %shard_map.95.last_ref.refs_1_.refs_4_, bf16[4,128,256]{2,1,0:T(8,128)(2,1)S(1)} %collective-permute-done.refs_2_.refs_5_, ...), custom_call_target="tpu_custom_call" | custom-call | flops 1811939328 | bytes 8388608 | tf_op jit(solution)/shard_map/pallas_call | solution.py:413
  27.9 3.4 %collective-permute-start.2 = (bf16[2,4,128,256]{3,2,1,0:T(8,128)(2,1)S(1)}, bf16[2,4,128,256]{3,2,1,0:T(8,128)(2,1)S(1)}, u32[]{:S(2)}, u32[]{:S(2)}) collective-permute-start(bf16[2,4,128,256]{3,2,1,0:T(8,128)(2,1)S(1)} %get-tuple-element.22.refs_2_.last), channel_id=1, source_target_pairs={{0,8},{8,16},{16,24},{1,9},{9,17},{17,25},{2,10},{10,18},{18,26},{... | collective-permute-start | bytes 1572872 | tf_op jit(solution)/shard_map/ppermute | solution.py:362
  31.3 0.0 collective-permute-done.3.refs_0_
  31.4 0.1 collective-permute-start.4
  31.5 0.7 collective-permute-start.5
  32.1 0.7 collective-permute-done.4.refs_1_
  32.8 0.0 collective-permute-done.5.refs_2_
  32.8 0.0 copy-start.7
  32.8 4.2 %shard_map.98 = (bf16[2,4,128,256]{3,2,1,0:T(8,128)(2,1)S(1)}, f32[32,2,256]{2,1,0:T(2,128)S(1)}) custom-call(bf16[2,4,128,256]{3,2,1,0:T(8,128)(2,1)S(1)} %collective-permute-done.3.refs_0_, bf16[2,128,256]{2,1,0:T(8,128)(2,1)S(1)} %collective-permute-done.4.refs_1_, bf16[2,128,256]{2,1,0:T(8,128)(2,1)S(1)} %collective-permute-done.5.refs_2_, ...), custom_call_target="tpu_custom_call" | custom-call | flops 1811939328 | bytes 8388608 | tf_op jit(solution)/shard_map/pallas_call | solution.py:413
  37.1 18.1 %all_to_all.16.refs_3_.stats = f32[32,2,256]{2,1,0:T(2,128)S(1)} all-to-all(f32[32,2,256]{2,1,0:T(2,128)S(1)} %get-tuple-element.27), channel_id=1, replica_groups=mesh['tm'=4,'tile'=8] {'tm','tile'}, dimensions={0} | all-to-all | bytes 131072 | tf_op jit(solution)/shard_map/all_to_all | solution.py:385
  55.2 0.0 collective-permute-done.2.refs_0_.past
  55.2 0.1 pick.3
  55.2 0.2 collective-permute-start.6
  55.4 0.9 %collective-permute-start.7 = (bf16[6,128,256]{2,1,0:T(8,128)(2,1)S(1)}, bf16[6,128,256]{2,1,0:T(8,128)(2,1)S(1)}, u32[]{:S(2)}, u32[]{:S(2)}) collective-permute-start(bf16[6,128,256]{2,1,0:T(8,128)(2,1)S(1)} %get-tuple-element.29), channel_id=1, source_target_pairs={{1,2},{2,1},{3,4},{4,3},{5,6},{6,5},{9,10},{10,9},{11,12},{12,11},... | collective-permute-start | bytes 1179656 | tf_op jit(solution)/shard_map/ppermute | solution.py:370
  56.3 0.0 copy-start.3
  56.3 6.7 %shard_map.99 = (bf16[4,2,128,256]{3,2,1,0:T(8,128)(2,1)S(1)}, f32[2,512,256]{2,1,0:T(8,128)S(1)}) custom-call(bf16[2,4,128,256]{3,2,1,0:T(8,128)(2,1)S(1)} %collective-permute-done.2.refs_0_.past, bf16[2,4,128,256]{3,2,1,0:T(8,128)(2,1)S(1)} %get-tuple-element.26.refs_1_.head, bf16[2,4,128,256]{3,2,1,0:T(8,128)(2,1)S(1)} %get-tuple-element.22.refs_2_.last, ...), custom_call_target="tpu_custom_call" | custom-call | flops 3623878656 | bytes 8388608 | tf_op jit(solution)/shard_map/pallas_call | solution.py:413
  63.0 0.0 collective-permute-done.6.near
  63.0 0.0 collective-permute-done.7.far
  63.0 2.8 %shard_map.100 = (bf16[4,4,128,256]{3,2,1,0:T(8,128)(2,1)}, bf16[8,32,128]{2,1,0:T(8,128)(2,1)S(1)}) custom-call(bf16[6,128,256]{2,1,0:T(8,128)(2,1)S(1)} %collective-permute-done.6.near, bf16[6,128,256]{2,1,0:T(8,128)(2,1)S(1)} %collective-permute-done.7.far, f32[32,2,256]{2,1,0:T(2,128)S(1)} %all_to_all.16.refs_3_.stats, f32[1,256]{1,0:T(1,128)S(1)} %bitcast.11, ...), custom_call_target="tpu_custom_call" | custom-call | flops 3623878656 | bytes 8388608 | tf_op jit(solution)/shard_map/pallas_call | solution.py:413
  65.9 10.2 %all_to_all.17.received = bf16[8,32,128]{2,1,0:T(8,128)(2,1)S(1)} all-to-all(bf16[8,32,128]{2,1,0:T(8,128)(2,1)S(1)} %get-tuple-element.33), channel_id=1, replica_groups=mesh['tm'=4,'tile'=8] {'tile'}, dimensions={0} | all-to-all | bytes 131072 | tf_op jit(solution)/shard_map/all_to_all | solution.py:465
  76.1 0.8 unpack.1
  (12 shorter events, 0.1 us)
Async XLA Ops:
  1.7 22.0 %copy-start = (bf16[3,3,3,256,256]{4,3,2,1,0:T(8,128)(2,1)S(1)}, bf16[3,3,3,256,256]{4,3,2,1,0:T(8,128)(2,1)}, u32[]{:S(2)}) copy-start(bf16[3,3,3,256,256]{4,3,2,1,0:T(8,128)(2,1)} %refs_10_.1) | copy-start | bytes 10616836
  1.7 22.0 %copy-start.4 = (f32[256]{0:T(256)S(1)}, f32[256]{0:T(256)}, u32[]{:S(2)}) copy-start(f32[256]{0:T(256)} %param.9) | copy-start | bytes 3076
  1.7 22.0 %copy-start.5 = (f32[256]{0:T(256)S(1)}, f32[256]{0:T(256)}, u32[]{:S(2)}) copy-start(f32[256]{0:T(256)} %param.10) | copy-start | bytes 3076
  3.1 20.6 %collective-permute-start = (bf16[4,128,256]{2,1,0:T(8,128)(2,1)S(1)}, bf16[4,128,256]{2,1,0:T(8,128)(2,1)S(1)}, u32[]{:S(2)}, u32[]{:S(2)}) collective-permute-start(bf16[4,128,256]{2,1,0:T(8,128)(2,1)S(1)} %get-tuple-element.19), channel_id=1, source_target_pairs={{0,1},{1,0},{2,3},{3,2},{4,5},{5,4},{6,7},{7,6},{8,9},{9,8},{10,11... | collective-permute-start | bytes 786440 | tf_op jit(solution)/shard_map/ppermute | solution.py:369
  3.6 20.1 %collective-permute-start.1 = (bf16[4,128,256]{2,1,0:T(8,128)(2,1)S(1)}, bf16[4,128,256]{2,1,0:T(8,128)(2,1)S(1)}, u32[]{:S(2)}, u32[]{:S(2)}) collective-permute-start(bf16[4,128,256]{2,1,0:T(8,128)(2,1)S(1)} %get-tuple-element.20), channel_id=1, source_target_pairs={{1,2},{2,1},{3,4},{4,3},{5,6},{6,5},{9,10},{10,9},{11,12},{12,11},... | collective-permute-start | bytes 786440 | tf_op jit(solution)/shard_map/ppermute | solution.py:370
  4.3 27.0 %collective-permute-start.3 = (bf16[2,4,128,256]{3,2,1,0:T(8,128)(2,1)S(1)}, bf16[2,4,128,256]{3,2,1,0:T(8,128)(2,1)S(1)}, u32[]{:S(2)}, u32[]{:S(2)}) collective-permute-start(bf16[2,4,128,256]{3,2,1,0:T(8,128)(2,1)S(1)} %shard_map.95.last_ref.refs_1_.refs_4_), channel_id=1, source_target_pairs={{0,8},{8,16},{16,24},{1,9},{9,17},{17,25},{2,10},{10,18},{18,26},{... | collective-permute-start | bytes 1572872 | tf_op jit(solution)/shard_map/ppermute | solution.py:362
  27.9 27.2 %collective-permute-start.2 = (bf16[2,4,128,256]{3,2,1,0:T(8,128)(2,1)S(1)}, bf16[2,4,128,256]{3,2,1,0:T(8,128)(2,1)S(1)}, u32[]{:S(2)}, u32[]{:S(2)}) collective-permute-start(bf16[2,4,128,256]{3,2,1,0:T(8,128)(2,1)S(1)} %get-tuple-element.22.refs_2_.last), channel_id=1, source_target_pairs={{0,8},{8,16},{16,24},{1,9},{9,17},{17,25},{2,10},{10,18},{18,26},{... | collective-permute-start | bytes 1572872 | tf_op jit(solution)/shard_map/ppermute | solution.py:362
  31.4 1.4 %collective-permute-start.4 = (bf16[2,128,256]{2,1,0:T(8,128)(2,1)S(1)}, bf16[2,128,256]{2,1,0:T(8,128)(2,1)S(1)}, u32[]{:S(2)}, u32[]{:S(2)}) collective-permute-start(bf16[2,128,256]{2,1,0:T(8,128)(2,1)S(1)} %get-tuple-element.23), channel_id=1, source_target_pairs={{0,1},{1,0},{2,3},{3,2},{4,5},{5,4},{6,7},{7,6},{8,9},{9,8},{10,11... | collective-permute-start | bytes 393224 | tf_op jit(solution)/shard_map/ppermute | solution.py:369
  31.5 1.3 %collective-permute-start.5 = (bf16[2,128,256]{2,1,0:T(8,128)(2,1)S(1)}, bf16[2,128,256]{2,1,0:T(8,128)(2,1)S(1)}, u32[]{:S(2)}, u32[]{:S(2)}) collective-permute-start(bf16[2,128,256]{2,1,0:T(8,128)(2,1)S(1)} %get-tuple-element.24), channel_id=1, source_target_pairs={{1,2},{2,1},{3,4},{4,3},{5,6},{6,5},{9,10},{10,9},{11,12},{12,11},... | collective-permute-start | bytes 393224 | tf_op jit(solution)/shard_map/ppermute | solution.py:370
  32.8 23.5 %copy-start.1 = (bf16[3,3,3,256,256]{4,3,2,1,0:T(8,128)(2,1)S(1)}, bf16[3,3,3,256,256]{4,3,2,1,0:T(8,128)(2,1)}, u32[]{:S(2)}) copy-start(bf16[3,3,3,256,256]{4,3,2,1,0:T(8,128)(2,1)} %weight.3) | copy-start | bytes 10616836
  32.8 23.5 %copy-start.2 = (bf16[4,4,128,256]{3,2,1,0:T(8,128)(2,1)S(1)}, bf16[4,4,128,256]{3,2,1,0:T(8,128)(2,1)}, u32[]{:S(2)}) copy-start(bf16[4,4,128,256]{3,2,1,0:T(8,128)(2,1)} %frames.3) | copy-start | bytes 3145732
  32.8 23.5 %copy-start.6 = (f32[256]{0:T(256)S(1)}, f32[256]{0:T(256)}, u32[]{:S(2)}) copy-start(f32[256]{0:T(256)} %param.12) | copy-start | bytes 3076
  32.8 23.5 %copy-start.7 = (f32[256]{0:T(256)S(1)}, f32[256]{0:T(256)}, u32[]{:S(2)}) copy-start(f32[256]{0:T(256)} %param.13) | copy-start | bytes 3076
  55.2 7.8 %collective-permute-start.6 = (bf16[6,128,256]{2,1,0:T(8,128)(2,1)S(1)}, bf16[6,128,256]{2,1,0:T(8,128)(2,1)S(1)}, u32[]{:S(2)}, u32[]{:S(2)}) collective-permute-start(bf16[6,128,256]{2,1,0:T(8,128)(2,1)S(1)} %get-tuple-element.28), channel_id=1, source_target_pairs={{0,1},{1,0},{2,3},{3,2},{4,5},{5,4},{6,7},{7,6},{8,9},{9,8},{10,11... | collective-permute-start | bytes 1179656 | tf_op jit(solution)/shard_map/ppermute | solution.py:369
  55.4 7.6 %collective-permute-start.7 = (bf16[6,128,256]{2,1,0:T(8,128)(2,1)S(1)}, bf16[6,128,256]{2,1,0:T(8,128)(2,1)S(1)}, u32[]{:S(2)}, u32[]{:S(2)}) collective-permute-start(bf16[6,128,256]{2,1,0:T(8,128)(2,1)S(1)} %get-tuple-element.29), channel_id=1, source_target_pairs={{1,2},{2,1},{3,4},{4,3},{5,6},{6,5},{9,10},{10,9},{11,12},{12,11},... | collective-permute-start | bytes 1179656 | tf_op jit(solution)/shard_map/ppermute | solution.py:370
  56.3 6.7 %copy-start.3 = (bf16[256,16]{0,1:T(8,128)(2,1)S(1)}, bf16[256,16]{0,1:T(8,128)(2,1)}, u32[]{:S(2)}) copy-start(bf16[256,16]{0,1:T(8,128)(2,1)} %param.15) | copy-start | bytes 24580

commit v6 on v5

--- a/solution.py
+++ b/solution.py
@@ -36,18 +36,18 @@
     return jnp.where(even, height - 1, 0), jnp.where(even, 0, height - 1)
 
 
-def take_kernel(frames_hbm, last_ref, sem):
-    depth = frames_hbm.shape[0]
-    copy = pltpu.make_async_copy(frames_hbm.at[depth - 2 :], last_ref, sem)
-    copy.start()
-    copy.wait()
-
-
-def stats_kernel(frames_hbm, last_ref, out_ref, head_ref, near_ref, far_ref, sem):
+def stats_kernel(frames_hbm, out_ref, head_ref, last_ref, near_ref, far_ref, sem):
     before, height, _, channels = head_ref.shape
     near, far = sides(height)
-    load = pltpu.make_async_copy(frames_hbm.at[:before], head_ref, sem)
-    load.start()
+    loads = [
+        pltpu.make_async_copy(frames_hbm.at[before + t], last_ref.at[t], sem.at[before + t])
+        for t in range(last_ref.shape[0])
+    ]
+    loads += [
+        pltpu.make_async_copy(frames_hbm.at[t], head_ref.at[t], sem.at[t]) for t in range(before)
+    ]
+    for load in loads:
+        load.start()
 
     def totals(ref, shift, carry):
         def step(t, carry):
@@ -60,11 +60,14 @@
             far_ref[shift + t] = ref[t, far]
             return sums, squares
 
-        return lax.fori_loop(0, ref.shape[0], step, carry)
-
+        for t in range(ref.shape[0]):
+            loads[order.pop(0)].wait()
+            carry = step(t, carry)
+        return carry
+
+    order = list(range(len(loads)))
     zero = jnp.zeros((8, channels), jnp.float32)
     carry = totals(last_ref, before, (zero, zero))
-    load.wait()
     sums, squares = totals(head_ref, 0, carry)
     put_stats(out_ref, sums, squares)
 
@@ -423,12 +426,11 @@
         return pltpu.VMEM((count + 2, height + 2, columns, channels), jnp.bfloat16)
 
     cells = pltpu.with_memory_space_constraint(frames, pltpu.HBM)
-    (last,) = call(take_kernel, (last_shape,), (cells,), 1, (pltpu.SemaphoreType.DMA(()),), (0,))
+    stats, head, last, near, far = call(
+        stats_kernel, (stats_shape, head_shape, last_shape, row_shape, row_shape),
+        (cells,), 2, (pltpu.SemaphoreType.DMA((depth,)),), (0,),
+    )
     past = sent_ahead(last)
-    stats, head, near, far = call(
-        stats_kernel, (stats_shape, head_shape, row_shape, row_shape),
-        (cells, last), 2, (pltpu.SemaphoreType.DMA(()),), (0,),
-    )
     near, far = sent_sideways(near, far)
     stats = exchange(stats)
     corner = sent_sideways(*pick((past,), stats))

time: 77.2 us -> 76.2 us (0.987)
  Pallas kernels: 21.2 us -> 20.2 us
    pallas_call x6 -> x5, Pallas kernels: 20.3 us -> 19.4 us  [call(): pl.pallas_call(kernel, out_shape=outs, in_specs=[HBM if i in hbm else VME...]
where the time goes in v6:
time: 76.2 us; the launch traced here: 75.9 us
  blocking collectives  43.3 us (57%)
  Pallas kernels  20.2 us (27%)
  starting transfers between devices  10.8 us (14%)
  between operations  0.86 us (1%)
    all_to_all x2, blocking collectives, exchange(): return lax.all_to_all(stats, ALL, split_axis=0, concat_axis=0, tiled=True)  33 us
    pallas_call x5, Pallas kernels, call(): pl.pallas_call(kernel, out_shape=outs, in_specs=[HBM if i in hbm else VME...  19.4 us
    all_to_all x1, blocking collectives, body(): lax.all_to_all(patches, 'tile', split_axis=0, concat_axis=0, tiled=True)  10.2 us
    ppermute x2, starting transfers between devices, sent_ahead(): return lax.ppermute(last, 'tm', pairs)  7.82 us
    ppermute x3, starting transfers between devices, sent_sideways(): far = lax.ppermute(far, 'tile', far_pairs)  2.19 us
  transfers between devices with their start and end apart: 8, of which 1 were waited for; matrix products, arithmetic and copies ran while one was open for 0% of the time, Pallas kernels for 20%

profile of v6, /device:TPU:0, one launch (start us, length us, event | category | flops | bytes accessed | tf_op | source)
XLA Modules:
  0.0 75.9 jit_solution(13335050517143165532)
XLA Ops:
  0.6 0.0 copy-start
  0.6 0.0 copy-start.5
  0.7 0.0 copy-start.4
  0.7 1.5 %shard_map.95 = (f32[32,2,256]{2,1,0:T(2,128)S(1)}, bf16[2,4,128,256]{3,2,1,0:T(8,128)(2,1)S(1)}, bf16[2,4,128,256]{3,2,1,0:T(8,128)(2,1)S(1)}, bf16[4,128,256]{2,1,0:T(8,128)(2,1)S(1)}, bf16[4,128,256]{2,1,0:T(8,128)(2,1)S(1)}) custom-call(bf16[4,4,128,256]{3,2,1,0:T(8,128)(2,1)} %frames.3), custom_call_target="tpu_custom_call" | custom-call | flops 1811939328 | bytes 8388608 | tf_op jit(solution)/shard_map/pallas_call | solution.py:416
  2.1 0.6 collective-permute-start
  2.7 0.7 collective-permute-start.1
  3.4 4.4 %collective-permute-start.3 = (bf16[2,4,128,256]{3,2,1,0:T(8,128)(2,1)S(1)}, bf16[2,4,128,256]{3,2,1,0:T(8,128)(2,1)S(1)}, u32[]{:S(2)}, u32[]{:S(2)}) collective-permute-start(bf16[2,4,128,256]{3,2,1,0:T(8,128)(2,1)S(1)} %get-tuple-element.20.refs_1_.refs_4_), channel_id=1, source_target_pairs={{0,8},{8,16},{16,24},{1,9},{9,17},{17,25},{2,10},{10,18},{18,26},{... | collective-permute-start | bytes 1572872 | tf_op jit(solution)/shard_map/ppermute | solution.py:365
  7.8 14.9 %all_to_all.15.refs_4_.refs_1_.refs_7_ = f32[32,2,256]{2,1,0:T(2,128)S(1)} all-to-all(f32[32,2,256]{2,1,0:T(2,128)S(1)} %get-tuple-element.23), channel_id=1, replica_groups=mesh['tm'=4,'tile'=8] {'tm','tile'}, dimensions={0} | all-to-all | bytes 131072 | tf_op jit(solution)/shard_map/all_to_all | solution.py:388
  22.7 0.0 collective-permute-done.refs_2_.refs_5_
  22.7 0.0 collective-permute-done.1.refs_3_.refs_6_
  22.7 0.0 copy-done
  22.8 4.2 %shard_map.96 = (bf16[2,4,128,256]{3,2,1,0:T(8,128)(2,1)S(1)}, f32[2,8,256]{2,1,0:T(8,128)S(1)}) custom-call(bf16[2,4,128,256]{3,2,1,0:T(8,128)(2,1)S(1)} %get-tuple-element.19.refs_0_.refs_3_, bf16[2,4,128,256]{3,2,1,0:T(8,128)(2,1)S(1)} %get-tuple-element.20.refs_1_.refs_4_, bf16[4,128,256]{2,1,0:T(8,128)(2,1)S(1)} %collective-permute-done.refs_2_.refs_5_, ...), custom_call_target="tpu_custom_call" | custom-call | flops 1811939328 | bytes 8388608 | tf_op jit(solution)/shard_map/pallas_call | solution.py:416
  27.0 3.4 %collective-permute-start.2 = (bf16[2,4,128,256]{3,2,1,0:T(8,128)(2,1)S(1)}, bf16[2,4,128,256]{3,2,1,0:T(8,128)(2,1)S(1)}, u32[]{:S(2)}, u32[]{:S(2)}) collective-permute-start(bf16[2,4,128,256]{3,2,1,0:T(8,128)(2,1)S(1)} %get-tuple-element.24.refs_2_.last), channel_id=1, source_target_pairs={{0,8},{8,16},{16,24},{1,9},{9,17},{17,25},{2,10},{10,18},{18,26},{... | collective-permute-start | bytes 1572872 | tf_op jit(solution)/shard_map/ppermute | solution.py:365
  30.4 0.0 collective-permute-done.3.refs_0_
  30.4 0.1 collective-permute-start.4
  30.5 0.7 collective-permute-start.5
  31.2 0.7 collective-permute-done.4.refs_1_
  31.8 0.0 collective-permute-done.5.refs_2_
  31.9 0.0 copy-start.7
  31.9 4.2 %shard_map.97 = (bf16[2,4,128,256]{3,2,1,0:T(8,128)(2,1)S(1)}, f32[32,2,256]{2,1,0:T(2,128)S(1)}) custom-call(bf16[2,4,128,256]{3,2,1,0:T(8,128)(2,1)S(1)} %collective-permute-done.3.refs_0_, bf16[2,128,256]{2,1,0:T(8,128)(2,1)S(1)} %collective-permute-done.4.refs_1_, bf16[2,128,256]{2,1,0:T(8,128)(2,1)S(1)} %collective-permute-done.5.refs_2_, ...), custom_call_target="tpu_custom_call" | custom-call | flops 1811939328 | bytes 8388608 | tf_op jit(solution)/shard_map/pallas_call | solution.py:416
  36.1 18.1 %all_to_all.16.refs_3_.stats = f32[32,2,256]{2,1,0:T(2,128)S(1)} all-to-all(f32[32,2,256]{2,1,0:T(2,128)S(1)} %get-tuple-element.29), channel_id=1, replica_groups=mesh['tm'=4,'tile'=8] {'tm','tile'}, dimensions={0} | all-to-all | bytes 131072 | tf_op jit(solution)/shard_map/all_to_all | solution.py:388
  54.2 0.0 collective-permute-done.2.refs_0_.past
  54.2 0.1 pick.3
  54.3 0.2 collective-permute-start.6
  54.4 0.9 %collective-permute-start.7 = (bf16[6,128,256]{2,1,0:T(8,128)(2,1)S(1)}, bf16[6,128,256]{2,1,0:T(8,128)(2,1)S(1)}, u32[]{:S(2)}, u32[]{:S(2)}) collective-permute-start(bf16[6,128,256]{2,1,0:T(8,128)(2,1)S(1)} %get-tuple-element.31), channel_id=1, source_target_pairs={{1,2},{2,1},{3,4},{4,3},{5,6},{6,5},{9,10},{10,9},{11,12},{12,11},... | collective-permute-start | bytes 1179656 | tf_op jit(solution)/shard_map/ppermute | solution.py:373
  55.3 0.0 copy-start.3
  55.4 6.7 %shard_map.98 = (bf16[4,2,128,256]{3,2,1,0:T(8,128)(2,1)S(1)}, f32[2,512,256]{2,1,0:T(8,128)S(1)}) custom-call(bf16[2,4,128,256]{3,2,1,0:T(8,128)(2,1)S(1)} %collective-permute-done.2.refs_0_.past, bf16[2,4,128,256]{3,2,1,0:T(8,128)(2,1)S(1)} %get-tuple-element.28.refs_1_.head, bf16[2,4,128,256]{3,2,1,0:T(8,128)(2,1)S(1)} %get-tuple-element.24.refs_2_.last, ...), custom_call_target="tpu_custom_call" | custom-call | flops 3623878656 | bytes 8388608 | tf_op jit(solution)/shard_map/pallas_call | solution.py:416
  62.1 0.0 collective-permute-done.6.near
  62.1 0.0 collective-permute-done.7.far
  62.1 2.8 %shard_map.99 = (bf16[4,4,128,256]{3,2,1,0:T(8,128)(2,1)}, bf16[8,32,128]{2,1,0:T(8,128)(2,1)S(1)}) custom-call(bf16[6,128,256]{2,1,0:T(8,128)(2,1)S(1)} %collective-permute-done.6.near, bf16[6,128,256]{2,1,0:T(8,128)(2,1)S(1)} %collective-permute-done.7.far, f32[32,2,256]{2,1,0:T(2,128)S(1)} %all_to_all.16.refs_3_.stats, f32[1,256]{1,0:T(1,128)S(1)} %bitcast.11, ...), custom_call_target="tpu_custom_call" | custom-call | flops 3623878656 | bytes 8388608 | tf_op jit(solution)/shard_map/pallas_call | solution.py:416
  64.9 10.2 %all_to_all.17.received = bf16[8,32,128]{2,1,0:T(8,128)(2,1)S(1)} all-to-all(bf16[8,32,128]{2,1,0:T(8,128)(2,1)S(1)} %get-tuple-element.35), channel_id=1, replica_groups=mesh['tm'=4,'tile'=8] {'tile'}, dimensions={0} | all-to-all | bytes 131072 | tf_op jit(solution)/shard_map/all_to_all | solution.py:467
  75.1 0.8 unpack.1
  (11 shorter events, 0.1 us)
Async XLA Ops:
  0.6 22.1 %copy-start = (bf16[3,3,3,256,256]{4,3,2,1,0:T(8,128)(2,1)S(1)}, bf16[3,3,3,256,256]{4,3,2,1,0:T(8,128)(2,1)}, u32[]{:S(2)}) copy-start(bf16[3,3,3,256,256]{4,3,2,1,0:T(8,128)(2,1)} %refs_10_.1) | copy-start | bytes 10616836
  0.6 22.1 %copy-start.5 = (f32[256]{0:T(256)S(1)}, f32[256]{0:T(256)}, u32[]{:S(2)}) copy-start(f32[256]{0:T(256)} %param.10) | copy-start | bytes 3076
  0.7 22.1 %copy-start.4 = (f32[256]{0:T(256)S(1)}, f32[256]{0:T(256)}, u32[]{:S(2)}) copy-start(f32[256]{0:T(256)} %param.9) | copy-start | bytes 3076
  2.1 20.6 %collective-permute-start = (bf16[4,128,256]{2,1,0:T(8,128)(2,1)S(1)}, bf16[4,128,256]{2,1,0:T(8,128)(2,1)S(1)}, u32[]{:S(2)}, u32[]{:S(2)}) collective-permute-start(bf16[4,128,256]{2,1,0:T(8,128)(2,1)S(1)} %get-tuple-element.21), channel_id=1, source_target_pairs={{0,1},{1,0},{2,3},{3,2},{4,5},{5,4},{6,7},{7,6},{8,9},{9,8},{10,11... | collective-permute-start | bytes 786440 | tf_op jit(solution)/shard_map/ppermute | solution.py:372
  2.7 20.1 %collective-permute-start.1 = (bf16[4,128,256]{2,1,0:T(8,128)(2,1)S(1)}, bf16[4,128,256]{2,1,0:T(8,128)(2,1)S(1)}, u32[]{:S(2)}, u32[]{:S(2)}) collective-permute-start(bf16[4,128,256]{2,1,0:T(8,128)(2,1)S(1)} %get-tuple-element.22), channel_id=1, source_target_pairs={{1,2},{2,1},{3,4},{4,3},{5,6},{6,5},{9,10},{10,9},{11,12},{12,11},... | collective-permute-start | bytes 786440 | tf_op jit(solution)/shard_map/ppermute | solution.py:373
  3.4 27.0 %collective-permute-start.3 = (bf16[2,4,128,256]{3,2,1,0:T(8,128)(2,1)S(1)}, bf16[2,4,128,256]{3,2,1,0:T(8,128)(2,1)S(1)}, u32[]{:S(2)}, u32[]{:S(2)}) collective-permute-start(bf16[2,4,128,256]{3,2,1,0:T(8,128)(2,1)S(1)} %get-tuple-element.20.refs_1_.refs_4_), channel_id=1, source_target_pairs={{0,8},{8,16},{16,24},{1,9},{9,17},{17,25},{2,10},{10,18},{18,26},{... | collective-permute-start | bytes 1572872 | tf_op jit(solution)/shard_map/ppermute | solution.py:365
  27.0 27.2 %collective-permute-start.2 = (bf16[2,4,128,256]{3,2,1,0:T(8,128)(2,1)S(1)}, bf16[2,4,128,256]{3,2,1,0:T(8,128)(2,1)S(1)}, u32[]{:S(2)}, u32[]{:S(2)}) collective-permute-start(bf16[2,4,128,256]{3,2,1,0:T(8,128)(2,1)S(1)} %get-tuple-element.24.refs_2_.last), channel_id=1, source_target_pairs={{0,8},{8,16},{16,24},{1,9},{9,17},{17,25},{2,10},{10,18},{18,26},{... | collective-permute-start | bytes 1572872 | tf_op jit(solution)/shard_map/ppermute | solution.py:365
  30.4 1.4 %collective-permute-start.4 = (bf16[2,128,256]{2,1,0:T(8,128)(2,1)S(1)}, bf16[2,128,256]{2,1,0:T(8,128)(2,1)S(1)}, u32[]{:S(2)}, u32[]{:S(2)}) collective-permute-start(bf16[2,128,256]{2,1,0:T(8,128)(2,1)S(1)} %get-tuple-element.25), channel_id=1, source_target_pairs={{0,1},{1,0},{2,3},{3,2},{4,5},{5,4},{6,7},{7,6},{8,9},{9,8},{10,11... | collective-permute-start | bytes 393224 | tf_op jit(solution)/shard_map/ppermute | solution.py:372
  30.5 1.3 %collective-permute-start.5 = (bf16[2,128,256]{2,1,0:T(8,128)(2,1)S(1)}, bf16[2,128,256]{2,1,0:T(8,128)(2,1)S(1)}, u32[]{:S(2)}, u32[]{:S(2)}) collective-permute-start(bf16[2,128,256]{2,1,0:T(8,128)(2,1)S(1)} %get-tuple-element.26), channel_id=1, source_target_pairs={{1,2},{2,1},{3,4},{4,3},{5,6},{6,5},{9,10},{10,9},{11,12},{12,11},... | collective-permute-start | bytes 393224 | tf_op jit(solution)/shard_map/ppermute | solution.py:373
  31.8 23.5 %copy-start.1 = (bf16[3,3,3,256,256]{4,3,2,1,0:T(8,128)(2,1)S(1)}, bf16[3,3,3,256,256]{4,3,2,1,0:T(8,128)(2,1)}, u32[]{:S(2)}) copy-start(bf16[3,3,3,256,256]{4,3,2,1,0:T(8,128)(2,1)} %weight.3) | copy-start | bytes 10616836
  31.8 23.5 %copy-start.2 = (bf16[4,4,128,256]{3,2,1,0:T(8,128)(2,1)S(1)}, bf16[4,4,128,256]{3,2,1,0:T(8,128)(2,1)}, u32[]{:S(2)}) copy-start(bf16[4,4,128,256]{3,2,1,0:T(8,128)(2,1)} %frames.3) | copy-start | bytes 3145732
  31.8 23.5 %copy-start.6 = (f32[256]{0:T(256)S(1)}, f32[256]{0:T(256)}, u32[]{:S(2)}) copy-start(f32[256]{0:T(256)} %param.12) | copy-start | bytes 3076
  31.9 23.5 %copy-start.7 = (f32[256]{0:T(256)S(1)}, f32[256]{0:T(256)}, u32[]{:S(2)}) copy-start(f32[256]{0:T(256)} %param.13) | copy-start | bytes 3076
  54.3 7.8 %collective-permute-start.6 = (bf16[6,128,256]{2,1,0:T(8,128)(2,1)S(1)}, bf16[6,128,256]{2,1,0:T(8,128)(2,1)S(1)}, u32[]{:S(2)}, u32[]{:S(2)}) collective-permute-start(bf16[6,128,256]{2,1,0:T(8,128)(2,1)S(1)} %get-tuple-element.30), channel_id=1, source_target_pairs={{0,1},{1,0},{2,3},{3,2},{4,5},{5,4},{6,7},{7,6},{8,9},{9,8},{10,11... | collective-permute-start | bytes 1179656 | tf_op jit(solution)/shard_map/ppermute | solution.py:372
  54.4 7.6 %collective-permute-start.7 = (bf16[6,128,256]{2,1,0:T(8,128)(2,1)S(1)}, bf16[6,128,256]{2,1,0:T(8,128)(2,1)S(1)}, u32[]{:S(2)}, u32[]{:S(2)}) collective-permute-start(bf16[6,128,256]{2,1,0:T(8,128)(2,1)S(1)} %get-tuple-element.31), channel_id=1, source_target_pairs={{1,2},{2,1},{3,4},{4,3},{5,6},{6,5},{9,10},{10,9},{11,12},{12,11},... | collective-permute-start | bytes 1179656 | tf_op jit(solution)/shard_map/ppermute | solution.py:373
  55.3 6.7 %copy-start.3 = (bf16[256,16]{0,1:T(8,128)(2,1)S(1)}, bf16[256,16]{0,1:T(8,128)(2,1)}, u32[]{:S(2)}) copy-start(bf16[256,16]{0,1:T(8,128)(2,1)} %param.15) | copy-start | bytes 24580
